TPU v7x, 8 devices: a whole 2x2x1 slice. The times are simulated.
8 devices in a mesh: dp: 1 (over z), pz: 2 (over y), py: 2 (over x), px: 2 (over core).
Axes of the slice: x: 2, y: 2, z: 1, core: 2. Of those that a mesh axis runs over, the one named last changes fastest.
Arguments:
- volumes: bfloat16 [2, 32, 128, 128, 128], P('dp', None, 'px', 'py', 'pz')
- filter_taps: float32 [3, 3, 15], replicated
- mix_weight: bfloat16 [3, 32, 32], replicated
- mix_bias: float32 [3, 32], replicated
Outputs:
- output: bfloat16 [2, 32, 128, 128, 128], P('dp', None, 'px', 'py', 'pz')
All inputs are finite; a program needn't handle non-finite values.
Results may differ from a plain program's by a relative error of at most 0.00422.
Values are sent between devices in bfloat16 or wider.
A program may use at most 1 GiB of HBM per device.

v0:
```python
import jax
import jax.numpy as jnp
from jax import lax
from jax.sharding import PartitionSpec as P

PASS_FORMS = ('vcsyz,si->vciyz', 'vcxsz,si->vcxiz', 'vcxys,si->vcxyi')
GRID_AXES = ((2, 'px'), (3, 'py'), (4, 'pz'))


def band_matrix(tap_row, out_len):
    tap_count = tap_row.shape[0]
    tap_index = jnp.arange(out_len + tap_count - 1)[:, None] - jnp.arange(out_len)[None, :]
    inside = (tap_index >= 0) & (tap_index < tap_count)
    picked = tap_row[jnp.clip(tap_index, 0, tap_count - 1)]
    return jnp.where(inside, picked, 0.0).astype(jnp.bfloat16)


def neighbour_planes(block, plane_count, axis_dim, axis_name, axis_size):
    if axis_size == 1:
        zero_shape = block.shape[:axis_dim] + (plane_count,) + block.shape[axis_dim + 1:]
        zero_planes = jnp.zeros(zero_shape, block.dtype)
        return zero_planes, zero_planes
    extent = block.shape[axis_dim]
    low_planes = lax.slice_in_dim(block, 0, plane_count, axis=axis_dim)
    high_planes = lax.slice_in_dim(block, extent - plane_count, extent, axis=axis_dim)
    upward = [(source, source + 1) for source in range(axis_size - 1)]
    downward = [(source + 1, source) for source in range(axis_size - 1)]
    from_lower = lax.ppermute(high_planes, axis_name, upward)
    from_upper = lax.ppermute(low_planes, axis_name, downward)
    return from_lower, from_upper


def solution(mesh):
    axis_sizes = {'px': mesh.shape['px'], 'py': mesh.shape['py'], 'pz': mesh.shape['pz']}
    vol_spec = P('dp', None, 'px', 'py', 'pz')

    def local_layers(vol_block, filter_taps, mix_weight, mix_bias):
        half_width = (filter_taps.shape[2] - 1) // 2
        vol_state = vol_block
        for layer_idx in range(filter_taps.shape[0]):
            current = vol_state
            for pass_idx in range(3):
                axis_dim, axis_name = GRID_AXES[pass_idx]
                from_lower, from_upper = neighbour_planes(current, half_width, axis_dim, axis_name, axis_sizes[axis_name])
                padded = jnp.concatenate([from_lower, current, from_upper], axis=axis_dim)
                matrix = band_matrix(filter_taps[layer_idx, pass_idx], current.shape[axis_dim])
                current = jnp.einsum(PASS_FORMS[pass_idx], padded, matrix, preferred_element_type=jnp.float32).astype(jnp.bfloat16)
            mix_out = jnp.einsum('cd,vcxyz->vdxyz', mix_weight[layer_idx], current, preferred_element_type=jnp.float32)
            activated = jax.nn.gelu(mix_out + mix_bias[layer_idx][None, :, None, None, None], approximate=True)
            vol_state = (vol_state.astype(jnp.float32) + activated).astype(jnp.bfloat16)
        return vol_state

    return jax.shard_map(local_layers, mesh=mesh, in_specs=(vol_spec, P(), P(), P()), out_specs=vol_spec, check_vma=False)
```

profile of v0, /device:TPU:0, one launch (start us, length us, event | category | flops | bytes accessed | tf_op | source)
XLA Modules:
  0.0 3144.2 jit_solution(14779917226828344770)
XLA Ops:
  0.0 11.7 fusion.782
  11.7 5.8 collective-permute-start
  18.9 93.0 %copy.20 = bf16[2,32,64,64,64]{2,4,3,1,0:T(8,128)(2,1)} copy(bf16[2,32,64,64,64]{4,3,2,1,0:T(8,128)(2,1)} %param.4) | data formatting | bytes 67108864 | tf_op args[0]
  113.3 51.5 %copy.19 = bf16[2,32,7,64,64]{2,4,3,1,0:T(8,128)(2,1)} copy(bf16[2,32,7,64,64]{4,3,2,1,0:T(8,128)(2,1)} %collective-permute-done) | data formatting | bytes 7340032 | tf_op jit(solution)/shard_map/ppermute | solution.py:28
  164.8 51.0 %copy.21 = bf16[2,32,7,64,64]{2,4,3,1,0:T(8,128)(2,1)} copy(bf16[2,32,7,64,64]{4,3,2,1,0:T(8,128)(2,1)} %collective-permute-done.1) | data formatting | bytes 7340032 | tf_op jit(solution)/shard_map/ppermute | solution.py:29
  215.8 108.1 %convert_bitcast_fusion.5 = bf16[2,32,64,64,64]{4,2,3,1,0:T(8,128)(2,1)} fusion(bf16[2,32,7,64,64]{2,4,3,1,0:T(8,128)(2,1)} %copy.21, bf16[2,32,64,64,64]{2,4,3,1,0:T(8,128)(2,1)} %copy.20, bf16[2,32,7,64,64]{2,4,3,1,0:T(8,128)(2,1)} %copy.19, bf16[]{:T(256)} %bitcast.34, bf16[]{:T(256)} %bitcast.35, bf16[]{:T(256)} %bitcast.36, bf16[]{:T(256)} %bitcast.37, ...), kind=kOutput, calls=%fused_computation.65 | convolution fusion | flops 2756896000 | bytes 74448928 | tf_op jit(solution)/shard_map/vcsyz,si->vciyz/dot_general | solution.py:47
  323.9 7.4 fusion.781
  331.3 4.8 collective-permute-start.2
  338.3 152.5 %collective-permute-done.2 = bf16[2,32,64,7,64]{4,2,3,1,0:T(8,128)(2,1)S(1)} collective-permute-done((bf16[2,32,64,7,64]{4,2,3,1,0:T(8,128)(2,1)S(1)}, bf16[2,32,64,7,64]{4,2,3,1,0:T(8,128)(2,1)S(1)}, u32[]{:S(2)}, u32[]{:S(2)}) %collective-permute-start.2) | collective-permute-done | bytes 3670048 | tf_op jit(solution)/shard_map/ppermute | solution.py:28
  490.9 3.0 copy-done.2
  496.0 54.9 %pad_maximum_fusion.3 = bf16[2,32,64,78,64]{4,2,3,1,0:T(8,128)(2,1)} fusion(bf16[2,32,64,7,64]{4,2,3,1,0:T(8,128)(2,1)} %collective-permute-done.3, bf16[2,32,64,64,64]{4,2,3,1,0:T(8,128)(2,1)} %convert_bitcast_fusion.5, bf16[2,32,64,7,64]{4,2,3,1,0:T(8,128)(2,1)} %copy-done.2), kind=kLoop, calls=%fused_computation.43 | loop fusion | flops 40894464 | bytes 81788928 | tf_op jit(solution)/shard_map/concatenate | solution.py:45
  550.9 88.6 %convert_bitcast_fusion.4 = bf16[2,32,64,64,64]{3,4,2,1,0:T(8,128)(2,1)} fusion(bf16[2,32,64,78,64]{4,2,3,1,0:T(8,128)(2,1)} %pad_maximum_fusion.3, bf16[]{:T(256)} %bitcast.16, bf16[]{:T(256)} %bitcast.17, bf16[]{:T(256)} %bitcast.18, bf16[]{:T(256)} %bitcast.19, bf16[]{:T(256)} %bitcast.20, bf16[]{:T(256)} %bitcast.22, bf16[]{:T(256)} %bitcast.21, ...), kind=kOutput, calls=%fused_computation.64 | convolution fusion | flops 2634212608 | bytes 74448928 | tf_op jit(solution)/shard_map/vcxsz,si->vcxiz/dot_general | solution.py:47
  639.5 9.9 fusion.780
  649.4 8.7 copy.23
  658.1 6.2 collective-permute-start.4
  664.2 5.3 copy.24
  671.7 146.1 %collective-permute-done.4 = bf16[2,32,64,64,7]{3,2,4,1,0:T(8,128)(2,1)} collective-permute-done((bf16[2,32,64,64,7]{3,2,4,1,0:T(8,128)(2,1)}, bf16[2,32,64,64,7]{3,2,4,1,0:T(8,128)(2,1)}, u32[]{:S(2)}, u32[]{:S(2)}) %collective-permute-start.4) | collective-permute-done | bytes 3670048 | tf_op jit(solution)/shard_map/ppermute | solution.py:28
  817.8 21.2 copy.25
  839.0 18.4 copy.26
  857.4 54.6 %pad_maximum_fusion = bf16[2,32,64,64,78]{3,4,2,1,0:T(8,128)(2,1)} fusion(bf16[2,32,64,64,7]{3,4,2,1,0:T(8,128)(2,1)} %copy.26, bf16[2,32,64,64,64]{3,4,2,1,0:T(8,128)(2,1)} %convert_bitcast_fusion.4, bf16[2,32,64,64,7]{3,4,2,1,0:T(8,128)(2,1)} %copy.25), kind=kLoop, calls=%fused_computation.30 | loop fusion | flops 122683392 | bytes 81788928 | tf_op jit(solution)/shard_map/concatenate | solution.py:45
  912.0 96.9 %copy.45 = bf16[2,32,64,64,78]{4,1,3,2,0:T(8,128)(2,1)} copy(bf16[2,32,64,64,78]{3,4,2,1,0:T(8,128)(2,1)} %pad_maximum_fusion) | data formatting | bytes 81788928 | tf_op jit(solution)/shard_map/concatenate | solution.py:45
  1008.9 56.8 %fusion.844 = bf16[2,32,64,64,64]{4,1,3,2,0:T(8,128)(2,1)} fusion(bf16[2,32,64,64,78]{4,1,3,2,0:T(8,128)(2,1)} %copy.45, bf16[]{:T(256)} %bitcast.54, bf16[]{:T(256)} %bitcast.55, bf16[]{:T(256)} %bitcast.56, bf16[]{:T(256)} %bitcast.57, bf16[]{:T(256)} %bitcast.58, bf16[]{:T(256)} %bitcast.60, bf16[]{:T(256)} %bitcast.59, ...), kind=kOutput, calls=%fused_computation.63.clone.clone.clone.2 | convolution fusion | flops 2634212608 | bytes 74448928 | tf_op jit(solution)/shard_map/vcxys,si->vcxyi/dot_general | solution.py:47
  1065.7 100.2 %fusion.8 = bf16[2,32,64,64,64]{4,1,3,2,0:T(8,128)(2,1)} fusion(bf16[2,32,64,64,64]{4,3,2,1,0:T(8,128)(2,1)} %param.4, f32[32]{0:T(128)S(1)} %get-tuple-element.159, bf16[3,32,32]{2,1,0:T(8,128)(2,1)} %param.6, bf16[2,32,64,64,64]{4,1,3,2,0:T(8,128)(2,1)} %fusion.844), kind=kOutput, calls=%fused_computation.11 | convolution fusion | flops 1275068416 | bytes 167780480 | tf_op jit(solution)/shard_map/cd,vcxyz->vdxyz/dot_general | solution.py:48
  1165.9 7.0 fusion.779
  1172.9 4.3 collective-permute-start.6
  1180.0 8.0 collective-permute-done.6
  1188.0 3.0 copy-done
  1191.0 55.1 %pad_maximum_fusion.4 = bf16[2,32,78,64,64]{4,1,3,2,0:T(8,128)(2,1)} fusion(bf16[2,32,7,64,64]{4,1,3,2,0:T(8,128)(2,1)} %collective-permute-done.7, bf16[2,32,64,64,64]{4,1,3,2,0:T(8,128)(2,1)} %fusion.8, bf16[2,32,7,64,64]{4,1,3,2,0:T(8,128)(2,1)} %copy-done), kind=kLoop, calls=%fused_computation.44 | loop fusion | flops 40894464 | bytes 81788928 | tf_op jit(solution)/shard_map/concatenate | solution.py:45
  1246.2 111.7 %convert_bitcast_fusion.3 = bf16[2,32,64,64,64]{4,2,3,1,0:T(8,128)(2,1)} fusion(bf16[2,32,78,64,64]{4,1,3,2,0:T(8,128)(2,1)} %pad_maximum_fusion.4, bf16[]{:T(256)} %bitcast.95, bf16[]{:T(256)} %bitcast.96, bf16[]{:T(256)} %bitcast.97, bf16[]{:T(256)} %bitcast.98, bf16[]{:T(256)} %bitcast.99, bf16[]{:T(256)} %bitcast.101, bf16[]{:T(256)} %bitcast.100, ...), kind=kOutput, calls=%fused_computation.61 | convolution fusion | flops 2634212608 | bytes 74448928 | tf_op jit(solution)/shard_map/vcsyz,si->vciyz/dot_general | solution.py:47
  1357.9 7.4 fusion.778
  1369.3 156.0 %collective-permute-done.8 = bf16[2,32,64,7,64]{4,2,3,1,0:T(8,128)(2,1)S(1)} collective-permute-done((bf16[2,32,64,7,64]{4,2,3,1,0:T(8,128)(2,1)S(1)}, bf16[2,32,64,7,64]{4,2,3,1,0:T(8,128)(2,1)S(1)}, u32[]{:S(2)}, u32[]{:S(2)}) %collective-permute-start.8) | collective-permute-done | bytes 3670048 | tf_op jit(solution)/shard_map/ppermute | solution.py:28
  1529.9 55.1 %pad_maximum_fusion.5 = bf16[2,32,64,78,64]{4,2,3,1,0:T(8,128)(2,1)} fusion(bf16[2,32,64,7,64]{4,2,3,1,0:T(8,128)(2,1)} %collective-permute-done.9, bf16[2,32,64,64,64]{4,2,3,1,0:T(8,128)(2,1)} %convert_bitcast_fusion.3, bf16[2,32,64,7,64]{4,2,3,1,0:T(8,128)(2,1)} %copy-done.3), kind=kLoop, calls=%fused_computation.45 | loop fusion | flops 40894464 | bytes 81788928 | tf_op jit(solution)/shard_map/concatenate | solution.py:45
  1585.0 88.4 %convert_bitcast_fusion.2 = bf16[2,32,64,64,64]{3,4,2,1,0:T(8,128)(2,1)} fusion(bf16[2,32,64,78,64]{4,2,3,1,0:T(8,128)(2,1)} %pad_maximum_fusion.5, bf16[]{:T(256)} %bitcast.77, bf16[]{:T(256)} %bitcast.78, bf16[]{:T(256)} %bitcast.79, bf16[]{:T(256)} %bitcast.80, bf16[]{:T(256)} %bitcast.81, bf16[]{:T(256)} %bitcast.83, bf16[]{:T(256)} %bitcast.82, ...), kind=kOutput, calls=%fused_computation.60 | convolution fusion | flops 2634212608 | bytes 74448928 | tf_op jit(solution)/shard_map/vcxsz,si->vcxiz/dot_general | solution.py:47
  1673.4 9.9 fusion.777
  1683.2 8.7 copy.30
  1691.9 7.1 collective-permute-start.10
  1699.0 5.3 copy.31
  1706.6 146.0 %collective-permute-done.10 = bf16[2,32,64,64,7]{3,2,4,1,0:T(8,128)(2,1)} collective-permute-done((bf16[2,32,64,64,7]{3,2,4,1,0:T(8,128)(2,1)}, bf16[2,32,64,64,7]{3,2,4,1,0:T(8,128)(2,1)}, u32[]{:S(2)}, u32[]{:S(2)}) %collective-permute-start.10) | collective-permute-done | bytes 3670048 | tf_op jit(solution)/shard_map/ppermute | solution.py:28
  1852.7 21.2 copy.32
  1873.9 18.3 copy.33
  1892.2 54.6 %pad_maximum_fusion.1 = bf16[2,32,64,64,78]{3,4,2,1,0:T(8,128)(2,1)} fusion(bf16[2,32,64,64,7]{3,4,2,1,0:T(8,128)(2,1)} %copy.33, bf16[2,32,64,64,64]{3,4,2,1,0:T(8,128)(2,1)} %convert_bitcast_fusion.2, bf16[2,32,64,64,7]{3,4,2,1,0:T(8,128)(2,1)} %copy.32), kind=kLoop, calls=%fused_computation.31 | loop fusion | flops 122683392 | bytes 81788928 | tf_op jit(solution)/shard_map/concatenate | solution.py:45
  1946.8 97.7 %copy.50 = bf16[2,32,64,64,78]{4,1,3,2,0:T(8,128)(2,1)} copy(bf16[2,32,64,64,78]{3,4,2,1,0:T(8,128)(2,1)} %pad_maximum_fusion.1) | data formatting | bytes 81788928 | tf_op jit(solution)/shard_map/concatenate | solution.py:45
  2044.5 88.5 %fusion.17 = bf16[2,32,64,64,64]{4,1,3,2,0:T(8,128)(2,1)} fusion(bf16[2,32,64,64,64]{4,1,3,2,0:T(8,128)(2,1)} %fusion.8, f32[32]{0:T(128)S(1)} %copy-done.11, bf16[2,32,64,64,78]{4,1,3,2,0:T(8,128)(2,1)} %copy.50, bf16[]{:T(256)} %bitcast.115, bf16[]{:T(256)} %bitcast.116, bf16[]{:T(256)} %bitcast.117, bf16[]{:T(256)} %bitcast.118, bf16[]{:T(256)} %bitcast.119, ...), kind=kOutput, calls=%fused_computation.20 | convolution fusion | flops 3909281024 | bytes 167788160 | tf_op jit(solution)/shard_map/cd,vcxyz->vdxyz/dot_general | solution.py:48
  2133.0 7.0 fusion.776
  2144.5 8.1 collective-permute-done.12
  2152.5 3.0 copy-done.1
  2155.5 55.1 %pad_maximum_fusion.6 = bf16[2,32,78,64,64]{4,1,3,2,0:T(8,128)(2,1)} fusion(bf16[2,32,7,64,64]{4,1,3,2,0:T(8,128)(2,1)} %collective-permute-done.13, bf16[2,32,64,64,64]{4,1,3,2,0:T(8,128)(2,1)} %fusion.17, bf16[2,32,7,64,64]{4,1,3,2,0:T(8,128)(2,1)} %copy-done.1), kind=kLoop, calls=%fused_computation.46 | loop fusion | flops 40894464 | bytes 81788928 | tf_op jit(solution)/shard_map/concatenate | solution.py:45
  2210.7 111.6 %convert_bitcast_fusion.1 = bf16[2,32,64,64,64]{4,2,3,1,0:T(8,128)(2,1)} fusion(bf16[2,32,78,64,64]{4,1,3,2,0:T(8,128)(2,1)} %pad_maximum_fusion.6, bf16[]{:T(256)} %bitcast.156, bf16[]{:T(256)} %bitcast.157, bf16[]{:T(256)} %bitcast.158, bf16[]{:T(256)} %bitcast.159, bf16[]{:T(256)} %bitcast.160, bf16[]{:T(256)} %bitcast.162, bf16[]{:T(256)} %bitcast.161, ...), kind=kOutput, calls=%fused_computation.57 | convolution fusion | flops 2634212608 | bytes 74448928 | tf_op jit(solution)/shard_map/vcsyz,si->vciyz/dot_general | solution.py:47
  2322.3 7.4 fusion.775
  2329.7 3.4 collective-permute-start.14
  2334.4 156.0 %collective-permute-done.14 = bf16[2,32,64,7,64]{4,2,3,1,0:T(8,128)(2,1)S(1)} collective-permute-done((bf16[2,32,64,7,64]{4,2,3,1,0:T(8,128)(2,1)S(1)}, bf16[2,32,64,7,64]{4,2,3,1,0:T(8,128)(2,1)S(1)}, u32[]{:S(2)}, u32[]{:S(2)}) %collective-permute-start.14) | collective-permute-done | bytes 3670048 | tf_op jit(solution)/shard_map/ppermute | solution.py:28
  2495.0 55.1 %pad_maximum_fusion.7 = bf16[2,32,64,78,64]{4,2,3,1,0:T(8,128)(2,1)} fusion(bf16[2,32,64,7,64]{4,2,3,1,0:T(8,128)(2,1)} %collective-permute-done.15, bf16[2,32,64,64,64]{4,2,3,1,0:T(8,128)(2,1)} %convert_bitcast_fusion.1, bf16[2,32,64,7,64]{4,2,3,1,0:T(8,128)(2,1)} %copy-done.4), kind=kLoop, calls=%fused_computation.47 | loop fusion | flops 40894464 | bytes 81788928 | tf_op jit(solution)/shard_map/concatenate | solution.py:45
  2550.1 88.4 %convert_bitcast_fusion = bf16[2,32,64,64,64]{3,4,2,1,0:T(8,128)(2,1)} fusion(bf16[2,32,64,78,64]{4,2,3,1,0:T(8,128)(2,1)} %pad_maximum_fusion.7, bf16[]{:T(256)} %bitcast.138, bf16[]{:T(256)} %bitcast.139, bf16[]{:T(256)} %bitcast.140, bf16[]{:T(256)} %bitcast.141, bf16[]{:T(256)} %bitcast.142, bf16[]{:T(256)} %bitcast.144, bf16[]{:T(256)} %bitcast.143, ...), kind=kOutput, calls=%fused_computation.56 | convolution fusion | flops 2634212608 | bytes 74448928 | tf_op jit(solution)/shard_map/vcxsz,si->vcxiz/dot_general | solution.py:47
  2638.4 9.9 fusion.774
  2648.3 8.7 copy.37
  2657.0 7.4 collective-permute-start.16
  2664.4 5.3 copy.38
  2671.3 146.8 %collective-permute-done.16 = bf16[2,32,64,64,7]{3,2,4,1,0:T(8,128)(2,1)} collective-permute-done((bf16[2,32,64,64,7]{3,2,4,1,0:T(8,128)(2,1)}, bf16[2,32,64,64,7]{3,2,4,1,0:T(8,128)(2,1)}, u32[]{:S(2)}, u32[]{:S(2)}) %collective-permute-start.16) | collective-permute-done | bytes 3670048 | tf_op jit(solution)/shard_map/ppermute | solution.py:28
  2818.1 21.2 copy.39
  2839.3 18.1 copy.40
  2857.4 54.9 %pad_maximum_fusion.2 = bf16[2,32,64,64,78]{3,4,2,1,0:T(8,128)(2,1)} fusion(bf16[2,32,64,64,7]{3,4,2,1,0:T(8,128)(2,1)} %copy.40, bf16[2,32,64,64,64]{3,4,2,1,0:T(8,128)(2,1)} %convert_bitcast_fusion, bf16[2,32,64,64,7]{3,4,2,1,0:T(8,128)(2,1)} %copy.39), kind=kLoop, calls=%fused_computation.32 | loop fusion | flops 122683392 | bytes 81788928 | tf_op jit(solution)/shard_map/concatenate | solution.py:45
  2912.2 97.7 %copy.55 = bf16[2,32,64,64,78]{4,1,3,2,0:T(8,128)(2,1)} copy(bf16[2,32,64,64,78]{3,4,2,1,0:T(8,128)(2,1)} %pad_maximum_fusion.2) | data formatting | bytes 81788928 | tf_op jit(solution)/shard_map/concatenate | solution.py:45
  3009.9 88.5 %fusion.26 = bf16[2,32,64,64,64]{4,1,3,2,0:T(8,128)(2,1)} fusion(bf16[2,32,64,64,64]{4,1,3,2,0:T(8,128)(2,1)} %fusion.17, f32[32]{0:T(128)S(1)} %copy-done.10, bf16[2,32,64,64,78]{4,1,3,2,0:T(8,128)(2,1)} %copy.55, bf16[]{:T(256)} %bitcast.176, bf16[]{:T(256)} %bitcast.177, bf16[]{:T(256)} %bitcast.178, bf16[]{:T(256)} %bitcast.179, bf16[]{:T(256)} %bitcast.180, ...), kind=kOutput, calls=%fused_computation.29 | convolution fusion | flops 3909281024 | bytes 167788160 | tf_op jit(solution)/shard_map/cd,vcxyz->vdxyz/dot_general | solution.py:48
  3098.5 45.2 %copy.42 = bf16[2,32,64,64,64]{4,3,2,1,0:T(8,128)(2,1)} copy(bf16[2,32,64,64,64]{4,1,3,2,0:T(8,128)(2,1)} %fusion.26) | data formatting | bytes 67108864 | tf_op jit(solution)/shard_map/convert_element_type | solution.py:50
  (51 shorter events, 35.4 us)
Async XLA Ops:
  11.7 101.6 %collective-permute-start = (bf16[2,32,7,64,64]{4,3,2,1,0:T(8,128)(2,1)}, bf16[2,32,7,64,64]{4,3,2,1,0:T(8,128)(2,1)}, u32[]{:S(2)}, u32[]{:S(2)}) collective-permute-start(bf16[2,32,7,64,64]{4,3,2,1,0:T(8,128)(2,1)} %get-tuple-element.21), channel_id=1, source_target_pairs={{0,1},{2,3},{4,5},{6,7}} | collective-permute-start | bytes 11010056 | tf_op jit(solution)/shard_map/ppermute | solution.py:28
  17.5 94.4 %copy-start.5 = (f32[3,3,15]{2,1,0:T(4,128)S(1)}, f32[3,3,15]{2,1,0:T(4,128)}, u32[]{:S(2)}) copy-start(f32[3,3,15]{2,1,0:T(4,128)} %param.5) | copy-start | bytes 1624
  17.5 147.3 %collective-permute-start.1 = (bf16[2,32,7,64,64]{4,3,2,1,0:T(8,128)(2,1)}, bf16[2,32,7,64,64]{4,3,2,1,0:T(8,128)(2,1)}, u32[]{:S(2)}, u32[]{:S(2)}) collective-permute-start(bf16[2,32,7,64,64]{4,3,2,1,0:T(8,128)(2,1)} %get-tuple-element.22), channel_id=1, source_target_pairs={{1,0},{3,2},{5,4},{7,6}} | collective-permute-start | bytes 11010056 | tf_op jit(solution)/shard_map/ppermute | solution.py:29
  331.3 159.6 %collective-permute-start.2 = (bf16[2,32,64,7,64]{4,2,3,1,0:T(8,128)(2,1)S(1)}, bf16[2,32,64,7,64]{4,2,3,1,0:T(8,128)(2,1)S(1)}, u32[]{:S(2)}, u32[]{:S(2)}) collective-permute-start(bf16[2,32,64,7,64]{4,2,3,1,0:T(8,128)(2,1)S(1)} %get-tuple-element.19), channel_id=1, source_target_pairs={{0,2},{1,3},{4,6},{5,7}} | collective-permute-start | bytes 11010056 | tf_op jit(solution)/shard_map/ppermute | solution.py:28
  336.1 159.9 %collective-permute-start.3 = (bf16[2,32,64,7,64]{4,2,3,1,0:T(8,128)(2,1)S(1)}, bf16[2,32,64,7,64]{4,2,3,1,0:T(8,128)(2,1)}, u32[]{:S(2)}, u32[]{:S(2)}) collective-permute-start(bf16[2,32,64,7,64]{4,2,3,1,0:T(8,128)(2,1)S(1)} %get-tuple-element.20), channel_id=1, source_target_pairs={{2,0},{3,1},{6,4},{7,5}} | collective-permute-start | bytes 11010056 | tf_op jit(solution)/shard_map/ppermute | solution.py:29
  490.9 3.0 copy-start.2
  550.9 120.3 %copy-start.9 = (f32[3,32]{1,0:T(4,128)S(1)}, f32[3,32]{1,0:T(4,128)}, u32[]{:S(2)}) copy-start(f32[3,32]{1,0:T(4,128)} %param.7) | copy-start | bytes 1156
  658.1 159.7 %collective-permute-start.4 = (bf16[2,32,64,64,7]{3,2,4,1,0:T(8,128)(2,1)}, bf16[2,32,64,64,7]{3,2,4,1,0:T(8,128)(2,1)}, u32[]{:S(2)}, u32[]{:S(2)}) collective-permute-start(bf16[2,32,64,64,7]{3,2,4,1,0:T(8,128)(2,1)} %copy.23), channel_id=1, source_target_pairs={{0,4},{1,5},{2,6},{3,7}} | collective-permute-start | bytes 11010056 | tf_op jit(solution)/shard_map/ppermute | solution.py:28
  669.5 169.5 %collective-permute-start.5 = (bf16[2,32,64,64,7]{3,2,4,1,0:T(8,128)(2,1)}, bf16[2,32,64,64,7]{3,2,4,1,0:T(8,128)(2,1)S(1)}, u32[]{:S(2)}, u32[]{:S(2)}) collective-permute-start(bf16[2,32,64,64,7]{3,2,4,1,0:T(8,128)(2,1)} %copy.24), channel_id=1, source_target_pairs={{4,0},{5,1},{6,2},{7,3}} | collective-permute-start | bytes 11010056 | tf_op jit(solution)/shard_map/ppermute | solution.py:29
  1065.7 112.8 %copy-start.6 = (f32[3,3,15]{2,1,0:T(4,128)S(1)}, f32[3,3,15]{2,1,0:T(4,128)}, u32[]{:S(2)}) copy-start(f32[3,3,15]{2,1,0:T(4,128)} %param.5) | copy-start | bytes 1624
  1172.9 15.1 collective-permute-start.6
  1177.2 13.8 collective-permute-start.7
  1188.0 3.0 copy-start
  1365.3 160.0 %collective-permute-start.8 = (bf16[2,32,64,7,64]{4,2,3,1,0:T(8,128)(2,1)S(1)}, bf16[2,32,64,7,64]{4,2,3,1,0:T(8,128)(2,1)S(1)}, u32[]{:S(2)}, u32[]{:S(2)}) collective-permute-start(bf16[2,32,64,7,64]{4,2,3,1,0:T(8,128)(2,1)S(1)} %get-tuple-element.13), channel_id=1, source_target_pairs={{0,2},{1,3},{4,6},{5,7}} | collective-permute-start | bytes 11010056 | tf_op jit(solution)/shard_map/ppermute | solution.py:28
  1368.0 161.9 %collective-permute-start.9 = (bf16[2,32,64,7,64]{4,2,3,1,0:T(8,128)(2,1)S(1)}, bf16[2,32,64,7,64]{4,2,3,1,0:T(8,128)(2,1)}, u32[]{:S(2)}, u32[]{:S(2)}) collective-permute-start(bf16[2,32,64,7,64]{4,2,3,1,0:T(8,128)(2,1)S(1)} %get-tuple-element.14), channel_id=1, source_target_pairs={{2,0},{3,1},{6,4},{7,5}} | collective-permute-start | bytes 11010056 | tf_op jit(solution)/shard_map/ppermute | solution.py:29
  1525.3 3.0 copy-start.3
  1585.0 120.9 %copy-start.7 = (f32[3,3,15]{2,1,0:T(4,128)S(1)}, f32[3,3,15]{2,1,0:T(4,128)}, u32[]{:S(2)}) copy-start(f32[3,3,15]{2,1,0:T(4,128)} %param.5) | copy-start | bytes 1624
  1691.9 160.8 %collective-permute-start.10 = (bf16[2,32,64,64,7]{3,2,4,1,0:T(8,128)(2,1)}, bf16[2,32,64,64,7]{3,2,4,1,0:T(8,128)(2,1)}, u32[]{:S(2)}, u32[]{:S(2)}) collective-permute-start(bf16[2,32,64,64,7]{3,2,4,1,0:T(8,128)(2,1)} %copy.30), channel_id=1, source_target_pairs={{0,4},{1,5},{2,6},{3,7}} | collective-permute-start | bytes 11010056 | tf_op jit(solution)/shard_map/ppermute | solution.py:28
  1704.2 169.6 %collective-permute-start.11 = (bf16[2,32,64,64,7]{3,2,4,1,0:T(8,128)(2,1)}, bf16[2,32,64,64,7]{3,2,4,1,0:T(8,128)(2,1)S(1)}, u32[]{:S(2)}, u32[]{:S(2)}) collective-permute-start(bf16[2,32,64,64,7]{3,2,4,1,0:T(8,128)(2,1)} %copy.31), channel_id=1, source_target_pairs={{4,0},{5,1},{6,2},{7,3}} | collective-permute-start | bytes 11010056 | tf_op jit(solution)/shard_map/ppermute | solution.py:29
  1946.8 97.7 %copy-start.11 = (f32[32]{0:T(128)S(1)}, f32[32]{0:T(128)}, u32[]{:S(2)}) copy-start(f32[32]{0:T(128)} %get-tuple-element.160) | copy-start | bytes 388
  2044.5 98.6 %copy-start.8 = (f32[3,3,15]{2,1,0:T(4,128)S(1)}, f32[3,3,15]{2,1,0:T(4,128)}, u32[]{:S(2)}) copy-start(f32[3,3,15]{2,1,0:T(4,128)} %param.5) | copy-start | bytes 1624
  2140.0 12.6 collective-permute-start.12
  2141.7 13.8 collective-permute-start.13
  2152.5 3.0 copy-start.1
  2329.7 160.7 %collective-permute-start.14 = (bf16[2,32,64,7,64]{4,2,3,1,0:T(8,128)(2,1)S(1)}, bf16[2,32,64,7,64]{4,2,3,1,0:T(8,128)(2,1)S(1)}, u32[]{:S(2)}, u32[]{:S(2)}) collective-permute-start(bf16[2,32,64,7,64]{4,2,3,1,0:T(8,128)(2,1)S(1)} %get-tuple-element.7), channel_id=1, source_target_pairs={{0,2},{1,3},{4,6},{5,7}} | collective-permute-start | bytes 11010056 | tf_op jit(solution)/shard_map/ppermute | solution.py:28
  2333.1 161.9 %collective-permute-start.15 = (bf16[2,32,64,7,64]{4,2,3,1,0:T(8,128)(2,1)S(1)}, bf16[2,32,64,7,64]{4,2,3,1,0:T(8,128)(2,1)}, u32[]{:S(2)}, u32[]{:S(2)}) collective-permute-start(bf16[2,32,64,7,64]{4,2,3,1,0:T(8,128)(2,1)S(1)} %get-tuple-element.8), channel_id=1, source_target_pairs={{2,0},{3,1},{6,4},{7,5}} | collective-permute-start | bytes 11010056 | tf_op jit(solution)/shard_map/ppermute | solution.py:29
  2490.4 3.0 copy-start.4
  2657.0 161.1 %collective-permute-start.16 = (bf16[2,32,64,64,7]{3,2,4,1,0:T(8,128)(2,1)}, bf16[2,32,64,64,7]{3,2,4,1,0:T(8,128)(2,1)}, u32[]{:S(2)}, u32[]{:S(2)}) collective-permute-start(bf16[2,32,64,64,7]{3,2,4,1,0:T(8,128)(2,1)} %copy.37), channel_id=1, source_target_pairs={{0,4},{1,5},{2,6},{3,7}} | collective-permute-start | bytes 11010056 | tf_op jit(solution)/shard_map/ppermute | solution.py:28
  2669.6 169.6 %collective-permute-start.17 = (bf16[2,32,64,64,7]{3,2,4,1,0:T(8,128)(2,1)}, bf16[2,32,64,64,7]{3,2,4,1,0:T(8,128)(2,1)S(1)}, u32[]{:S(2)}, u32[]{:S(2)}) collective-permute-start(bf16[2,32,64,64,7]{3,2,4,1,0:T(8,128)(2,1)} %copy.38), channel_id=1, source_target_pairs={{4,0},{5,1},{6,2},{7,3}} | collective-permute-start | bytes 11010056 | tf_op jit(solution)/shard_map/ppermute | solution.py:29
  2912.2 97.7 %copy-start.10 = (f32[32]{0:T(128)S(1)}, f32[32]{0:T(128)}, u32[]{:S(2)}) copy-start(f32[32]{0:T(128)} %get-tuple-element.158) | copy-start | bytes 388
where the time goes:
time: 3170 us; the launch traced here: 3140 us
  matrix products  931 us (29%)
  waiting for transfers between devices  925 us (29%)
  local copies, waits for them, and re-layouts  792 us (25%)
  other arithmetic  439 us (14%)
  starting transfers between devices  56.6 us (2%)
    ppermute x9, waiting for transfers between devices, neighbour_planes(): from_lower = lax.ppermute(high_planes, axis_name, upward)  919 us
    dot_general x7, matrix products, local_layers(): jnp.einsum(PASS_FORMS[pass_idx], padded, matrix, preferred_element_type=j...  654 us
    concatenate x8, other arithmetic, local_layers(): padded = jnp.concatenate([from_lower, current, from_upper], axis=axis_dim)  439 us
    concatenate x3, local copies, waits for them, and re-layouts, local_layers(): padded = jnp.concatenate([from_lower, current, from_upper], axis=axis_dim)  292 us
    dot_general x3, matrix products, local_layers(): jnp.einsum('cd,vcxyz->vdxyz', mix_weight[layer_idx], current, preferred_e...  277 us
    ppermute x4, local copies, waits for them, and re-layouts, neighbour_planes(): from_lower = lax.ppermute(high_planes, axis_name, upward)  115 us
    unnamed x25, local copies, waits for them, and re-layouts  108 us
    ppermute x4, local copies, waits for them, and re-layouts, neighbour_planes(): from_upper = lax.ppermute(low_planes, axis_name, downward)  106 us
  transfers between devices with their start and end apart: 18, of which 11 were waited for; matrix products, arithmetic and copies ran while one was open for 7% of the time, Pallas kernels for 0%

commit v1 on v0

v1 whole, which is shorter than its diff:
```python
import functools

import jax
import jax.numpy as jnp
from jax import lax
from jax.experimental import pallas as pl
from jax.experimental.pallas import tpu as pltpu
from jax.sharding import PartitionSpec as P

SWAP = [(0, 1), (1, 0)]
DIAG = [(0, 3), (1, 2), (2, 1), (3, 0)]
SUB = 16
GROUPS = 4
LANES = 128
PARAMS = pltpu.CompilerParams(vmem_limit_bytes=60 * 1024 * 1024)


def band(taps, offset):
    out = jnp.zeros(taps.shape[:-1] + offset.shape, jnp.float32)
    for t in range(taps.shape[-1]):
        out = out + jnp.where(offset == t, taps[..., t].reshape(taps.shape[:-1] + (1,) * offset.ndim), 0.0)
    return out


def pass_i_weights(taps):
    half = (taps.shape[-1] - 1) // 2
    row = lax.broadcasted_iota(jnp.int32, (8 * SUB, 16 * SUB), 0)
    col = lax.broadcasted_iota(jnp.int32, (8 * SUB, 16 * SUB), 1)
    own, up = col < 8 * SUB, col < 12 * SUB
    point = jnp.where(own, col // SUB, (col % (4 * SUB)) // 8)
    source = jnp.where(own, col % SUB, jnp.where(up, SUB + col % 8, col % 8 - 8))
    offset = jnp.where(row // SUB == point, source - row % SUB + half, -1)
    return band(taps, offset).astype(jnp.bfloat16)


def pass_jk_weights(taps, side):
    half = (taps.shape[-1] - 1) // 2
    shape = (3, SUB, 2 * SUB)
    variant = lax.broadcasted_iota(jnp.int32, shape, 0)
    out = lax.broadcasted_iota(jnp.int32, shape, 1)
    slot = lax.broadcasted_iota(jnp.int32, shape, 2)
    missing_low = (variant == 0) & (slot < half) & (side == 0)
    missing_high = (variant == 2) & (slot >= SUB + half) & (side == 1)
    small = band(taps, jnp.where(missing_low | missing_high, -1, slot - out)).astype(jnp.bfloat16)
    rows, cols = SUB * SUB, 2 * SUB * SUB
    spread_rows = (jnp.arange(rows)[:, None] // SUB == jnp.arange(SUB)[None, :]).astype(jnp.bfloat16)
    spread_cols = (jnp.arange(2 * SUB)[:, None] == jnp.arange(cols)[None, :] // SUB).astype(jnp.bfloat16)
    same = jnp.arange(rows)[:, None] % SUB == jnp.arange(cols)[None, :] % SUB
    tall = jnp.einsum('ra,lvas->lvrs', spread_rows, small, preferred_element_type=jnp.float32).astype(jnp.bfloat16)
    wide = jnp.einsum('lvrs,sc->lvrc', tall, spread_cols, preferred_element_type=jnp.float32)
    return jnp.where(same, wide, 0.0).astype(jnp.bfloat16)


def pass_i_kernel(flags, w_ref, y_ref, n_ref, o_ref):
    jb, kk = y_ref.shape[0], y_ref.shape[1]
    lane = lax.broadcasted_iota(jnp.int32, (1, SUB, LANES), 2)
    has_up, has_low = flags[0] > 0, flags[1] > 0
    weights = w_ref[...]
    zero = jnp.zeros((4, SUB, LANES), jnp.bfloat16)
    width = LANES // GROUPS

    def columns(j, k):
        own = y_ref[j, pl.ds(k, 8)]
        full = own.astype(jnp.float32)
        peer = n_ref[j, pl.ds(k // 2, 4)]
        lo = full[:, :8].reshape(4, SUB, LANES).astype(jnp.bfloat16)
        hi = full[:, 8:].reshape(4, SUB, LANES).astype(jnp.bfloat16)
        up = jnp.where(lane < width, jnp.where(has_up, peer, zero), lo)
        low = jnp.where(lane >= LANES - width, jnp.where(has_low, peer, zero), hi)
        up = pltpu.roll(up, LANES - width, 2)
        low = pltpu.roll(low, width, 2)
        return jnp.concatenate([own.reshape(8 * SUB, LANES), up.reshape(4 * SUB, LANES), low.reshape(4 * SUB, LANES)], axis=0)

    group = 4

    def step(q, carry):
        for r in range(group):
            j = q * group + r
            stacks = [jnp.concatenate([columns(j, k), columns(j, k + 8)], axis=1) for k in range(0, kk, 16)]
            for stack, k in zip(stacks, range(0, kk, 16)):
                out = jnp.dot(weights, stack, preferred_element_type=jnp.float32).astype(jnp.bfloat16)
                o_ref[j, pl.ds(k, 8)] = out[:, :LANES].reshape(8, SUB, LANES)
                o_ref[j, pl.ds(k + 8, 8)] = out[:, LANES:].reshape(8, SUB, LANES)
        return carry

    lax.fori_loop(0, jb // group, step, 0)


def pass_i(flags, weights, y, peer, block=8):
    nj, nk = y.shape[0], y.shape[1]
    return pl.pallas_call(
        pass_i_kernel,
        out_shape=jax.ShapeDtypeStruct(y.shape, y.dtype),
        grid=(nj // block,),
        in_specs=[
            pl.BlockSpec(memory_space=pltpu.SMEM),
            pl.BlockSpec(weights.shape, lambda b: (0, 0)),
            pl.BlockSpec((block, nk, SUB, LANES), lambda b: (b, 0, 0, 0)),
            pl.BlockSpec((block, nk // 2, SUB, LANES), lambda b: (b, 0, 0, 0)),
        ],
        out_specs=pl.BlockSpec((block, nk, SUB, LANES), lambda b: (b, 0, 0, 0)),
        compiler_params=PARAMS,
        cost_estimate=pl.CostEstimate(flops=nj * nk * 2 * SUB * 32 * 8 * LANES, bytes_accessed=nj * nk * 10240, transcendentals=0),
        name="pass_i",
    )(flags, weights, y, peer)


def slots(part, own, halo, n, half):
    lo, hi = part * SUB - half, part * SUB - half + 2 * SUB
    pieces = []
    if lo < 0:
        pieces.append(halo(slice(0, -lo)))
    pieces.append(own(slice(max(lo, 0), min(hi, n))))
    if hi > n:
        pieces.append(halo(slice(0, half)))
        if hi - n > half:
            pieces.append(halo(slice(0, hi - n - half)))
    stack = jnp.concatenate(pieces, axis=0) if len(pieces) > 1 else pieces[0]
    return stack.reshape(2 * SUB * SUB, LANES)


def pass_j_kernel(w_ref, u_ref, h_ref, o_ref):
    nj, kb = u_ref.shape[0], u_ref.shape[1]
    half = h_ref.shape[0]
    parts = nj // SUB

    def pair(k0, k1):
        for part in range(parts):
            sides = [slots(part, lambda s, k=k: u_ref[s, k], lambda s, k=k: h_ref[s, k], nj, half) for k in (k0, k1)]
            variant = 0 if part == 0 else (2 if part == parts - 1 else 1)
            out = jnp.dot(w_ref[variant], jnp.concatenate(sides, axis=1), preferred_element_type=jnp.float32).astype(jnp.bfloat16)
            o_ref[part * SUB:(part + 1) * SUB, k0] = out[:, :LANES].reshape(SUB, SUB, LANES)
            o_ref[part * SUB:(part + 1) * SUB, k1] = out[:, LANES:].reshape(SUB, SUB, LANES)

    for q in range((kb + 1) // 2):
        pair(2 * q, min(2 * q + 1, kb - 1))


def pass_j(weights, u, halo, block):
    nj, nk = u.shape[0], u.shape[1]
    return pl.pallas_call(
        pass_j_kernel,
        out_shape=jax.ShapeDtypeStruct(u.shape, u.dtype),
        grid=(nk // block,),
        in_specs=[
            pl.BlockSpec(weights.shape, lambda b: (0, 0, 0)),
            pl.BlockSpec((nj, block, SUB, LANES), lambda b: (0, b, 0, 0)),
            pl.BlockSpec((halo.shape[0], block, SUB, LANES), lambda b: (0, b, 0, 0)),
        ],
        out_specs=pl.BlockSpec((nj, block, SUB, LANES), lambda b: (0, b, 0, 0)),
        compiler_params=PARAMS,
        cost_estimate=pl.CostEstimate(flops=nj * nk * 2 * SUB * 512 * LANES, bytes_accessed=nj * nk * 8192, transcendentals=0),
        name="pass_j",
    )(weights, u, halo)


def gelu_tanh(x):
    inner = x * (0.7978845608028654 + (0.7978845608028654 * 0.044715) * (x * x))
    half_x = 0.5 * x
    return half_x + half_x * jnp.tanh(inner)


def pass_k_kernel(flags, w_ref, m_ref, b_ref, u_ref, h_ref, y_ref, o_ref, f_ref):
    jb, nk = u_ref.shape[0], u_ref.shape[1]
    half = h_ref.shape[1]
    parts = nk // SUB
    send_high = flags[0] > 0
    rows = 128
    tiles = rows // SUB

    def filtered(j0, part):
        sides = [slots(part, lambda s, j=j: u_ref[j, s], lambda s, j=j: h_ref[j, s], nk, half) for j in (j0, j0 + 1)]
        variant = 0 if part == 0 else (2 if part == parts - 1 else 1)
        return jnp.dot(w_ref[variant], jnp.concatenate(sides, axis=1), preferred_element_type=jnp.float32).astype(jnp.bfloat16)

    def finish(j0, part, u3):
        for r in range(SUB * SUB // rows):
            z = jnp.dot(u3[r * rows:(r + 1) * rows], m_ref[...], preferred_element_type=jnp.float32) + b_ref[...]
            act = gelu_tanh(z)
            k0 = part * SUB + r * tiles
            for side in range(2):
                new = y_ref[j0 + side, k0:k0 + tiles].astype(jnp.float32) + act[:, side * LANES:(side + 1) * LANES].reshape(tiles, SUB, LANES)
                o_ref[j0 + side, k0:k0 + tiles] = new.astype(jnp.bfloat16)
                face = jnp.where(send_high, new[:, 8:], new[:, :8])
                f_ref[j0 + side, k0 // 2:(k0 + tiles) // 2] = face.reshape(tiles // 2, SUB, LANES).astype(jnp.bfloat16)

    def step(q, carry):
        waiting = []
        for j0 in (4 * q, 4 * q + 2):
            for part in range(parts):
                waiting.append((j0, part, filtered(j0, part)))
                if len(waiting) > 2:
                    finish(*waiting.pop(0))
        for item in waiting:
            finish(*item)
        return carry

    lax.fori_loop(0, jb // 4, step, 0)


def pass_k(flags, weights, mix, bias, u, halo, y, block=4):
    nj, nk = u.shape[0], u.shape[1]
    return pl.pallas_call(
        pass_k_kernel,
        out_shape=(jax.ShapeDtypeStruct(u.shape, u.dtype), jax.ShapeDtypeStruct((nj, nk // 2, SUB, LANES), u.dtype)),
        grid=(nj // block,),
        in_specs=[
            pl.BlockSpec(memory_space=pltpu.SMEM),
            pl.BlockSpec(weights.shape, lambda b: (0, 0, 0)),
            pl.BlockSpec(mix.shape, lambda b: (0, 0)),
            pl.BlockSpec(bias.shape, lambda b: (0, 0)),
            pl.BlockSpec((block, nk, SUB, LANES), lambda b: (b, 0, 0, 0)),
            pl.BlockSpec((block, halo.shape[1], SUB, LANES), lambda b: (b, 0, 0, 0)),
            pl.BlockSpec((block, nk, SUB, LANES), lambda b: (b, 0, 0, 0)),
        ],
        out_specs=(
            pl.BlockSpec((block, nk, SUB, LANES), lambda b: (b, 0, 0, 0)),
            pl.BlockSpec((block, nk // 2, SUB, LANES), lambda b: (b, 0, 0, 0)),
        ),
        compiler_params=PARAMS,
        cost_estimate=pl.CostEstimate(flops=nj * nk * 2 * SUB * (512 + 256) * LANES, bytes_accessed=nj * nk * 14336, transcendentals=nj * nk * SUB * LANES),
        name="pass_k_mix",
    )(flags, weights, mix, bias, u, halo, y)


PITCH = 24


def enter_kernel(flags, x_ref, o_ref, f_ref, s1, s2):
    nc, nk = x_ref.shape[1], x_ref.shape[4]
    rows = GROUPS * nc
    send_high = flags[0] > 0

    def pair(p, carry):
        for g in range(GROUPS):
            for c in range(nc):
                i0 = g * SUB + 2 * p
                tile = jnp.concatenate([x_ref[0, c, i0], x_ref[0, c, i0 + 1]], axis=1)
                s1[(g * nc + c) * PITCH:(g * nc + c) * PITCH + SUB, :] = tile.astype(jnp.float32)
        for j in range(SUB):
            flip = s1[pl.ds(j, rows, stride=PITCH), :].T
            base = j * nk * PITCH + 2 * p
            s2[pl.ds(base, nk, stride=PITCH), :] = flip[:nk]
            s2[pl.ds(base + 1, nk, stride=PITCH), :] = flip[nk:]
        return carry

    lax.fori_loop(0, SUB // 2, pair, 0)

    def emit(j, carry):
        base = pl.multiple_of(j * (nk * PITCH), 8)
        for k in range(0, nk, 2):
            faces = []
            for side in range(2):
                tile = s2[pl.ds(base + (k + side) * PITCH, SUB), :]
                o_ref[j, k + side] = tile.astype(jnp.bfloat16)
                faces.append(jnp.where(send_high, tile[8:], tile[:8]))
            f_ref[j, k // 2] = jnp.concatenate(faces, axis=0).astype(jnp.bfloat16)
        return carry

    lax.fori_loop(0, SUB, emit, 0)


def enter(flags, vol, v):
    nv, nc, ni, nj, nk = vol.shape
    return pl.pallas_call(
        enter_kernel,
        out_shape=(jax.ShapeDtypeStruct((nj, nk, SUB, LANES), vol.dtype), jax.ShapeDtypeStruct((nj, nk // 2, SUB, LANES), vol.dtype)),
        grid=(nj // SUB,),
        in_specs=[pl.BlockSpec(memory_space=pltpu.SMEM), pl.BlockSpec((1, nc, ni, SUB, nk), lambda b: (v, 0, 0, b, 0))],
        out_specs=(
            pl.BlockSpec((SUB, nk, SUB, LANES), lambda b: (b, 0, 0, 0)),
            pl.BlockSpec((SUB, nk // 2, SUB, LANES), lambda b: (b, 0, 0, 0)),
        ),
        scratch_shapes=[pltpu.VMEM((GROUPS * nc * PITCH, 2 * nk), jnp.float32), pltpu.VMEM((SUB * nk * PITCH, LANES), jnp.float32)],
        compiler_params=PARAMS,
        cost_estimate=pl.CostEstimate(flops=10**8, bytes_accessed=nj * nk * 12288, transcendentals=0),
        name="enter",
    )(flags, vol)


def leave_kernel(y_ref, *rest):
    o_ref, s1, s2 = rest[-3:]
    nc, nk = o_ref.shape[1], o_ref.shape[4]
    rows = GROUPS * nc

    def take(j, carry):
        base = pl.multiple_of(j * (nk * PITCH), 8)
        for k in range(nk):
            s2[pl.ds(base + k * PITCH, SUB), :] = y_ref[j, k].astype(jnp.float32)
        return carry

    lax.fori_loop(0, SUB, take, 0)

    def pair(p, carry):
        for j in range(SUB):
            base = j * nk * PITCH + 2 * p
            both = jnp.concatenate([s2[pl.ds(base, nk, stride=PITCH), :], s2[pl.ds(base + 1, nk, stride=PITCH), :]], axis=0)
            s1[pl.ds(j, rows, stride=PITCH), :] = both.T
        for g in range(GROUPS):
            for c in range(nc):
                i0 = g * SUB + 2 * p
                tile = s1[(g * nc + c) * PITCH:(g * nc + c) * PITCH + SUB, :].astype(jnp.bfloat16)
                o_ref[0, c, i0] = tile[:, :nk]
                o_ref[0, c, i0 + 1] = tile[:, nk:]
        return carry

    lax.fori_loop(0, SUB // 2, pair, 0)


def leave(y, v, shape, previous):
    nv, nc, ni, nj, nk = shape
    extra = [] if previous is None else [previous]
    return pl.pallas_call(
        leave_kernel,
        out_shape=jax.ShapeDtypeStruct(shape, y.dtype),
        grid=(nj // SUB,),
        in_specs=[pl.BlockSpec((SUB, nk, SUB, LANES), lambda b: (b, 0, 0, 0))] + [pl.BlockSpec(memory_space=pl.ANY)] * len(extra),
        out_specs=pl.BlockSpec((1, nc, ni, SUB, nk), lambda b: (v, 0, 0, b, 0)),
        scratch_shapes=[pltpu.VMEM((GROUPS * nc * PITCH, 2 * nk), jnp.float32), pltpu.VMEM((SUB * nk * PITCH, LANES), jnp.float32)],
        input_output_aliases={1: 0} if extra else {},
        compiler_params=PARAMS,
        cost_estimate=pl.CostEstimate(flops=10**8, bytes_accessed=nj * nk * 12288, transcendentals=0),
        name="leave",
    )(y, *extra)


def solution(mesh):
    vol_spec = P('dp', None, 'px', 'py', 'pz')

    def local_layers(vol_block, filter_taps, mix_weight, mix_bias):
        nv, nc, ni, nj, nk = vol_block.shape
        layers = filter_taps.shape[0]
        half = (filter_taps.shape[2] - 1) // 2
        px, py, pz = lax.axis_index('px'), lax.axis_index('py'), lax.axis_index('pz')
        taps = filter_taps.astype(jnp.bfloat16).astype(jnp.float32)
        w_i = pass_i_weights(taps[:, 0])
        w_j = pass_jk_weights(taps[:, 1], py)
        w_k = pass_jk_weights(taps[:, 2], pz)
        eye = jnp.eye(2 * GROUPS, dtype=jnp.bfloat16)
        mix = (eye[None, :, None, :, None] * mix_weight[:, None, :, None, :]).reshape(layers, 2 * LANES, 2 * LANES)
        bias = jnp.tile(mix_bias, (1, 2 * GROUPS)).reshape(layers, 1, 2 * LANES)
        flags_x = jnp.stack([px == 0, px == 1]).astype(jnp.int32)
        j_at = jnp.where(py == 0, nj - half, 0)
        k_at = jnp.where(pz == 0, nk - half, 0)

        state, peers = [], []
        for v in range(nv):
            y, face = enter(flags_x, vol_block, v)
            state.append(y)
            peers.append(lax.ppermute(face, 'px', SWAP))
        for layer in range(layers):
            firsts = []
            for v in range(nv):
                u1 = pass_i(flags_x, w_i[layer], state[v], peers[v])
                j_face = lax.dynamic_slice_in_dim(u1, j_at, half, axis=0)
                k_face = lax.dynamic_slice_in_dim(u1, k_at, half, axis=1)
                corner = lax.dynamic_slice_in_dim(j_face, k_at, half, axis=1)
                firsts.append((
                    u1,
                    lax.ppermute(j_face, 'py', SWAP),
                    lax.ppermute(k_face, 'pz', SWAP),
                    lax.ppermute(corner, ('pz', 'py'), DIAG),
                ))
            for v in range(nv):
                u1, j_halo, k_halo, corner = firsts[v]
                u2 = pass_j(w_j[layer], u1, j_halo, 16)
                u2_halo = pass_j(w_j[layer], k_halo, corner, half)
                state[v], face = pass_k(flags_x, w_k[layer], mix[layer], bias[layer], u2, u2_halo, state[v])
                if layer + 1 < layers:
                    peers[v] = lax.ppermute(face, 'px', SWAP)
        out = None
        for v in range(nv):
            out = leave(state[v], v, vol_block.shape, out)
        return out

    return jax.shard_map(local_layers, mesh=mesh, in_specs=(vol_spec, P(), P(), P()), out_specs=vol_spec, check_vma=False)
```

time: 3170 us -> 684 us (0.22)
  matrix products: 931 us -> 3.92 us
  waiting for transfers between devices: 925 us -> 41.4 us
  local copies, waits for them, and re-layouts: 792 us -> 53.2 us
  Pallas kernels: 0 us -> 547 us
  other arithmetic: 439 us -> 2.26 us
  starting transfers between devices: 56.6 us -> 24.2 us
    dot_general x10 -> x2, matrix products: 931 us -> 3.92 us  [pass_jk_weights(): jnp.einsum('lvrs,sc->lvrc', tall, spread_cols, preferred_element_type=jnp...]
    ppermute x18 -> x24, waiting for transfers between devices: 925 us -> 41.4 us  [the longest x6 33.4 us: local_layers(): lax.ppermute(corner, ('pz', 'py'), DIAG)]
    pallas_call x0 -> x28, Pallas kernels: none -> 547 us  [the longest x6 187 us: pass_k(): pl.pallas_call(pass_k_kernel, out_shape=(jax.ShapeDtypeStruct(u.shape, u....]
    concatenate x8 -> x0, other arithmetic: 439 us -> none  [local_layers(): padded = jnp.concatenate([from_lower, current, from_upper], axis=axis_dim)]
    concatenate x3 -> x0, local copies, waits for them, and re-layouts: 292 us -> none  [local_layers(): padded = jnp.concatenate([from_lower, current, from_upper], axis=axis_dim)]
    ppermute x8 -> x0, local copies, waits for them, and re-layouts: 221 us -> none  [the longest x4 115 us: neighbour_planes(): from_lower = lax.ppermute(high_planes, axis_name, upward)]
    slice x15 -> x6, local copies, waits for them, and re-layouts: 119 us -> 2.73 us  [the longest x3 1.21 us: band(): taps[..., t].reshape(taps.shape[:-1] + (1,) * offset.ndim)]
    unnamed x25 -> x26, local copies, waits for them, and re-layouts: 108 us -> 3.1 us
  transfers between devices with their start and end apart: 18 -> 24, of which waited for: 11 -> 4; matrix products, arithmetic and copies ran while one was open for 7% -> 8% of each run, Pallas kernels for 0% -> 67%
where the time goes in v1:
time: 684 us; the launch traced here: 673 us
  Pallas kernels  547 us (80%)
  local copies, waits for them, and re-layouts  53.2 us (8%)
  waiting for transfers between devices  41.4 us (6%)
  starting transfers between devices  24.2 us (4%)
    pallas_call x6, Pallas kernels, pass_k(): pl.pallas_call(pass_k_kernel, out_shape=(jax.ShapeDtypeStruct(u.shape, u....  187 us
    pallas_call x12, Pallas kernels, pass_j(): pl.pallas_call(pass_j_kernel, out_shape=jax.ShapeDtypeStruct(u.shape, u.d...  126 us
    pallas_call x6, Pallas kernels, pass_i(): pl.pallas_call(pass_i_kernel, out_shape=jax.ShapeDtypeStruct(y.shape, y.d...  115 us
    pallas_call x2, Pallas kernels, leave(): pl.pallas_call(leave_kernel, out_shape=jax.ShapeDtypeStruct(shape, y.dtyp...  65 us
    pallas_call x2, Pallas kernels, enter(): pl.pallas_call(enter_kernel, out_shape=(jax.ShapeDtypeStruct((nj, nk, SUB...  54 us
    ppermute x6, waiting for transfers between devices, local_layers(): lax.ppermute(corner, ('pz', 'py'), DIAG)  33.4 us
    dynamic_slice x6, local copies, waits for them, and re-layouts, local_layers(): k_face = lax.dynamic_slice_in_dim(u1, k_at, half, axis=1)  17.3 us
    dynamic_slice x6, local copies, waits for them, and re-layouts, local_layers(): j_face = lax.dynamic_slice_in_dim(u1, j_at, half, axis=0)  16 us
  transfers between devices with their start and end apart: 24, of which 4 were waited for; matrix products, arithmetic and copies ran while one was open for 8% of the time, Pallas kernels for 67%

profile of v1, /device:TPU:0, one launch (start us, length us, event | category | flops | bytes accessed | tf_op | source)
XLA Modules:
  0.0 672.7 jit_solution(1405571444938126249)
XLA Ops:
  0.6 26.9 %enter.3 = (bf16[64,64,16,128]{3,2,1,0:T(8,128)(2,1)}, bf16[64,32,16,128]{3,2,1,0:T(8,128)(2,1)}) custom-call(s32[2]{0:T(128)} %add_convert_fusion.7.flags, bf16[2,32,64,64,64]{4,3,2,1,0:T(8,128)(2,1)} %x_ref.3), custom_call_target="tpu_custom_call" | custom-call | flops 100000000 | bytes 50331648 | tf_op jit(solution)/shard_map/enter/pallas_call | solution.py:265
  28.4 27.1 %enter.2 = (bf16[64,64,16,128]{3,2,1,0:T(8,128)(2,1)}, bf16[64,32,16,128]{3,2,1,0:T(8,128)(2,1)}) custom-call(s32[2]{0:T(128)} %add_convert_fusion.7.flags, bf16[2,32,64,64,64]{4,3,2,1,0:T(8,128)(2,1)} %x_ref.3), custom_call_target="tpu_custom_call" | custom-call | flops 100000000 | bytes 50331648 | tf_op jit(solution)/shard_map/enter/pallas_call | solution.py:265
  57.9 1.0 squeeze.81.m_ref
  62.4 1.2 select_convert_fusion
  63.6 19.2 %pass_i.9.u_ref = bf16[64,64,16,128]{3,2,1,0:T(8,128)(2,1)} custom-call(s32[2]{0:T(128)} %add_convert_fusion.7.flags, bf16[128,256]{1,0:T(8,128)(2,1)} %get-tuple-element.89.w_ref, bf16[64,64,16,128]{3,2,1,0:T(8,128)(2,1)} %get-tuple-element.26.y_ref, bf16[64,32,16,128]{3,2,1,0:T(8,128)(2,1)} %collective-permute-done.12.n_ref), custom_call_target="tpu_custom_call" | custom-call | flops 4294967296 | bytes 41943040 | tf_op jit(solution)/shard_map/pass_i/pallas_call | solution.py:91
  82.8 3.1 constant_dynamic-slice_fusion.8
  85.8 3.0 collective-permute-start.13
  88.8 3.1 constant_dynamic-slice_fusion.7
  91.9 1.5 collective-permute-start.14
  93.4 2.7 select_convert_fusion.1
  96.1 1.5 slice_bitcast_fusion
  97.6 1.0 copy-done
  98.6 1.4 slice_bitcast_fusion.1
  101.0 19.1 %pass_i.6.u_ref = bf16[64,64,16,128]{3,2,1,0:T(8,128)(2,1)} custom-call(s32[2]{0:T(128)} %add_convert_fusion.7.flags, bf16[128,256]{1,0:T(8,128)(2,1)} %get-tuple-element.89.w_ref, bf16[64,64,16,128]{3,2,1,0:T(8,128)(2,1)} %get-tuple-element.19.y_ref, bf16[64,32,16,128]{3,2,1,0:T(8,128)(2,1)} %collective-permute-done.n_ref), custom_call_target="tpu_custom_call" | custom-call | flops 4294967296 | bytes 41943040 | tf_op jit(solution)/shard_map/pass_i/pallas_call | solution.py:91
  120.2 3.2 constant_dynamic-slice_fusion.17
  123.4 0.9 constant_dynamic-slice_fusion.15
  124.3 2.9 collective-permute-start.3
  127.8 1.8 constant_dynamic-slice_fusion.16
  129.6 5.9 collective-permute-done.15.h_ref
  135.5 7.9 %collective-permute-done.14.u_ref = bf16[64,7,16,128]{3,2,1,0:T(8,128)(2,1)} collective-permute-done((bf16[64,7,16,128]{3,2,1,0:T(8,128)(2,1)}, bf16[64,7,16,128]{3,2,1,0:T(8,128)(2,1)}, u32[]{:S(2)}, u32[]{:S(2)}) %collective-permute-start.14) | collective-permute-done | bytes 1835040 | tf_op jit(solution)/shard_map/ppermute | solution.py:361
  143.4 4.2 pass_j.19.h_ref
  147.6 16.9 %pass_j.18.u_ref = bf16[64,64,16,128]{3,2,1,0:T(8,128)(2,1)} custom-call(bf16[3,256,512]{2,1,0:T(8,128)(2,1)} %get-tuple-element.80.w_ref, bf16[64,64,16,128]{3,2,1,0:T(8,128)(2,1)} %pass_i.9.u_ref, bf16[7,64,16,128]{3,2,1,0:T(8,128)(2,1)} %collective-permute-done.13.h_ref), custom_call_target="tpu_custom_call" | custom-call | flops 8589934592 | bytes 33554432 | tf_op jit(solution)/shard_map/pass_j/pallas_call | solution.py:141
  164.5 31.1 %pass_k_mix.9 = (bf16[64,64,16,128]{3,2,1,0:T(8,128)(2,1)}, bf16[64,32,16,128]{3,2,1,0:T(8,128)(2,1)}) custom-call(s32[2]{0:T(128)} %add_convert_fusion.7.flags, bf16[3,256,512]{2,1,0:T(8,128)(2,1)} %get-tuple-element.83.w_ref, bf16[256,256]{1,0:T(8,128)(2,1)} %squeeze.81.m_ref, f32[1,256]{1,0:T(1,128)} %tile.21.b_ref, ...), custom_call_target="tpu_custom_call" | custom-call | flops 12884901888 | bytes 58720256 | tf_op jit(solution)/shard_map/pass_k_mix/pallas_call | solution.py:203
  195.7 16.7 %pass_j.12.u_ref = bf16[64,64,16,128]{3,2,1,0:T(8,128)(2,1)} custom-call(bf16[3,256,512]{2,1,0:T(8,128)(2,1)} %get-tuple-element.80.w_ref, bf16[64,64,16,128]{3,2,1,0:T(8,128)(2,1)} %pass_i.6.u_ref, bf16[7,64,16,128]{3,2,1,0:T(8,128)(2,1)} %collective-permute-done.1.h_ref), custom_call_target="tpu_custom_call" | custom-call | flops 8589934592 | bytes 33554432 | tf_op jit(solution)/shard_map/pass_j/pallas_call | solution.py:141
  213.1 4.2 pass_j.13.h_ref
  217.3 31.1 %pass_k_mix.6 = (bf16[64,64,16,128]{3,2,1,0:T(8,128)(2,1)}, bf16[64,32,16,128]{3,2,1,0:T(8,128)(2,1)}) custom-call(s32[2]{0:T(128)} %add_convert_fusion.7.flags, bf16[3,256,512]{2,1,0:T(8,128)(2,1)} %get-tuple-element.83.w_ref, bf16[256,256]{1,0:T(8,128)(2,1)} %squeeze.81.m_ref, f32[1,256]{1,0:T(1,128)} %tile.21.b_ref, ...), custom_call_target="tpu_custom_call" | custom-call | flops 12884901888 | bytes 58720256 | tf_op jit(solution)/shard_map/pass_k_mix/pallas_call | solution.py:203
  248.9 19.1 %pass_i.10.u_ref = bf16[64,64,16,128]{3,2,1,0:T(8,128)(2,1)} custom-call(s32[2]{0:T(128)} %add_convert_fusion.7.flags, bf16[128,256]{1,0:T(8,128)(2,1)} %get-tuple-element.90.w_ref, bf16[64,64,16,128]{3,2,1,0:T(8,128)(2,1)} %get-tuple-element.28.y_ref, bf16[64,32,16,128]{3,2,1,0:T(8,128)(2,1)} %collective-permute-done.16.n_ref), custom_call_target="tpu_custom_call" | custom-call | flops 4294967296 | bytes 41943040 | tf_op jit(solution)/shard_map/pass_i/pallas_call | solution.py:91
  268.1 3.1 constant_dynamic-slice_fusion.4
  271.2 1.5 collective-permute-start.18
  272.7 1.8 constant_dynamic-slice_fusion.5
  275.7 1.0 squeeze.38.m_ref
  276.7 0.9 constant_dynamic-slice_fusion.3
  277.6 1.5 collective-permute-start.19
  279.1 19.1 %pass_i.7.u_ref = bf16[64,64,16,128]{3,2,1,0:T(8,128)(2,1)} custom-call(s32[2]{0:T(128)} %add_convert_fusion.7.flags, bf16[128,256]{1,0:T(8,128)(2,1)} %get-tuple-element.90.w_ref, bf16[64,64,16,128]{3,2,1,0:T(8,128)(2,1)} %get-tuple-element.21.y_ref, bf16[64,32,16,128]{3,2,1,0:T(8,128)(2,1)} %collective-permute-done.4.n_ref), custom_call_target="tpu_custom_call" | custom-call | flops 4294967296 | bytes 41943040 | tf_op jit(solution)/shard_map/pass_i/pallas_call | solution.py:91
  298.2 3.1 constant_dynamic-slice_fusion.14
  302.2 1.5 collective-permute-start.7
  303.7 1.5 collective-permute-start.5
  305.2 3.1 constant_dynamic-slice_fusion.13
  308.3 13.3 %collective-permute-done.19.h_ref = bf16[7,7,16,128]{3,2,1,0:T(8,128)(2,1)S(1)} collective-permute-done((bf16[7,7,16,128]{3,2,1,0:T(8,128)(2,1)S(1)}, bf16[7,7,16,128]{3,2,1,0:T(8,128)(2,1)S(1)}, u32[]{:S(2)}, u32[]{:S(2)}) %collective-permute-start.19) | collective-permute-done | bytes 200736 | tf_op jit(solution)/shard_map/ppermute | solution.py:362
  321.6 1.5 collective-permute-start.6
  323.2 4.2 pass_j.21.h_ref
  327.4 16.9 %pass_j.20.u_ref = bf16[64,64,16,128]{3,2,1,0:T(8,128)(2,1)} custom-call(bf16[3,256,512]{2,1,0:T(8,128)(2,1)} %get-tuple-element.81.w_ref, bf16[64,64,16,128]{3,2,1,0:T(8,128)(2,1)} %pass_i.10.u_ref, bf16[7,64,16,128]{3,2,1,0:T(8,128)(2,1)} %collective-permute-done.17.h_ref), custom_call_target="tpu_custom_call" | custom-call | flops 8589934592 | bytes 33554432 | tf_op jit(solution)/shard_map/pass_j/pallas_call | solution.py:141
  344.4 31.1 %pass_k_mix.10 = (bf16[64,64,16,128]{3,2,1,0:T(8,128)(2,1)}, bf16[64,32,16,128]{3,2,1,0:T(8,128)(2,1)}) custom-call(s32[2]{0:T(128)} %add_convert_fusion.7.flags, bf16[3,256,512]{2,1,0:T(8,128)(2,1)} %get-tuple-element.84.w_ref, bf16[256,256]{1,0:T(8,128)(2,1)} %squeeze.38.m_ref, f32[1,256]{1,0:T(1,128)} %tile.19.b_ref, ...), custom_call_target="tpu_custom_call" | custom-call | flops 12884901888 | bytes 58720256 | tf_op jit(solution)/shard_map/pass_k_mix/pallas_call | solution.py:203
  375.5 16.7 %pass_j.14.u_ref = bf16[64,64,16,128]{3,2,1,0:T(8,128)(2,1)} custom-call(bf16[3,256,512]{2,1,0:T(8,128)(2,1)} %get-tuple-element.81.w_ref, bf16[64,64,16,128]{3,2,1,0:T(8,128)(2,1)} %pass_i.7.u_ref, bf16[7,64,16,128]{3,2,1,0:T(8,128)(2,1)} %collective-permute-done.5.h_ref), custom_call_target="tpu_custom_call" | custom-call | flops 8589934592 | bytes 33554432 | tf_op jit(solution)/shard_map/pass_j/pallas_call | solution.py:141
  392.9 4.2 pass_j.15.h_ref
  397.2 31.1 %pass_k_mix.7 = (bf16[64,64,16,128]{3,2,1,0:T(8,128)(2,1)}, bf16[64,32,16,128]{3,2,1,0:T(8,128)(2,1)}) custom-call(s32[2]{0:T(128)} %add_convert_fusion.7.flags, bf16[3,256,512]{2,1,0:T(8,128)(2,1)} %get-tuple-element.84.w_ref, bf16[256,256]{1,0:T(8,128)(2,1)} %squeeze.38.m_ref, f32[1,256]{1,0:T(1,128)} %tile.19.b_ref, ...), custom_call_target="tpu_custom_call" | custom-call | flops 12884901888 | bytes 58720256 | tf_op jit(solution)/shard_map/pass_k_mix/pallas_call | solution.py:203
  428.7 19.1 %pass_i.11.u_ref = bf16[64,64,16,128]{3,2,1,0:T(8,128)(2,1)} custom-call(s32[2]{0:T(128)} %add_convert_fusion.7.flags, bf16[128,256]{1,0:T(8,128)(2,1)} %get-tuple-element.91.w_ref, bf16[64,64,16,128]{3,2,1,0:T(8,128)(2,1)} %get-tuple-element.30.y_ref, bf16[64,32,16,128]{3,2,1,0:T(8,128)(2,1)} %collective-permute-done.20.n_ref), custom_call_target="tpu_custom_call" | custom-call | flops 4294967296 | bytes 41943040 | tf_op jit(solution)/shard_map/pass_i/pallas_call | solution.py:91
  447.9 3.2 constant_dynamic-slice_fusion.1
  451.7 1.8 constant_dynamic-slice_fusion.2
  454.7 1.0 squeeze.32.m_ref
  456.6 2.3 collective-permute-start.23
  458.9 19.1 %pass_i.8.u_ref = bf16[64,64,16,128]{3,2,1,0:T(8,128)(2,1)} custom-call(s32[2]{0:T(128)} %add_convert_fusion.7.flags, bf16[128,256]{1,0:T(8,128)(2,1)} %get-tuple-element.91.w_ref, bf16[64,64,16,128]{3,2,1,0:T(8,128)(2,1)} %get-tuple-element.23.y_ref, bf16[64,32,16,128]{3,2,1,0:T(8,128)(2,1)} %collective-permute-done.8.n_ref), custom_call_target="tpu_custom_call" | custom-call | flops 4294967296 | bytes 41943040 | tf_op jit(solution)/shard_map/pass_i/pallas_call | solution.py:91
  478.1 3.0 constant_dynamic-slice_fusion.11
  482.7 1.5 collective-permute-start.9
  484.2 3.1 constant_dynamic-slice_fusion.10
  487.3 14.2 %collective-permute-done.23.h_ref = bf16[7,7,16,128]{3,2,1,0:T(8,128)(2,1)S(1)} collective-permute-done((bf16[7,7,16,128]{3,2,1,0:T(8,128)(2,1)S(1)}, bf16[7,7,16,128]{3,2,1,0:T(8,128)(2,1)S(1)}, u32[]{:S(2)}, u32[]{:S(2)}) %collective-permute-start.23) | collective-permute-done | bytes 200736 | tf_op jit(solution)/shard_map/ppermute | solution.py:362
  502.2 4.2 pass_j.23.h_ref
  506.4 17.0 %pass_j.22.u_ref = bf16[64,64,16,128]{3,2,1,0:T(8,128)(2,1)} custom-call(bf16[3,256,512]{2,1,0:T(8,128)(2,1)} %get-tuple-element.82.w_ref, bf16[64,64,16,128]{3,2,1,0:T(8,128)(2,1)} %pass_i.11.u_ref, bf16[7,64,16,128]{3,2,1,0:T(8,128)(2,1)} %collective-permute-done.21.h_ref), custom_call_target="tpu_custom_call" | custom-call | flops 8589934592 | bytes 33554432 | tf_op jit(solution)/shard_map/pass_j/pallas_call | solution.py:141
  523.4 31.1 %pass_k_mix.11 = (bf16[64,64,16,128]{3,2,1,0:T(8,128)(2,1)}, bf16[64,32,16,128]{3,2,1,0:T(8,128)(2,1)}) custom-call(s32[2]{0:T(128)} %add_convert_fusion.7.flags, bf16[3,256,512]{2,1,0:T(8,128)(2,1)} %get-tuple-element.85.w_ref, bf16[256,256]{1,0:T(8,128)(2,1)} %squeeze.32.m_ref, f32[1,256]{1,0:T(1,128)} %tile.17.b_ref, ...), custom_call_target="tpu_custom_call" | custom-call | flops 12884901888 | bytes 58720256 | tf_op jit(solution)/shard_map/pass_k_mix/pallas_call | solution.py:203
  554.5 16.7 %pass_j.16.u_ref = bf16[64,64,16,128]{3,2,1,0:T(8,128)(2,1)} custom-call(bf16[3,256,512]{2,1,0:T(8,128)(2,1)} %get-tuple-element.82.w_ref, bf16[64,64,16,128]{3,2,1,0:T(8,128)(2,1)} %pass_i.8.u_ref, bf16[7,64,16,128]{3,2,1,0:T(8,128)(2,1)} %collective-permute-done.9.h_ref), custom_call_target="tpu_custom_call" | custom-call | flops 8589934592 | bytes 33554432 | tf_op jit(solution)/shard_map/pass_j/pallas_call | solution.py:141
  571.3 32.5 %leave.2.rest_0_ = bf16[2,32,64,64,64]{4,3,2,1,0:T(8,128)(2,1)} custom-call(bf16[64,64,16,128]{3,2,1,0:T(8,128)(2,1)} %get-tuple-element.32.y_ref), custom_call_target="tpu_custom_call" | custom-call | flops 100000000 | bytes 50331648 | tf_op jit(solution)/shard_map/leave/pallas_call | solution.py:313
  604.4 4.2 pass_j.17.h_ref
  608.7 31.1 %pass_k_mix.8 = (bf16[64,64,16,128]{3,2,1,0:T(8,128)(2,1)}, bf16[64,32,16,128]{3,2,1,0:T(8,128)(2,1)}) custom-call(s32[2]{0:T(128)} %add_convert_fusion.7.flags, bf16[3,256,512]{2,1,0:T(8,128)(2,1)} %get-tuple-element.85.w_ref, bf16[256,256]{1,0:T(8,128)(2,1)} %squeeze.32.m_ref, f32[1,256]{1,0:T(1,128)} %tile.17.b_ref, ...), custom_call_target="tpu_custom_call" | custom-call | flops 12884901888 | bytes 58720256 | tf_op jit(solution)/shard_map/pass_k_mix/pallas_call | solution.py:203
  639.7 32.5 %leave.3 = bf16[2,32,64,64,64]{4,3,2,1,0:T(8,128)(2,1)} custom-call(bf16[64,64,16,128]{3,2,1,0:T(8,128)(2,1)} %get-tuple-element.25.y_ref, bf16[2,32,64,64,64]{4,3,2,1,0:T(8,128)(2,1)} %leave.2.rest_0_), custom_call_target="tpu_custom_call", output_to_operand_aliasing={{}: (1, {})} | custom-call | flops 100000000 | bytes 50331648 | tf_op jit(solution)/shard_map/leave/pallas_call | solution.py:313
  (99 shorter events, 19.0 us)
Async XLA Ops:
  27.6 28.0 %copy-start.11 = (f32[3,32]{1,0:T(4,128)S(1)}, f32[3,32]{1,0:T(4,128)}, u32[]{:S(2)}) copy-start(f32[3,32]{1,0:T(4,128)} %param.7) | copy-start | bytes 1156
  27.6 29.2 %copy-start.9 = (f32[3,3,15]{2,1,0:T(4,128)S(1)}, f32[3,3,15]{2,1,0:T(4,128)}, u32[]{:S(2)}) copy-start(f32[3,3,15]{2,1,0:T(4,128)} %param.5) | copy-start | bytes 1624
  27.6 29.2 %copy-start.8 = (bf16[3,32,32]{2,1,0:T(8,128)(2,1)S(1)}, bf16[3,32,32]{2,1,0:T(8,128)(2,1)}, u32[]{:S(2)}) copy-start(bf16[3,32,32]{2,1,0:T(8,128)(2,1)} %param.6) | copy-start | bytes 18436
  27.6 36.1 %collective-permute-start.12 = (bf16[64,32,16,128]{3,2,1,0:T(8,128)(2,1)}, bf16[64,32,16,128]{3,2,1,0:T(8,128)(2,1)}, u32[]{:S(2)}, u32[]{:S(2)}) collective-permute-start(bf16[64,32,16,128]{3,2,1,0:T(8,128)(2,1)} %get-tuple-element.27), channel_id=1, source_target_pairs={{0,1},{1,0},{2,3},{3,2},{4,5},{5,4},{6,7},{7,6}} | collective-permute-start | bytes 25165832 | tf_op jit(solution)/shard_map/ppermute | solution.py:350
  55.5 45.5 %collective-permute-start = (bf16[64,32,16,128]{3,2,1,0:T(8,128)(2,1)}, bf16[64,32,16,128]{3,2,1,0:T(8,128)(2,1)}, u32[]{:S(2)}, u32[]{:S(2)}) collective-permute-start(bf16[64,32,16,128]{3,2,1,0:T(8,128)(2,1)} %get-tuple-element.20), channel_id=1, source_target_pairs={{0,1},{1,0},{2,3},{3,2},{4,5},{5,4},{6,7},{7,6}} | collective-permute-start | bytes 25165832 | tf_op jit(solution)/shard_map/ppermute | solution.py:350
  85.8 61.8 %collective-permute-start.13 = (bf16[7,64,16,128]{3,2,1,0:T(8,128)(2,1)}, bf16[7,64,16,128]{3,2,1,0:T(8,128)(2,1)}, u32[]{:S(2)}, u32[]{:S(2)}) collective-permute-start(bf16[7,64,16,128]{3,2,1,0:T(8,128)(2,1)} %constant_dynamic-slice_fusion.8), channel_id=1, source_target_pairs={{0,2},{2,0},{1,3},{3,1},{4,6},{6,4},{5,7},{7,5}} | collective-permute-start | bytes 5505032 | tf_op jit(solution)/shard_map/ppermute | solution.py:360
  91.9 51.5 %collective-permute-start.14 = (bf16[64,7,16,128]{3,2,1,0:T(8,128)(2,1)}, bf16[64,7,16,128]{3,2,1,0:T(8,128)(2,1)}, u32[]{:S(2)}, u32[]{:S(2)}) collective-permute-start(bf16[64,7,16,128]{3,2,1,0:T(8,128)(2,1)} %constant_dynamic-slice_fusion.7), channel_id=1, source_target_pairs={{0,4},{4,0},{1,5},{5,1},{2,6},{6,2},{3,7},{7,3}} | collective-permute-start | bytes 5505032 | tf_op jit(solution)/shard_map/ppermute | solution.py:361
  96.1 2.5 copy-start
  101.0 34.5 %collective-permute-start.15 = (bf16[7,7,16,128]{3,2,1,0:T(8,128)(2,1)S(1)}, bf16[7,7,16,128]{3,2,1,0:T(8,128)(2,1)S(1)}, u32[]{:S(2)}, u32[]{:S(2)}) collective-permute-start(bf16[7,7,16,128]{3,2,1,0:T(8,128)(2,1)S(1)} %constant_dynamic-slice_fusion.6), channel_id=1, source_target_pairs={{0,6},{2,4},{4,2},{6,0},{1,7},{3,5},{5,3},{7,1}} | collective-permute-start | bytes 602120 | tf_op jit(solution)/shard_map/ppermute | solution.py:362
  124.3 88.1 %collective-permute-start.3 = (bf16[7,7,16,128]{3,2,1,0:T(8,128)(2,1)S(1)}, bf16[7,7,16,128]{3,2,1,0:T(8,128)(2,1)S(1)}, u32[]{:S(2)}, u32[]{:S(2)}) collective-permute-start(bf16[7,7,16,128]{3,2,1,0:T(8,128)(2,1)S(1)} %constant_dynamic-slice_fusion.15), channel_id=1, source_target_pairs={{0,6},{2,4},{4,2},{6,0},{1,7},{3,5},{5,3},{7,1}} | collective-permute-start | bytes 602120 | tf_op jit(solution)/shard_map/ppermute | solution.py:362
  127.2 68.4 %collective-permute-start.1 = (bf16[7,64,16,128]{3,2,1,0:T(8,128)(2,1)}, bf16[7,64,16,128]{3,2,1,0:T(8,128)(2,1)}, u32[]{:S(2)}, u32[]{:S(2)}) collective-permute-start(bf16[7,64,16,128]{3,2,1,0:T(8,128)(2,1)} %constant_dynamic-slice_fusion.17), channel_id=1, source_target_pairs={{0,2},{2,0},{1,3},{3,1},{4,6},{6,4},{5,7},{7,5}} | collective-permute-start | bytes 5505032 | tf_op jit(solution)/shard_map/ppermute | solution.py:360
  135.5 7.9 %copy-start.6 = (bf16[7,7,16,128]{3,2,1,0:T(8,128)(2,1)}, bf16[7,7,16,128]{3,2,1,0:T(8,128)(2,1)S(1)}, u32[]{:S(2)}) copy-start(bf16[7,7,16,128]{3,2,1,0:T(8,128)(2,1)S(1)} %collective-permute-done.15.h_ref) | copy-start | bytes 602116
  135.5 76.9 %collective-permute-start.2 = (bf16[64,7,16,128]{3,2,1,0:T(8,128)(2,1)S(1)}, bf16[64,7,16,128]{3,2,1,0:T(8,128)(2,1)}, u32[]{:S(2)}, u32[]{:S(2)}) collective-permute-start(bf16[64,7,16,128]{3,2,1,0:T(8,128)(2,1)S(1)} %constant_dynamic-slice_fusion.16), channel_id=1, source_target_pairs={{0,4},{4,0},{1,5},{5,1},{2,6},{6,2},{3,7},{7,3}} | collective-permute-start | bytes 5505032 | tf_op jit(solution)/shard_map/ppermute | solution.py:361
  195.7 53.3 %collective-permute-start.16 = (bf16[64,32,16,128]{3,2,1,0:T(8,128)(2,1)}, bf16[64,32,16,128]{3,2,1,0:T(8,128)(2,1)}, u32[]{:S(2)}, u32[]{:S(2)}) collective-permute-start(bf16[64,32,16,128]{3,2,1,0:T(8,128)(2,1)} %get-tuple-element.29), channel_id=1, source_target_pairs={{0,1},{1,0},{2,3},{3,2},{4,5},{5,4},{6,7},{7,6}} | collective-permute-start | bytes 25165832 | tf_op jit(solution)/shard_map/ppermute | solution.py:370
  212.4 0.7 copy-start.3
  248.5 30.6 %collective-permute-start.4 = (bf16[64,32,16,128]{3,2,1,0:T(8,128)(2,1)}, bf16[64,32,16,128]{3,2,1,0:T(8,128)(2,1)}, u32[]{:S(2)}, u32[]{:S(2)}) collective-permute-start(bf16[64,32,16,128]{3,2,1,0:T(8,128)(2,1)} %get-tuple-element.22), channel_id=1, source_target_pairs={{0,1},{1,0},{2,3},{3,2},{4,5},{5,4},{6,7},{7,6}} | collective-permute-start | bytes 25165832 | tf_op jit(solution)/shard_map/ppermute | solution.py:370
  271.2 52.0 %collective-permute-start.18 = (bf16[64,7,16,128]{3,2,1,0:T(8,128)(2,1)}, bf16[64,7,16,128]{3,2,1,0:T(8,128)(2,1)}, u32[]{:S(2)}, u32[]{:S(2)}) collective-permute-start(bf16[64,7,16,128]{3,2,1,0:T(8,128)(2,1)} %constant_dynamic-slice_fusion.4), channel_id=1, source_target_pairs={{0,4},{4,0},{1,5},{5,1},{2,6},{6,2},{3,7},{7,3}} | collective-permute-start | bytes 5505032 | tf_op jit(solution)/shard_map/ppermute | solution.py:361
  274.5 52.9 %collective-permute-start.17 = (bf16[7,64,16,128]{3,2,1,0:T(8,128)(2,1)S(1)}, bf16[7,64,16,128]{3,2,1,0:T(8,128)(2,1)}, u32[]{:S(2)}, u32[]{:S(2)}) collective-permute-start(bf16[7,64,16,128]{3,2,1,0:T(8,128)(2,1)S(1)} %constant_dynamic-slice_fusion.5), channel_id=1, source_target_pairs={{0,2},{2,0},{1,3},{3,1},{4,6},{6,4},{5,7},{7,5}} | collective-permute-start | bytes 5505032 | tf_op jit(solution)/shard_map/ppermute | solution.py:360
  277.6 44.0 %collective-permute-start.19 = (bf16[7,7,16,128]{3,2,1,0:T(8,128)(2,1)S(1)}, bf16[7,7,16,128]{3,2,1,0:T(8,128)(2,1)S(1)}, u32[]{:S(2)}, u32[]{:S(2)}) collective-permute-start(bf16[7,7,16,128]{3,2,1,0:T(8,128)(2,1)S(1)} %constant_dynamic-slice_fusion.3), channel_id=1, source_target_pairs={{0,6},{2,4},{4,2},{6,0},{1,7},{3,5},{5,3},{7,1}} | collective-permute-start | bytes 602120 | tf_op jit(solution)/shard_map/ppermute | solution.py:362
  302.2 90.0 %collective-permute-start.7 = (bf16[7,7,16,128]{3,2,1,0:T(8,128)(2,1)S(1)}, bf16[7,7,16,128]{3,2,1,0:T(8,128)(2,1)S(1)}, u32[]{:S(2)}, u32[]{:S(2)}) collective-permute-start(bf16[7,7,16,128]{3,2,1,0:T(8,128)(2,1)S(1)} %constant_dynamic-slice_fusion.12), channel_id=1, source_target_pairs={{0,6},{2,4},{4,2},{6,0},{1,7},{3,5},{5,3},{7,1}} | collective-permute-start | bytes 602120 | tf_op jit(solution)/shard_map/ppermute | solution.py:362
  303.7 71.8 %collective-permute-start.5 = (bf16[7,64,16,128]{3,2,1,0:T(8,128)(2,1)}, bf16[7,64,16,128]{3,2,1,0:T(8,128)(2,1)}, u32[]{:S(2)}, u32[]{:S(2)}) collective-permute-start(bf16[7,64,16,128]{3,2,1,0:T(8,128)(2,1)} %constant_dynamic-slice_fusion.14), channel_id=1, source_target_pairs={{0,2},{2,0},{1,3},{3,1},{4,6},{6,4},{5,7},{7,5}} | collective-permute-start | bytes 5505032 | tf_op jit(solution)/shard_map/ppermute | solution.py:360
  321.6 1.5 copy-start.7
  321.6 70.6 %collective-permute-start.6 = (bf16[64,7,16,128]{3,2,1,0:T(8,128)(2,1)}, bf16[64,7,16,128]{3,2,1,0:T(8,128)(2,1)}, u32[]{:S(2)}, u32[]{:S(2)}) collective-permute-start(bf16[64,7,16,128]{3,2,1,0:T(8,128)(2,1)} %constant_dynamic-slice_fusion.13), channel_id=1, source_target_pairs={{0,4},{4,0},{1,5},{5,1},{2,6},{6,2},{3,7},{7,3}} | collective-permute-start | bytes 5505032 | tf_op jit(solution)/shard_map/ppermute | solution.py:361
  375.5 53.2 %collective-permute-start.20 = (bf16[64,32,16,128]{3,2,1,0:T(8,128)(2,1)}, bf16[64,32,16,128]{3,2,1,0:T(8,128)(2,1)}, u32[]{:S(2)}, u32[]{:S(2)}) collective-permute-start(bf16[64,32,16,128]{3,2,1,0:T(8,128)(2,1)} %get-tuple-element.31), channel_id=1, source_target_pairs={{0,1},{1,0},{2,3},{3,2},{4,5},{5,4},{6,7},{7,6}} | collective-permute-start | bytes 25165832 | tf_op jit(solution)/shard_map/ppermute | solution.py:370
  392.3 0.7 copy-start.4
  428.2 30.7 %collective-permute-start.8 = (bf16[64,32,16,128]{3,2,1,0:T(8,128)(2,1)}, bf16[64,32,16,128]{3,2,1,0:T(8,128)(2,1)}, u32[]{:S(2)}, u32[]{:S(2)}) collective-permute-start(bf16[64,32,16,128]{3,2,1,0:T(8,128)(2,1)} %get-tuple-element.24), channel_id=1, source_target_pairs={{0,1},{1,0},{2,3},{3,2},{4,5},{5,4},{6,7},{7,6}} | collective-permute-start | bytes 25165832 | tf_op jit(solution)/shard_map/ppermute | solution.py:370
  447.9 6.2 copy-start.10
  447.9 6.8 %copy-start.1 = (bf16[1,8,32,8,32]{4,3,2,1,0:T(8,128)(2,1)S(1)}, bf16[1,8,32,8,32]{4,3,2,1,0:T(8,128)(2,1)}, u32[]{:S(2)}) copy-start(bf16[1,8,32,8,32]{4,3,2,1,0:T(8,128)(2,1)} %get-tuple-element.88) | copy-start | bytes 393220
  451.0 51.2 %collective-permute-start.22 = (bf16[64,7,16,128]{3,2,1,0:T(8,128)(2,1)}, bf16[64,7,16,128]{3,2,1,0:T(8,128)(2,1)}, u32[]{:S(2)}, u32[]{:S(2)}) collective-permute-start(bf16[64,7,16,128]{3,2,1,0:T(8,128)(2,1)} %constant_dynamic-slice_fusion.1), channel_id=1, source_target_pairs={{0,4},{4,0},{1,5},{5,1},{2,6},{6,2},{3,7},{7,3}} | collective-permute-start | bytes 5505032 | tf_op jit(solution)/shard_map/ppermute | solution.py:361
  453.5 52.9 %collective-permute-start.21 = (bf16[7,64,16,128]{3,2,1,0:T(8,128)(2,1)S(1)}, bf16[7,64,16,128]{3,2,1,0:T(8,128)(2,1)}, u32[]{:S(2)}, u32[]{:S(2)}) collective-permute-start(bf16[7,64,16,128]{3,2,1,0:T(8,128)(2,1)S(1)} %constant_dynamic-slice_fusion.2), channel_id=1, source_target_pairs={{0,2},{2,0},{1,3},{3,1},{4,6},{6,4},{5,7},{7,5}} | collective-permute-start | bytes 5505032 | tf_op jit(solution)/shard_map/ppermute | solution.py:360
  456.6 44.9 %collective-permute-start.23 = (bf16[7,7,16,128]{3,2,1,0:T(8,128)(2,1)S(1)}, bf16[7,7,16,128]{3,2,1,0:T(8,128)(2,1)S(1)}, u32[]{:S(2)}, u32[]{:S(2)}) collective-permute-start(bf16[7,7,16,128]{3,2,1,0:T(8,128)(2,1)S(1)} %constant_dynamic-slice_fusion), channel_id=1, source_target_pairs={{0,6},{2,4},{4,2},{6,0},{1,7},{3,5},{5,3},{7,1}} | collective-permute-start | bytes 602120 | tf_op jit(solution)/shard_map/ppermute | solution.py:362
  482.0 121.7 %collective-permute-start.11 = (bf16[7,7,16,128]{3,2,1,0:T(8,128)(2,1)S(1)}, bf16[7,7,16,128]{3,2,1,0:T(8,128)(2,1)S(1)}, u32[]{:S(2)}, u32[]{:S(2)}) collective-permute-start(bf16[7,7,16,128]{3,2,1,0:T(8,128)(2,1)S(1)} %constant_dynamic-slice_fusion.9), channel_id=1, source_target_pairs={{0,6},{2,4},{4,2},{6,0},{1,7},{3,5},{5,3},{7,1}} | collective-permute-start | bytes 602120 | tf_op jit(solution)/shard_map/ppermute | solution.py:362
  482.7 71.8 %collective-permute-start.9 = (bf16[7,64,16,128]{3,2,1,0:T(8,128)(2,1)}, bf16[7,64,16,128]{3,2,1,0:T(8,128)(2,1)}, u32[]{:S(2)}, u32[]{:S(2)}) collective-permute-start(bf16[7,64,16,128]{3,2,1,0:T(8,128)(2,1)} %constant_dynamic-slice_fusion.11), channel_id=1, source_target_pairs={{0,2},{2,0},{1,3},{3,1},{4,6},{6,4},{5,7},{7,5}} | collective-permute-start | bytes 5505032 | tf_op jit(solution)/shard_map/ppermute | solution.py:360
  501.5 0.7 copy-start.5
  501.5 102.3 %collective-permute-start.10 = (bf16[64,7,16,128]{3,2,1,0:T(8,128)(2,1)}, bf16[64,7,16,128]{3,2,1,0:T(8,128)(2,1)}, u32[]{:S(2)}, u32[]{:S(2)}) collective-permute-start(bf16[64,7,16,128]{3,2,1,0:T(8,128)(2,1)} %constant_dynamic-slice_fusion.10), channel_id=1, source_target_pairs={{0,4},{4,0},{1,5},{5,1},{2,6},{6,2},{3,7},{7,3}} | collective-permute-start | bytes 5505032 | tf_op jit(solution)/shard_map/ppermute | solution.py:361
  603.8 0.7 copy-start.2

commit v2 on v1

v2 whole, which is shorter than its diff:
```python
import jax
import jax.numpy as jnp
from jax import lax
from jax.experimental import pallas as pl
from jax.experimental.pallas import tpu as pltpu
from jax.sharding import PartitionSpec as P


SWAP = [(0, 1), (1, 0)]
DIAG = [(0, 3), (1, 2), (2, 1), (3, 0)]
SUB = 16
GROUPS = 4
LANES = 128
PARAMS = pltpu.CompilerParams(vmem_limit_bytes=60 * 1024 * 1024)


def band(taps, offset):
    out = jnp.zeros(taps.shape[:-1] + offset.shape, jnp.float32)
    for t in range(taps.shape[-1]):
        out = out + jnp.where(offset == t, taps[..., t].reshape(taps.shape[:-1] + (1,) * offset.ndim), 0.0)
    return out


def pass_i_weights(taps):
    half = (taps.shape[-1] - 1) // 2
    row = lax.broadcasted_iota(jnp.int32, (8 * SUB, 16 * SUB), 0)
    col = lax.broadcasted_iota(jnp.int32, (8 * SUB, 16 * SUB), 1)
    own, up = col < 8 * SUB, col < 12 * SUB
    point = jnp.where(own, col // SUB, (col % (4 * SUB)) // 8)
    source = jnp.where(own, col % SUB, jnp.where(up, SUB + col % 8, col % 8 - 8))
    offset = jnp.where(row // SUB == point, source - row % SUB + half, -1)
    return band(taps, offset).astype(jnp.bfloat16)


def pass_jk_weights(taps, side):
    half = (taps.shape[-1] - 1) // 2
    shape = (3, SUB, 2 * SUB)
    variant = lax.broadcasted_iota(jnp.int32, shape, 0)
    out = lax.broadcasted_iota(jnp.int32, shape, 1)
    slot = lax.broadcasted_iota(jnp.int32, shape, 2)
    missing_low = (variant == 0) & (slot < half) & (side == 0)
    missing_high = (variant == 2) & (slot >= SUB + half) & (side == 1)
    small = band(taps, jnp.where(missing_low | missing_high, -1, slot - out)).astype(jnp.bfloat16)
    rows, cols = SUB * SUB, 2 * SUB * SUB
    spread_rows = (jnp.arange(rows)[:, None] // SUB == jnp.arange(SUB)[None, :]).astype(jnp.bfloat16)
    spread_cols = (jnp.arange(2 * SUB)[:, None] == jnp.arange(cols)[None, :] // SUB).astype(jnp.bfloat16)
    same = jnp.arange(rows)[:, None] % SUB == jnp.arange(cols)[None, :] % SUB
    tall = jnp.einsum('ra,lvas->lvrs', spread_rows, small, preferred_element_type=jnp.float32).astype(jnp.bfloat16)
    wide = jnp.einsum('lvrs,sc->lvrc', tall, spread_cols, preferred_element_type=jnp.float32)
    return jnp.where(same, wide, 0.0).astype(jnp.bfloat16)


WIDTH = LANES // GROUPS


def gather_faces(pairs, high):
    lane = lax.broadcasted_iota(jnp.int32, (SUB, LANES), 1)
    out = None
    for q in range(GROUPS):
        moved = pltpu.roll(pairs[q], WIDTH * lax.rem(q + high, GROUPS), 1)
        out = moved if out is None else jnp.where(lane // WIDTH == q, moved, out)
    return out


def pass_i_kernel(flags, w_ref, y_ref, n_ref, o_ref, f_ref):
    jb, kk = y_ref.shape[0], y_ref.shape[1]
    lane = lax.broadcasted_iota(jnp.int32, (1, SUB, LANES), 2)
    has_up, has_low = flags[0] > 0, flags[1] > 0
    weights = w_ref[...]
    zero = jnp.zeros((4, SUB, LANES), jnp.bfloat16)

    def columns(j, k):
        own = y_ref[j, pl.ds(k, 8)]
        full = own.astype(jnp.float32)
        tile = n_ref[j, k // 8]
        peer = jnp.stack([pltpu.roll(tile, WIDTH * lax.rem(2 * GROUPS - q - flags[0], GROUPS), 1) for q in range(GROUPS)])
        lo = full[:, :8].reshape(4, SUB, LANES).astype(jnp.bfloat16)
        hi = full[:, 8:].reshape(4, SUB, LANES).astype(jnp.bfloat16)
        up = jnp.where(lane >= LANES - WIDTH, jnp.where(has_up, peer, zero), pltpu.roll(lo, LANES - WIDTH, 2))
        low = jnp.where(lane < WIDTH, jnp.where(has_low, peer, zero), pltpu.roll(hi, WIDTH, 2))
        return jnp.concatenate([own.reshape(8 * SUB, LANES), up.reshape(4 * SUB, LANES), low.reshape(4 * SUB, LANES)], axis=0)

    group = 4

    def step(q, carry):
        for r in range(group):
            j = q * group + r
            stacks = [jnp.concatenate([columns(j, k), columns(j, k + 8)], axis=1) for k in range(0, kk, 16)]
            for stack, k in zip(stacks, range(0, kk, 16)):
                out = jnp.dot(weights, stack, preferred_element_type=jnp.float32).astype(jnp.bfloat16)
                o_ref[j, pl.ds(k, 8)] = out[:, :LANES].reshape(8, SUB, LANES)
                o_ref[j, pl.ds(k + 8, 8)] = out[:, LANES:].reshape(8, SUB, LANES)
        for r in range(group):
            j = q * group + r
            f_ref[j] = o_ref[j, pl.ds(flags[2], f_ref.shape[1])]
        return carry

    lax.fori_loop(0, jb // group, step, 0)


def pass_i(flags, weights, y, peer, half, block=8):
    nj, nk = y.shape[0], y.shape[1]
    return pl.pallas_call(
        pass_i_kernel,
        out_shape=(jax.ShapeDtypeStruct(y.shape, y.dtype), jax.ShapeDtypeStruct((nj, half, SUB, LANES), y.dtype)),
        grid=(nj // block,),
        in_specs=[
            pl.BlockSpec(memory_space=pltpu.SMEM),
            pl.BlockSpec(weights.shape, lambda b: (0, 0)),
            pl.BlockSpec((block, nk, SUB, LANES), lambda b: (b, 0, 0, 0)),
            pl.BlockSpec((block, nk // 8, SUB, LANES), lambda b: (b, 0, 0, 0)),
        ],
        out_specs=(
            pl.BlockSpec((block, nk, SUB, LANES), lambda b: (b, 0, 0, 0)),
            pl.BlockSpec((block, half, SUB, LANES), lambda b: (b, 0, 0, 0)),
        ),
        compiler_params=PARAMS,
        cost_estimate=pl.CostEstimate(flops=nj * nk * 2 * SUB * 32 * 8 * LANES, bytes_accessed=nj * nk * 10240, transcendentals=0),
        name="pass_i",
    )(flags, weights, y, peer)


def slots(part, own, halo, n, half):
    lo, hi = part * SUB - half, part * SUB - half + 2 * SUB
    pieces = []
    if lo < 0:
        pieces.append(halo(slice(0, -lo)))
    pieces.append(own(slice(max(lo, 0), min(hi, n))))
    if hi > n:
        pieces.append(halo(slice(0, half)))
        if hi - n > half:
            pieces.append(halo(slice(0, hi - n - half)))
    stack = jnp.concatenate(pieces, axis=0) if len(pieces) > 1 else pieces[0]
    return stack.reshape(2 * SUB * SUB, LANES)


def half_gelu(h):
    scale = 0.7978845608028654
    return h + h * jnp.tanh(h * (2.0 * scale + (8.0 * scale * 0.044715) * (h * h)))


def filter_mix_kernel(flags, wj_ref, wk_ref, m_ref, b_ref, u_ref, jh_ref, kh_ref, ch_ref, y_ref, o_ref, f_ref, u2, ahead_a, ahead_b):
    nj, kb = u_ref.shape[0], u_ref.shape[1]
    jb, nk = y_ref.shape[0], y_ref.shape[1]
    half = jh_ref.shape[0]
    first = nk // kb
    now = pl.program_id(0)
    send_high = flags[0] > 0
    rows = 128
    tiles = rows // SUB

    def variant(part, parts):
        return 0 if part == 0 else (2 if part == parts - 1 else 1)

    def along_j(src, halo, pairs, at):
        parts = nj // SUB
        for k0, k1 in pairs:
            for part in range(parts):
                sides = [slots(part, lambda s, k=k: src[s, k], lambda s, k=k: halo[s, k], nj, half) for k in (k0, k1)]
                out = jnp.dot(wj_ref[variant(part, parts)], jnp.concatenate(sides, axis=1), preferred_element_type=jnp.float32).astype(jnp.bfloat16)
                js = slice(part * SUB, (part + 1) * SUB)
                u2[js, at + k0] = out[:, :LANES].reshape(SUB, SUB, LANES)
                u2[js, at + k1] = out[:, LANES:].reshape(SUB, SUB, LANES)

    def along_k(j0, part):
        parts = nk // SUB
        sides = [slots(part, lambda s, j=j: u2[j, s], lambda s, j=j: u2[j, slice(nk + s.start, nk + s.stop)], nk, half) for j in (j0, j0 + 1)]
        return jnp.dot(wk_ref[variant(part, parts)], jnp.concatenate(sides, axis=1), preferred_element_type=jnp.float32).astype(jnp.bfloat16)

    def finish(j0, part, ready):
        for r in range(SUB * SUB // rows):
            h = jnp.dot(ready[part, r * rows:(r + 1) * rows], m_ref[...], preferred_element_type=jnp.float32) + b_ref[...]
            act = half_gelu(h)
            k0 = part * SUB + r * tiles
            for side in range(2):
                new = y_ref[j0 + side, k0:k0 + tiles].astype(jnp.float32) + act[:, side * LANES:(side + 1) * LANES].reshape(tiles, SUB, LANES)
                o_ref[j0 + side, k0:k0 + tiles] = new.astype(jnp.bfloat16)
                face = jnp.where(send_high, new[:, 8:], new[:, :8])
                f_ref[j0 + side, k0 // 8] = gather_faces(face.reshape(tiles // 2, SUB, LANES).astype(jnp.bfloat16), flags[0])

    @pl.when(now == 0)
    def _():
        along_j(kh_ref, ch_ref, [(2 * q, min(2 * q + 1, half - 1)) for q in range((half + 1) // 2)], nk)

    @pl.when(now < first)
    def _():
        def some(q, carry):
            along_j(u_ref, jh_ref, [(4 * q + 2 * r, 4 * q + 2 * r + 1) for r in range(2)], now * kb)
            return carry

        lax.fori_loop(0, kb // 4, some, 0)

    @pl.when(now == first - 1)
    def _():
        for part in range(nk // SUB):
            ahead_a[part] = along_k(0, part)

    @pl.when(now >= first)
    def _():
        base = (now - first) * jb
        for part in range(nk // SUB):
            ahead_b[part] = along_k(base + 2, part)
            finish(0, part, ahead_a)
        following = jnp.minimum(base + 4, nj - 2)
        for part in range(nk // SUB):
            ahead_a[part] = along_k(following, part)
            finish(2, part, ahead_b)


def filter_mix(flags, w_j, w_k, mix, bias, u, j_halo, k_halo, corner, y, kb=16):
    nj, nk = u.shape[0], u.shape[1]
    half = j_halo.shape[0]
    jb = 4
    first = nk // kb
    wide = lambda b: (0, 0, 0, 0)
    columns = lambda b: (0, jnp.minimum(b, first - 1), 0, 0)
    planes = lambda b: (jnp.maximum(b - first, 0), 0, 0, 0)
    return pl.pallas_call(
        filter_mix_kernel,
        out_shape=(jax.ShapeDtypeStruct(u.shape, u.dtype), jax.ShapeDtypeStruct((nj, nk // 8, SUB, LANES), u.dtype)),
        grid=(first + nj // jb,),
        in_specs=[
            pl.BlockSpec(memory_space=pltpu.SMEM),
            pl.BlockSpec(w_j.shape, lambda b: (0, 0, 0)),
            pl.BlockSpec(w_k.shape, lambda b: (0, 0, 0)),
            pl.BlockSpec(mix.shape, lambda b: (0, 0)),
            pl.BlockSpec(bias.shape, lambda b: (0, 0)),
            pl.BlockSpec((nj, kb, SUB, LANES), columns),
            pl.BlockSpec((half, kb, SUB, LANES), columns),
            pl.BlockSpec((nj, half, SUB, LANES), wide),
            pl.BlockSpec((half, half, SUB, LANES), wide),
            pl.BlockSpec((jb, nk, SUB, LANES), planes),
        ],
        out_specs=(
            pl.BlockSpec((jb, nk, SUB, LANES), planes),
            pl.BlockSpec((jb, nk // 8, SUB, LANES), planes),
        ),
        scratch_shapes=[
            pltpu.VMEM((nj, nk + 8, SUB, LANES), u.dtype),
            pltpu.VMEM((nk // SUB, SUB * SUB, 2 * LANES), u.dtype),
            pltpu.VMEM((nk // SUB, SUB * SUB, 2 * LANES), u.dtype),
        ],
        compiler_params=PARAMS,
        cost_estimate=pl.CostEstimate(flops=nj * nk * 2 * SUB * (512 * 2 + 256) * LANES, bytes_accessed=nj * nk * 14336, transcendentals=nj * nk * SUB * LANES),
        name="filter_mix",
    )(flags, w_j, w_k, mix, bias, u, j_halo, k_halo, corner, y)


PITCH = 24


def enter_kernel(flags, x_ref, o_ref, f_ref, s1, s2):
    nc, nk = x_ref.shape[1], x_ref.shape[4]
    rows = GROUPS * nc
    send_high = flags[0] > 0

    def pair(p, carry):
        for g in range(GROUPS):
            for c in range(nc):
                i0 = g * SUB + 2 * p
                tile = jnp.concatenate([x_ref[0, c, i0], x_ref[0, c, i0 + 1]], axis=1)
                s1[(g * nc + c) * PITCH:(g * nc + c) * PITCH + SUB, :] = tile.astype(jnp.float32)
        for j in range(SUB):
            flip = s1[pl.ds(j, rows, stride=PITCH), :].T
            base = j * nk * PITCH + 2 * p
            s2[pl.ds(base, nk, stride=PITCH), :] = flip[:nk]
            s2[pl.ds(base + 1, nk, stride=PITCH), :] = flip[nk:]
        return carry

    lax.fori_loop(0, SUB // 2, pair, 0)

    def emit(j, carry):
        base = pl.multiple_of(j * (nk * PITCH), 8)
        for k in range(0, nk, 8):
            faces = []
            for side in range(8):
                tile = s2[pl.ds(base + (k + side) * PITCH, SUB), :]
                o_ref[j, k + side] = tile.astype(jnp.bfloat16)
                faces.append(jnp.where(send_high, tile[8:], tile[:8]))
            pairs = [jnp.concatenate(faces[2 * q:2 * q + 2], axis=0).astype(jnp.bfloat16) for q in range(GROUPS)]
            f_ref[j, k // 8] = gather_faces(pairs, flags[0])
        return carry

    lax.fori_loop(0, SUB, emit, 0)


def enter(flags, vol, v):
    _, nc, ni, nj, nk = vol.shape
    return pl.pallas_call(
        enter_kernel,
        out_shape=(jax.ShapeDtypeStruct((nj, nk, SUB, LANES), vol.dtype), jax.ShapeDtypeStruct((nj, nk // 8, SUB, LANES), vol.dtype)),
        grid=(nj // SUB,),
        in_specs=[pl.BlockSpec(memory_space=pltpu.SMEM), pl.BlockSpec((1, nc, ni, SUB, nk), lambda b: (v, 0, 0, b, 0))],
        out_specs=(
            pl.BlockSpec((SUB, nk, SUB, LANES), lambda b: (b, 0, 0, 0)),
            pl.BlockSpec((SUB, nk // 8, SUB, LANES), lambda b: (b, 0, 0, 0)),
        ),
        scratch_shapes=[pltpu.VMEM((GROUPS * nc * PITCH, 2 * nk), jnp.float32), pltpu.VMEM((SUB * nk * PITCH, LANES), jnp.float32)],
        compiler_params=PARAMS,
        cost_estimate=pl.CostEstimate(flops=10**8, bytes_accessed=nj * nk * 12288, transcendentals=0),
        name="enter",
    )(flags, vol)


def leave_kernel(y_ref, *rest):
    o_ref, s1, s2 = rest[-3:]
    nc, nk = o_ref.shape[1], o_ref.shape[4]
    rows = GROUPS * nc

    def take(j, carry):
        base = pl.multiple_of(j * (nk * PITCH), 8)
        for k in range(nk):
            s2[pl.ds(base + k * PITCH, SUB), :] = y_ref[j, k].astype(jnp.float32)
        return carry

    lax.fori_loop(0, SUB, take, 0)

    def pair(p, carry):
        for j in range(SUB):
            base = j * nk * PITCH + 2 * p
            both = jnp.concatenate([s2[pl.ds(base, nk, stride=PITCH), :], s2[pl.ds(base + 1, nk, stride=PITCH), :]], axis=0)
            s1[pl.ds(j, rows, stride=PITCH), :] = both.T
        for g in range(GROUPS):
            for c in range(nc):
                i0 = g * SUB + 2 * p
                tile = s1[(g * nc + c) * PITCH:(g * nc + c) * PITCH + SUB, :].astype(jnp.bfloat16)
                o_ref[0, c, i0] = tile[:, :nk]
                o_ref[0, c, i0 + 1] = tile[:, nk:]
        return carry

    lax.fori_loop(0, SUB // 2, pair, 0)


def leave(y, v, shape, previous):
    _, nc, ni, nj, nk = shape
    extra = [] if previous is None else [previous]
    return pl.pallas_call(
        leave_kernel,
        out_shape=jax.ShapeDtypeStruct(shape, y.dtype),
        grid=(nj // SUB,),
        in_specs=[pl.BlockSpec((SUB, nk, SUB, LANES), lambda b: (b, 0, 0, 0))] + [pl.BlockSpec(memory_space=pl.ANY)] * len(extra),
        out_specs=pl.BlockSpec((1, nc, ni, SUB, nk), lambda b: (v, 0, 0, b, 0)),
        scratch_shapes=[pltpu.VMEM((GROUPS * nc * PITCH, 2 * nk), jnp.float32), pltpu.VMEM((SUB * nk * PITCH, LANES), jnp.float32)],
        input_output_aliases={1: 0} if extra else {},
        compiler_params=PARAMS,
        cost_estimate=pl.CostEstimate(flops=10**8, bytes_accessed=nj * nk * 12288, transcendentals=0),
        name="leave",
    )(y, *extra)


def solution(mesh):
    vol_spec = P('dp', None, 'px', 'py', 'pz')

    def local_layers(vol_block, filter_taps, mix_weight, mix_bias):
        nv, _, _, nj, nk = vol_block.shape
        layers = filter_taps.shape[0]
        half = (filter_taps.shape[2] - 1) // 2
        px, py, pz = lax.axis_index('px'), lax.axis_index('py'), lax.axis_index('pz')
        taps = filter_taps.astype(jnp.bfloat16).astype(jnp.float32)
        w_i = pass_i_weights(taps[:, 0])
        w_j = pass_jk_weights(taps[:, 1], py)
        w_k = pass_jk_weights(taps[:, 2], pz)
        eye = jnp.eye(2 * GROUPS, dtype=jnp.bfloat16)
        mix = (eye[None, :, None, :, None] * (0.5 * mix_weight)[:, None, :, None, :]).reshape(layers, 2 * LANES, 2 * LANES)
        bias = jnp.tile(0.5 * mix_bias, (1, 2 * GROUPS)).reshape(layers, 1, 2 * LANES)
        j_at = jnp.where(py == 0, nj - half, 0)
        k_at = jnp.where(pz == 0, nk - half, 0)
        flags_x = jnp.stack([px == 0, px == 1, k_at]).astype(jnp.int32)

        last = [mix]

        def after(value):
            value, _ = lax.optimization_barrier((value, last[0]))
            return value

        def first_half(layer, y, peer):
            u1, k_face = pass_i(flags_x, w_i[layer], after(y), peer, half)
            last[0] = k_face
            j_face = lax.dynamic_slice_in_dim(u1, j_at, half, axis=0)
            corner = lax.dynamic_slice_in_dim(k_face, j_at, half, axis=0)
            j_halo = lax.ppermute(j_face, 'py', SWAP)
            k_halo = lax.ppermute(k_face, 'pz', SWAP)
            corner = lax.ppermute(corner, ('pz', 'py'), DIAG)
            halos = (j_halo, k_halo, corner)
            return u1, halos

        def second_half(layer, y, u1, halos):
            u1 = after(u1)
            y, face = filter_mix(flags_x, w_j[layer], w_k[layer], mix[layer], bias[layer], u1, *halos, y)
            last[0] = face
            return y, lax.ppermute(face, 'px', SWAP) if layer + 1 < layers else None

        def begin(v):
            vol = after(vol_block)
            y, face = enter(flags_x, vol, v)
            last[0] = face
            return y, lax.ppermute(face, 'px', SWAP)

        state = [None] * nv
        firsts = [None] * nv
        for v in range(nv):
            state[v], peer = begin(v)
            firsts[v] = first_half(0, state[v], peer)
        out = None
        for layer in range(layers):
            for v in range(nv):
                state[v], peer = second_half(layer, state[v], *firsts[v])
                if layer + 1 < layers:
                    firsts[v] = first_half(layer + 1, state[v], peer)
                else:
                    out = leave(after(state[v]), v, vol_block.shape, out)
                    last[0] = out
        return out

    return jax.shard_map(local_layers, mesh=mesh, in_specs=(vol_spec, P(), P(), P()), out_specs=vol_spec, check_vma=False)
```

time: 684 us -> 673 us (0.984)
  waiting for transfers between devices: 41.4 us -> 102 us
  Pallas kernels: 547 us -> 488 us
  local copies, waits for them, and re-layouts: 53.2 us -> 45.2 us
    pallas_call x24 -> x12, Pallas kernels: 428 us -> 361 us  [the longest x6 250 us: filter_mix(): pl.pallas_call(filter_mix_kernel, out_shape=(jax.ShapeDtypeStruct(u.shape...]
    ppermute x24, waiting for transfers between devices: 41.4 us -> 102 us  [the longest x6 96.9 us: first_half(): corner = lax.ppermute(corner, ('pz', 'py'), DIAG)]
    dynamic_slice x18 -> x12, local copies, waits for them, and re-layouts: 39 us -> 23 us  [the longest x6 17.2 us: first_half(): j_face = lax.dynamic_slice_in_dim(u1, j_at, half, axis=0)]
    unnamed x26 -> x38, local copies, waits for them, and re-layouts: 3.1 us -> 10.5 us
    pallas_call x2, Pallas kernels: 54 us -> 61.3 us  [enter(): pl.pallas_call(enter_kernel, out_shape=(jax.ShapeDtypeStruct((nj, nk, SUB...]
  transfers between devices with their start and end apart: 24 -> 24, of which waited for: 4 -> 9; matrix products, arithmetic and copies ran while one was open for 8% -> 7% of each run, Pallas kernels for 67% -> 25%
where the time goes in v2:
time: 673 us; the launch traced here: 668 us
  Pallas kernels  488 us (73%)
  waiting for transfers between devices  102 us (15%)
  local copies, waits for them, and re-layouts  45.2 us (7%)
  starting transfers between devices  23.1 us (3%)
    pallas_call x6, Pallas kernels, filter_mix(): pl.pallas_call(filter_mix_kernel, out_shape=(jax.ShapeDtypeStruct(u.shape...  250 us
    pallas_call x6, Pallas kernels, pass_i(): pl.pallas_call(pass_i_kernel, out_shape=(jax.ShapeDtypeStruct(y.shape, y....  111 us
    ppermute x6, waiting for transfers between devices, first_half(): corner = lax.ppermute(corner, ('pz', 'py'), DIAG)  96.9 us
    pallas_call x2, Pallas kernels, leave(): pl.pallas_call(leave_kernel, out_shape=jax.ShapeDtypeStruct(shape, y.dtyp...  65.1 us
    pallas_call x2, Pallas kernels, enter(): pl.pallas_call(enter_kernel, out_shape=(jax.ShapeDtypeStruct((nj, nk, SUB...  61.3 us
    dynamic_slice x6, local copies, waits for them, and re-layouts, first_half(): j_face = lax.dynamic_slice_in_dim(u1, j_at, half, axis=0)  17.2 us
  transfers between devices with their start and end apart: 24, of which 9 were waited for; matrix products, arithmetic and copies ran while one was open for 7% of the time, Pallas kernels for 25%

profile of v2, /device:TPU:0, one launch (start us, length us, event | category | flops | bytes accessed | tf_op | source)
XLA Modules:
  0.0 668.0 jit_solution(2364784904439473212)
XLA Ops:
  0.7 30.7 %enter.2 = (bf16[64,64,16,128]{3,2,1,0:T(8,128)(2,1)}, bf16[64,8,16,128]{3,2,1,0:T(8,128)(2,1)}) custom-call(s32[3]{0:T(128)} %pad_add_fusion.flags, bf16[2,32,64,64,64]{4,3,2,1,0:T(8,128)(2,1)} %x_ref.1), custom_call_target="tpu_custom_call" | custom-call | flops 100000000 | bytes 50331648 | tf_op jit(solution)/shard_map/enter/pallas_call | solution.py:289
  31.3 0.8 collective-permute-start
  34.2 0.9 fusion.183
  36.9 1.3 copy-done.1
  38.2 18.4 %pass_i.6 = (bf16[64,64,16,128]{3,2,1,0:T(8,128)(2,1)}, bf16[64,7,16,128]{3,2,1,0:T(8,128)(2,1)}) custom-call(s32[3]{0:T(128)} %pad_add_fusion.flags, bf16[128,256]{1,0:T(8,128)(2,1)} %get-tuple-element.135.w_ref, bf16[64,64,16,128]{3,2,1,0:T(8,128)(2,1)} %get-tuple-element.46.y_ref, bf16[64,8,16,128]{3,2,1,0:T(8,128)(2,1)} %copy-done.1), custom_call_target="tpu_custom_call" | custom-call | flops 4294967296 | bytes 41943040 | tf_op jit(solution)/shard_map/pass_i/pallas_call | solution.py:103
  56.6 30.6 %enter.3 = (bf16[64,64,16,128]{3,2,1,0:T(8,128)(2,1)}, bf16[64,8,16,128]{3,2,1,0:T(8,128)(2,1)}) custom-call(s32[3]{0:T(128)} %pad_add_fusion.flags, bf16[2,32,64,64,64]{4,3,2,1,0:T(8,128)(2,1)} %x_ref.1), custom_call_target="tpu_custom_call" | custom-call | flops 100000000 | bytes 50331648 | tf_op jit(solution)/shard_map/enter/pallas_call | solution.py:289
  88.0 3.0 collective-permute-start.3
  91.0 3.1 constant_dynamic-slice_fusion.11
  94.0 1.5 collective-permute-start.2
  95.6 1.0 slice_reduce_fusion.44
  97.2 1.0 squeeze.76.m_ref
  98.2 1.0 slice_reduce_fusion.29
  99.2 2.1 select_convert_fusion
  101.3 3.5 select_convert_fusion.1
  104.8 1.5 slice_bitcast_fusion
  106.3 1.0 copy-done
  107.4 1.5 slice_bitcast_fusion.1
  108.9 0.9 constant_dynamic-slice_fusion.10
  109.9 18.5 %pass_i.7 = (bf16[64,64,16,128]{3,2,1,0:T(8,128)(2,1)}, bf16[64,7,16,128]{3,2,1,0:T(8,128)(2,1)}) custom-call(s32[3]{0:T(128)} %pad_add_fusion.flags, bf16[128,256]{1,0:T(8,128)(2,1)} %get-tuple-element.135.w_ref, bf16[64,64,16,128]{3,2,1,0:T(8,128)(2,1)} %get-tuple-element.50.y_ref, bf16[64,8,16,128]{3,2,1,0:T(8,128)(2,1)} %collective-permute-done.1.n_ref), custom_call_target="tpu_custom_call" | custom-call | flops 4294967296 | bytes 41943040 | tf_op jit(solution)/shard_map/pass_i/pallas_call | solution.py:103
  128.4 11.6 %collective-permute-done.4.ch_ref = bf16[7,7,16,128]{3,2,1,0:T(8,128)(2,1)S(1)} collective-permute-done((bf16[7,7,16,128]{3,2,1,0:T(8,128)(2,1)S(1)}, bf16[7,7,16,128]{3,2,1,0:T(8,128)(2,1)S(1)}, u32[]{:S(2)}, u32[]{:S(2)}) %collective-permute-start.4) | collective-permute-done | bytes 200736 | tf_op jit(solution)/shard_map/ppermute | solution.py:383
  140.6 41.7 %filter_mix.6 = (bf16[64,64,16,128]{3,2,1,0:T(8,128)(2,1)}, bf16[64,8,16,128]{3,2,1,0:T(8,128)(2,1)}) custom-call(s32[3]{0:T(128)} %pad_add_fusion.flags, bf16[3,256,512]{2,1,0:T(8,128)(2,1)} %get-tuple-element.129.wj_ref, bf16[3,256,512]{2,1,0:T(8,128)(2,1)} %get-tuple-element.126.wk_ref, bf16[256,256]{1,0:T(8,128)(2,1)} %squeeze.76.m_ref, ...), custom_call_target="tpu_custom_call" | custom-call | flops 21474836480 | bytes 58720256 | tf_op jit(solution)/shard_map/filter_mix/pallas_call | solution.py:218
  182.3 3.1 constant_dynamic-slice_fusion.9
  185.5 1.8 collective-permute-start.6
  187.2 1.5 collective-permute-start.7
  188.7 1.0 constant_dynamic-slice_fusion.8
  190.0 1.4 copy-done.5
  191.3 18.5 %pass_i.8 = (bf16[64,64,16,128]{3,2,1,0:T(8,128)(2,1)}, bf16[64,7,16,128]{3,2,1,0:T(8,128)(2,1)}) custom-call(s32[3]{0:T(128)} %pad_add_fusion.flags, bf16[128,256]{1,0:T(8,128)(2,1)} %get-tuple-element.136.w_ref, bf16[64,64,16,128]{3,2,1,0:T(8,128)(2,1)} %get-tuple-element.56.y_ref, bf16[64,8,16,128]{3,2,1,0:T(8,128)(2,1)} %copy-done.5), custom_call_target="tpu_custom_call" | custom-call | flops 4294967296 | bytes 41943040 | tf_op jit(solution)/shard_map/pass_i/pallas_call | solution.py:103
  209.8 23.9 %collective-permute-done.8.ch_ref = bf16[7,7,16,128]{3,2,1,0:T(8,128)(2,1)S(1)} collective-permute-done((bf16[7,7,16,128]{3,2,1,0:T(8,128)(2,1)S(1)}, bf16[7,7,16,128]{3,2,1,0:T(8,128)(2,1)S(1)}, u32[]{:S(2)}, u32[]{:S(2)}) %collective-permute-start.8) | collective-permute-done | bytes 200736 | tf_op jit(solution)/shard_map/ppermute | solution.py:383
  234.3 41.7 %filter_mix.7 = (bf16[64,64,16,128]{3,2,1,0:T(8,128)(2,1)}, bf16[64,8,16,128]{3,2,1,0:T(8,128)(2,1)}) custom-call(s32[3]{0:T(128)} %pad_add_fusion.flags, bf16[3,256,512]{2,1,0:T(8,128)(2,1)} %get-tuple-element.129.wj_ref, bf16[3,256,512]{2,1,0:T(8,128)(2,1)} %get-tuple-element.126.wk_ref, bf16[256,256]{1,0:T(8,128)(2,1)} %squeeze.76.m_ref, ...), custom_call_target="tpu_custom_call" | custom-call | flops 21474836480 | bytes 58720256 | tf_op jit(solution)/shard_map/filter_mix/pallas_call | solution.py:218
  276.0 3.1 constant_dynamic-slice_fusion.7
  279.1 1.5 collective-permute-start.10
  281.9 1.0 squeeze.72.m_ref
  282.9 0.9 constant_dynamic-slice_fusion.6
  283.8 1.4 collective-permute-start.12
  285.3 1.3 copy-done.3
  286.6 18.5 %pass_i.9 = (bf16[64,64,16,128]{3,2,1,0:T(8,128)(2,1)}, bf16[64,7,16,128]{3,2,1,0:T(8,128)(2,1)}) custom-call(s32[3]{0:T(128)} %pad_add_fusion.flags, bf16[128,256]{1,0:T(8,128)(2,1)} %get-tuple-element.136.w_ref, bf16[64,64,16,128]{3,2,1,0:T(8,128)(2,1)} %get-tuple-element.60.y_ref, bf16[64,8,16,128]{3,2,1,0:T(8,128)(2,1)} %copy-done.3), custom_call_target="tpu_custom_call" | custom-call | flops 4294967296 | bytes 41943040 | tf_op jit(solution)/shard_map/pass_i/pallas_call | solution.py:103
  305.1 21.7 %collective-permute-done.12.ch_ref = bf16[7,7,16,128]{3,2,1,0:T(8,128)(2,1)S(1)} collective-permute-done((bf16[7,7,16,128]{3,2,1,0:T(8,128)(2,1)S(1)}, bf16[7,7,16,128]{3,2,1,0:T(8,128)(2,1)S(1)}, u32[]{:S(2)}, u32[]{:S(2)}) %collective-permute-start.12) | collective-permute-done | bytes 200736 | tf_op jit(solution)/shard_map/ppermute | solution.py:383
  327.5 41.7 %filter_mix.8 = (bf16[64,64,16,128]{3,2,1,0:T(8,128)(2,1)}, bf16[64,8,16,128]{3,2,1,0:T(8,128)(2,1)}) custom-call(s32[3]{0:T(128)} %pad_add_fusion.flags, bf16[3,256,512]{2,1,0:T(8,128)(2,1)} %get-tuple-element.130.wj_ref, bf16[3,256,512]{2,1,0:T(8,128)(2,1)} %get-tuple-element.127.wk_ref, bf16[256,256]{1,0:T(8,128)(2,1)} %squeeze.72.m_ref, ...), custom_call_target="tpu_custom_call" | custom-call | flops 21474836480 | bytes 58720256 | tf_op jit(solution)/shard_map/filter_mix/pallas_call | solution.py:218
  369.2 3.1 constant_dynamic-slice_fusion.5
  372.3 0.9 collective-permute-start.14
  373.1 1.3 collective-permute-start.15
  374.5 1.0 constant_dynamic-slice_fusion.4
  375.4 1.3 collective-permute-start.16
  376.7 1.3 copy-done.4
  378.1 18.5 %pass_i.10 = (bf16[64,64,16,128]{3,2,1,0:T(8,128)(2,1)}, bf16[64,7,16,128]{3,2,1,0:T(8,128)(2,1)}) custom-call(s32[3]{0:T(128)} %pad_add_fusion.flags, bf16[128,256]{1,0:T(8,128)(2,1)} %get-tuple-element.137.w_ref, bf16[64,64,16,128]{3,2,1,0:T(8,128)(2,1)} %get-tuple-element.66.y_ref, bf16[64,8,16,128]{3,2,1,0:T(8,128)(2,1)} %copy-done.4), custom_call_target="tpu_custom_call" | custom-call | flops 4294967296 | bytes 41943040 | tf_op jit(solution)/shard_map/pass_i/pallas_call | solution.py:103
  396.5 23.0 %collective-permute-done.16.ch_ref = bf16[7,7,16,128]{3,2,1,0:T(8,128)(2,1)S(1)} collective-permute-done((bf16[7,7,16,128]{3,2,1,0:T(8,128)(2,1)S(1)}, bf16[7,7,16,128]{3,2,1,0:T(8,128)(2,1)S(1)}, u32[]{:S(2)}, u32[]{:S(2)}) %collective-permute-start.16) | collective-permute-done | bytes 200736 | tf_op jit(solution)/shard_map/ppermute | solution.py:383
  420.2 41.8 %filter_mix.9 = (bf16[64,64,16,128]{3,2,1,0:T(8,128)(2,1)}, bf16[64,8,16,128]{3,2,1,0:T(8,128)(2,1)}) custom-call(s32[3]{0:T(128)} %pad_add_fusion.flags, bf16[3,256,512]{2,1,0:T(8,128)(2,1)} %get-tuple-element.130.wj_ref, bf16[3,256,512]{2,1,0:T(8,128)(2,1)} %get-tuple-element.127.wk_ref, bf16[256,256]{1,0:T(8,128)(2,1)} %squeeze.72.m_ref, ...), custom_call_target="tpu_custom_call" | custom-call | flops 21474836480 | bytes 58720256 | tf_op jit(solution)/shard_map/filter_mix/pallas_call | solution.py:218
  462.0 3.1 constant_dynamic-slice_fusion.3
  465.1 1.3 collective-permute-start.18
  467.7 1.0 squeeze.67.m_ref
  468.8 0.9 constant_dynamic-slice_fusion.2
  469.7 1.5 collective-permute-start.20
  471.2 1.3 copy-done.2
  472.5 18.5 %pass_i.11 = (bf16[64,64,16,128]{3,2,1,0:T(8,128)(2,1)}, bf16[64,7,16,128]{3,2,1,0:T(8,128)(2,1)}) custom-call(s32[3]{0:T(128)} %pad_add_fusion.flags, bf16[128,256]{1,0:T(8,128)(2,1)} %get-tuple-element.137.w_ref, bf16[64,64,16,128]{3,2,1,0:T(8,128)(2,1)} %get-tuple-element.70.y_ref, bf16[64,8,16,128]{3,2,1,0:T(8,128)(2,1)} %copy-done.2), custom_call_target="tpu_custom_call" | custom-call | flops 4294967296 | bytes 41943040 | tf_op jit(solution)/shard_map/pass_i/pallas_call | solution.py:103
  491.0 0.9 constant_dynamic-slice_fusion
  492.0 1.3 collective-permute-start.22
  493.3 1.5 collective-permute-start.23
  494.8 1.8 constant_dynamic-slice_fusion.1
  496.6 16.8 %collective-permute-done.20.ch_ref = bf16[7,7,16,128]{3,2,1,0:T(8,128)(2,1)} collective-permute-done((bf16[7,7,16,128]{3,2,1,0:T(8,128)(2,1)S(1)}, bf16[7,7,16,128]{3,2,1,0:T(8,128)(2,1)}, u32[]{:S(2)}, u32[]{:S(2)}) %collective-permute-start.20) | collective-permute-done | bytes 200736 | tf_op jit(solution)/shard_map/ppermute | solution.py:383
  514.2 4.1 collective-permute-done.19.kh_ref
  518.2 41.7 %filter_mix.10 = (bf16[64,64,16,128]{3,2,1,0:T(8,128)(2,1)}, bf16[64,8,16,128]{3,2,1,0:T(8,128)(2,1)}) custom-call(s32[3]{0:T(128)} %pad_add_fusion.flags, bf16[3,256,512]{2,1,0:T(8,128)(2,1)} %get-tuple-element.131.wj_ref, bf16[3,256,512]{2,1,0:T(8,128)(2,1)} %get-tuple-element.128.wk_ref, bf16[256,256]{1,0:T(8,128)(2,1)} %squeeze.67.m_ref, ...), custom_call_target="tpu_custom_call" | custom-call | flops 21474836480 | bytes 58720256 | tf_op jit(solution)/shard_map/filter_mix/pallas_call | solution.py:218
  559.9 32.6 %leave.2.rest_0_ = bf16[2,32,64,64,64]{4,3,2,1,0:T(8,128)(2,1)} custom-call(bf16[64,64,16,128]{3,2,1,0:T(8,128)(2,1)} %get-tuple-element.76.y_ref), custom_call_target="tpu_custom_call" | custom-call | flops 100000000 | bytes 50331648 | tf_op jit(solution)/shard_map/leave/pallas_call | solution.py:337
  593.7 41.7 %filter_mix.11 = (bf16[64,64,16,128]{3,2,1,0:T(8,128)(2,1)}, bf16[64,8,16,128]{3,2,1,0:T(8,128)(2,1)}) custom-call(s32[3]{0:T(128)} %pad_add_fusion.flags, bf16[3,256,512]{2,1,0:T(8,128)(2,1)} %get-tuple-element.131.wj_ref, bf16[3,256,512]{2,1,0:T(8,128)(2,1)} %get-tuple-element.128.wk_ref, bf16[256,256]{1,0:T(8,128)(2,1)} %squeeze.67.m_ref, ...), custom_call_target="tpu_custom_call" | custom-call | flops 21474836480 | bytes 58720256 | tf_op jit(solution)/shard_map/filter_mix/pallas_call | solution.py:218
  635.5 32.6 %leave.3 = bf16[2,32,64,64,64]{4,3,2,1,0:T(8,128)(2,1)} custom-call(bf16[64,64,16,128]{3,2,1,0:T(8,128)(2,1)} %get-tuple-element.78.y_ref, bf16[2,32,64,64,64]{4,3,2,1,0:T(8,128)(2,1)} %leave.2.rest_0_), custom_call_target="tpu_custom_call", output_to_operand_aliasing={{}: (1, {})} | custom-call | flops 100000000 | bytes 50331648 | tf_op jit(solution)/shard_map/leave/pallas_call | solution.py:337
  (95 shorter events, 13.4 us)
Async XLA Ops:
  0.7 32.8 %copy-start.8 = (f32[3,3,15]{2,1,0:T(4,128)S(1)}, f32[3,3,15]{2,1,0:T(4,128)}, u32[]{:S(2)}) copy-start(f32[3,3,15]{2,1,0:T(4,128)} %param.5) | copy-start | bytes 1624
  0.7 33.2 %copy-start.9 = (f32[3,32]{1,0:T(4,128)S(1)}, f32[3,32]{1,0:T(4,128)}, u32[]{:S(2)}) copy-start(f32[3,32]{1,0:T(4,128)} %param.7) | copy-start | bytes 1156
  0.7 33.2 %copy-start.6 = (bf16[3,32,32]{2,1,0:T(8,128)(2,1)S(1)}, bf16[3,32,32]{2,1,0:T(8,128)(2,1)}, u32[]{:S(2)}) copy-start(bf16[3,32,32]{2,1,0:T(8,128)(2,1)} %param.6) | copy-start | bytes 18436
  31.3 5.6 collective-permute-start
  36.9 1.3 copy-start.1
  87.3 22.6 %collective-permute-start.1 = (bf16[64,8,16,128]{3,2,1,0:T(8,128)(2,1)}, bf16[64,8,16,128]{3,2,1,0:T(8,128)(2,1)}, u32[]{:S(2)}, u32[]{:S(2)}) collective-permute-start(bf16[64,8,16,128]{3,2,1,0:T(8,128)(2,1)} %get-tuple-element.51), channel_id=1, source_target_pairs={{0,1},{1,0},{2,3},{3,2},{4,5},{5,4},{6,7},{7,6}} | collective-permute-start | bytes 6291464 | tf_op jit(solution)/shard_map/ppermute | solution.py:397
  88.0 52.0 %collective-permute-start.3 = (bf16[64,7,16,128]{3,2,1,0:T(8,128)(2,1)}, bf16[64,7,16,128]{3,2,1,0:T(8,128)(2,1)}, u32[]{:S(2)}, u32[]{:S(2)}) collective-permute-start(bf16[64,7,16,128]{3,2,1,0:T(8,128)(2,1)} %get-tuple-element.48), channel_id=1, source_target_pairs={{0,4},{4,0},{1,5},{5,1},{2,6},{6,2},{3,7},{7,3}} | collective-permute-start | bytes 5505032 | tf_op jit(solution)/shard_map/ppermute | solution.py:382
  94.0 45.9 %collective-permute-start.2 = (bf16[7,64,16,128]{3,2,1,0:T(8,128)(2,1)}, bf16[7,64,16,128]{3,2,1,0:T(8,128)(2,1)}, u32[]{:S(2)}, u32[]{:S(2)}) collective-permute-start(bf16[7,64,16,128]{3,2,1,0:T(8,128)(2,1)} %constant_dynamic-slice_fusion.11), channel_id=1, source_target_pairs={{0,2},{2,0},{1,3},{3,1},{4,6},{6,4},{5,7},{7,5}} | collective-permute-start | bytes 5505032 | tf_op jit(solution)/shard_map/ppermute | solution.py:381
  99.2 2.1 copy-start.7
  104.8 2.5 copy-start
  109.8 30.1 %collective-permute-start.4 = (bf16[7,7,16,128]{3,2,1,0:T(8,128)(2,1)S(1)}, bf16[7,7,16,128]{3,2,1,0:T(8,128)(2,1)S(1)}, u32[]{:S(2)}, u32[]{:S(2)}) collective-permute-start(bf16[7,7,16,128]{3,2,1,0:T(8,128)(2,1)S(1)} %constant_dynamic-slice_fusion.10), channel_id=1, source_target_pairs={{0,6},{2,4},{4,2},{6,0},{1,7},{3,5},{5,3},{7,1}} | collective-permute-start | bytes 602120 | tf_op jit(solution)/shard_map/ppermute | solution.py:383
  139.9 0.7 copy-start.16
  182.3 7.6 %collective-permute-start.5 = (bf16[64,8,16,128]{3,2,1,0:T(8,128)(2,1)}, bf16[64,8,16,128]{3,2,1,0:T(8,128)(2,1)S(1)}, u32[]{:S(2)}, u32[]{:S(2)}) collective-permute-start(bf16[64,8,16,128]{3,2,1,0:T(8,128)(2,1)} %get-tuple-element.57), channel_id=1, source_target_pairs={{0,1},{1,0},{2,3},{3,2},{4,5},{5,4},{6,7},{7,6}} | collective-permute-start | bytes 6291464 | tf_op jit(solution)/shard_map/ppermute | solution.py:391
  185.5 48.2 %collective-permute-start.6 = (bf16[7,64,16,128]{3,2,1,0:T(8,128)(2,1)}, bf16[7,64,16,128]{3,2,1,0:T(8,128)(2,1)}, u32[]{:S(2)}, u32[]{:S(2)}) collective-permute-start(bf16[7,64,16,128]{3,2,1,0:T(8,128)(2,1)} %constant_dynamic-slice_fusion.9), channel_id=1, source_target_pairs={{0,2},{2,0},{1,3},{3,1},{4,6},{6,4},{5,7},{7,5}} | collective-permute-start | bytes 5505032 | tf_op jit(solution)/shard_map/ppermute | solution.py:381
  187.2 46.7 %collective-permute-start.7 = (bf16[64,7,16,128]{3,2,1,0:T(8,128)(2,1)}, bf16[64,7,16,128]{3,2,1,0:T(8,128)(2,1)}, u32[]{:S(2)}, u32[]{:S(2)}) collective-permute-start(bf16[64,7,16,128]{3,2,1,0:T(8,128)(2,1)} %get-tuple-element.54), channel_id=1, source_target_pairs={{0,4},{4,0},{1,5},{5,1},{2,6},{6,2},{3,7},{7,3}} | collective-permute-start | bytes 5505032 | tf_op jit(solution)/shard_map/ppermute | solution.py:382
  189.7 43.9 %collective-permute-start.8 = (bf16[7,7,16,128]{3,2,1,0:T(8,128)(2,1)S(1)}, bf16[7,7,16,128]{3,2,1,0:T(8,128)(2,1)S(1)}, u32[]{:S(2)}, u32[]{:S(2)}) collective-permute-start(bf16[7,7,16,128]{3,2,1,0:T(8,128)(2,1)S(1)} %constant_dynamic-slice_fusion.8), channel_id=1, source_target_pairs={{0,6},{2,4},{4,2},{6,0},{1,7},{3,5},{5,3},{7,1}} | collective-permute-start | bytes 602120 | tf_op jit(solution)/shard_map/ppermute | solution.py:383
  190.0 1.4 copy-start.5
  233.6 0.7 copy-start.15
  276.0 5.2 copy-start.11
  276.0 9.2 %collective-permute-start.9 = (bf16[64,8,16,128]{3,2,1,0:T(8,128)(2,1)}, bf16[64,8,16,128]{3,2,1,0:T(8,128)(2,1)S(1)}, u32[]{:S(2)}, u32[]{:S(2)}) collective-permute-start(bf16[64,8,16,128]{3,2,1,0:T(8,128)(2,1)} %get-tuple-element.61), channel_id=1, source_target_pairs={{0,1},{1,0},{2,3},{3,2},{4,5},{5,4},{6,7},{7,6}} | collective-permute-start | bytes 6291464 | tf_op jit(solution)/shard_map/ppermute | solution.py:391
  279.1 47.7 %collective-permute-start.10 = (bf16[7,64,16,128]{3,2,1,0:T(8,128)(2,1)}, bf16[7,64,16,128]{3,2,1,0:T(8,128)(2,1)}, u32[]{:S(2)}, u32[]{:S(2)}) collective-permute-start(bf16[7,64,16,128]{3,2,1,0:T(8,128)(2,1)} %constant_dynamic-slice_fusion.7), channel_id=1, source_target_pairs={{0,2},{2,0},{1,3},{3,1},{4,6},{6,4},{5,7},{7,5}} | collective-permute-start | bytes 5505032 | tf_op jit(solution)/shard_map/ppermute | solution.py:381
  280.6 46.7 %collective-permute-start.11 = (bf16[64,7,16,128]{3,2,1,0:T(8,128)(2,1)}, bf16[64,7,16,128]{3,2,1,0:T(8,128)(2,1)}, u32[]{:S(2)}, u32[]{:S(2)}) collective-permute-start(bf16[64,7,16,128]{3,2,1,0:T(8,128)(2,1)} %get-tuple-element.58), channel_id=1, source_target_pairs={{0,4},{4,0},{1,5},{5,1},{2,6},{6,2},{3,7},{7,3}} | collective-permute-start | bytes 5505032 | tf_op jit(solution)/shard_map/ppermute | solution.py:382
  283.8 43.0 %collective-permute-start.12 = (bf16[7,7,16,128]{3,2,1,0:T(8,128)(2,1)S(1)}, bf16[7,7,16,128]{3,2,1,0:T(8,128)(2,1)S(1)}, u32[]{:S(2)}, u32[]{:S(2)}) collective-permute-start(bf16[7,7,16,128]{3,2,1,0:T(8,128)(2,1)S(1)} %constant_dynamic-slice_fusion.6), channel_id=1, source_target_pairs={{0,6},{2,4},{4,2},{6,0},{1,7},{3,5},{5,3},{7,1}} | collective-permute-start | bytes 602120 | tf_op jit(solution)/shard_map/ppermute | solution.py:383
  285.3 1.4 copy-start.3
  326.8 0.7 copy-start.17
  369.2 7.6 %collective-permute-start.13 = (bf16[64,8,16,128]{3,2,1,0:T(8,128)(2,1)}, bf16[64,8,16,128]{3,2,1,0:T(8,128)(2,1)S(1)}, u32[]{:S(2)}, u32[]{:S(2)}) collective-permute-start(bf16[64,8,16,128]{3,2,1,0:T(8,128)(2,1)} %get-tuple-element.67), channel_id=1, source_target_pairs={{0,1},{1,0},{2,3},{3,2},{4,5},{5,4},{6,7},{7,6}} | collective-permute-start | bytes 6291464 | tf_op jit(solution)/shard_map/ppermute | solution.py:391
  372.3 47.3 %collective-permute-start.14 = (bf16[7,64,16,128]{3,2,1,0:T(8,128)(2,1)}, bf16[7,64,16,128]{3,2,1,0:T(8,128)(2,1)}, u32[]{:S(2)}, u32[]{:S(2)}) collective-permute-start(bf16[7,64,16,128]{3,2,1,0:T(8,128)(2,1)} %constant_dynamic-slice_fusion.5), channel_id=1, source_target_pairs={{0,2},{2,0},{1,3},{3,1},{4,6},{6,4},{5,7},{7,5}} | collective-permute-start | bytes 5505032 | tf_op jit(solution)/shard_map/ppermute | solution.py:381
  373.1 46.7 %collective-permute-start.15 = (bf16[64,7,16,128]{3,2,1,0:T(8,128)(2,1)}, bf16[64,7,16,128]{3,2,1,0:T(8,128)(2,1)}, u32[]{:S(2)}, u32[]{:S(2)}) collective-permute-start(bf16[64,7,16,128]{3,2,1,0:T(8,128)(2,1)} %get-tuple-element.64), channel_id=1, source_target_pairs={{0,4},{4,0},{1,5},{5,1},{2,6},{6,2},{3,7},{7,3}} | collective-permute-start | bytes 5505032 | tf_op jit(solution)/shard_map/ppermute | solution.py:382
  375.4 44.1 %collective-permute-start.16 = (bf16[7,7,16,128]{3,2,1,0:T(8,128)(2,1)S(1)}, bf16[7,7,16,128]{3,2,1,0:T(8,128)(2,1)S(1)}, u32[]{:S(2)}, u32[]{:S(2)}) collective-permute-start(bf16[7,7,16,128]{3,2,1,0:T(8,128)(2,1)S(1)} %constant_dynamic-slice_fusion.4), channel_id=1, source_target_pairs={{0,6},{2,4},{4,2},{6,0},{1,7},{3,5},{5,3},{7,1}} | collective-permute-start | bytes 602120 | tf_op jit(solution)/shard_map/ppermute | solution.py:383
  376.7 1.3 copy-start.4
  419.5 0.7 copy-start.14
  462.0 5.2 copy-start.10
  462.0 9.2 %collective-permute-start.17 = (bf16[64,8,16,128]{3,2,1,0:T(8,128)(2,1)}, bf16[64,8,16,128]{3,2,1,0:T(8,128)(2,1)S(1)}, u32[]{:S(2)}, u32[]{:S(2)}) collective-permute-start(bf16[64,8,16,128]{3,2,1,0:T(8,128)(2,1)} %get-tuple-element.71), channel_id=1, source_target_pairs={{0,1},{1,0},{2,3},{3,2},{4,5},{5,4},{6,7},{7,6}} | collective-permute-start | bytes 6291464 | tf_op jit(solution)/shard_map/ppermute | solution.py:391
  465.1 49.1 %collective-permute-start.18 = (bf16[7,64,16,128]{3,2,1,0:T(8,128)(2,1)}, bf16[7,64,16,128]{3,2,1,0:T(8,128)(2,1)}, u32[]{:S(2)}, u32[]{:S(2)}) collective-permute-start(bf16[7,64,16,128]{3,2,1,0:T(8,128)(2,1)} %constant_dynamic-slice_fusion.3), channel_id=1, source_target_pairs={{0,2},{2,0},{1,3},{3,1},{4,6},{6,4},{5,7},{7,5}} | collective-permute-start | bytes 5505032 | tf_op jit(solution)/shard_map/ppermute | solution.py:381
  466.4 51.8 %collective-permute-start.19 = (bf16[64,7,16,128]{3,2,1,0:T(8,128)(2,1)}, bf16[64,7,16,128]{3,2,1,0:T(8,128)(2,1)}, u32[]{:S(2)}, u32[]{:S(2)}) collective-permute-start(bf16[64,7,16,128]{3,2,1,0:T(8,128)(2,1)} %get-tuple-element.68), channel_id=1, source_target_pairs={{0,4},{4,0},{1,5},{5,1},{2,6},{6,2},{3,7},{7,3}} | collective-permute-start | bytes 5505032 | tf_op jit(solution)/shard_map/ppermute | solution.py:382
  469.7 43.7 %collective-permute-start.20 = (bf16[7,7,16,128]{3,2,1,0:T(8,128)(2,1)S(1)}, bf16[7,7,16,128]{3,2,1,0:T(8,128)(2,1)}, u32[]{:S(2)}, u32[]{:S(2)}) collective-permute-start(bf16[7,7,16,128]{3,2,1,0:T(8,128)(2,1)S(1)} %constant_dynamic-slice_fusion.2), channel_id=1, source_target_pairs={{0,6},{2,4},{4,2},{6,0},{1,7},{3,5},{5,3},{7,1}} | collective-permute-start | bytes 602120 | tf_op jit(solution)/shard_map/ppermute | solution.py:383
  471.2 1.3 copy-start.2
  492.0 100.5 %collective-permute-start.22 = (bf16[64,7,16,128]{3,2,1,0:T(8,128)(2,1)}, bf16[64,7,16,128]{3,2,1,0:T(8,128)(2,1)}, u32[]{:S(2)}, u32[]{:S(2)}) collective-permute-start(bf16[64,7,16,128]{3,2,1,0:T(8,128)(2,1)} %get-tuple-element.74), channel_id=1, source_target_pairs={{0,4},{4,0},{1,5},{5,1},{2,6},{6,2},{3,7},{7,3}} | collective-permute-start | bytes 5505032 | tf_op jit(solution)/shard_map/ppermute | solution.py:382
  493.3 99.1 %collective-permute-start.23 = (bf16[7,7,16,128]{3,2,1,0:T(8,128)(2,1)S(1)}, bf16[7,7,16,128]{3,2,1,0:T(8,128)(2,1)S(1)}, u32[]{:S(2)}, u32[]{:S(2)}) collective-permute-start(bf16[7,7,16,128]{3,2,1,0:T(8,128)(2,1)S(1)} %constant_dynamic-slice_fusion), channel_id=1, source_target_pairs={{0,6},{2,4},{4,2},{6,0},{1,7},{3,5},{5,3},{7,1}} | collective-permute-start | bytes 602120 | tf_op jit(solution)/shard_map/ppermute | solution.py:383
  513.4 79.0 %collective-permute-start.21 = (bf16[7,64,16,128]{3,2,1,0:T(8,128)(2,1)S(1)}, bf16[7,64,16,128]{3,2,1,0:T(8,128)(2,1)S(1)}, u32[]{:S(2)}, u32[]{:S(2)}) collective-permute-start(bf16[7,64,16,128]{3,2,1,0:T(8,128)(2,1)S(1)} %constant_dynamic-slice_fusion.1), channel_id=1, source_target_pairs={{0,2},{2,0},{1,3},{3,1},{4,6},{6,4},{5,7},{7,5}} | collective-permute-start | bytes 5505032 | tf_op jit(solution)/shard_map/ppermute | solution.py:381
  592.4 0.7 copy-start.13
  592.4 1.3 copy-start.12

commit v3 on v2

--- a/solution.py
+++ b/solution.py
@@ -11,7 +11,7 @@
 SUB = 16
 GROUPS = 4
 LANES = 128
-PARAMS = pltpu.CompilerParams(vmem_limit_bytes=60 * 1024 * 1024)
+PARAMS = pltpu.CompilerParams(vmem_limit_bytes=67043328)
 
 
 def band(taps, offset):
@@ -62,7 +62,7 @@
     return out
 
 
-def pass_i_kernel(flags, w_ref, y_ref, n_ref, o_ref, f_ref):
+def pass_i_kernel(flags, w_ref, y_ref, n_ref, o_ref, f_ref, j_ref, c_ref):
     jb, kk = y_ref.shape[0], y_ref.shape[1]
     lane = lax.broadcasted_iota(jnp.int32, (1, SUB, LANES), 2)
     has_up, has_low = flags[0] > 0, flags[1] > 0
@@ -97,22 +97,36 @@
 
     lax.fori_loop(0, jb // group, step, 0)
 
-
-def pass_i(flags, weights, y, peer, half, block=8):
+    half = j_ref.shape[0]
+    at = pl.program_id(0) * jb
+
+    @pl.when((flags[3] >= at) & (flags[3] < at + jb))
+    def _():
+        def plane(r, carry):
+            j_ref[r] = o_ref[flags[3] - at + r]
+            c_ref[r] = f_ref[flags[3] - at + r]
+            return carry
+
+        lax.fori_loop(0, half, plane, 0)
+
+
+def pass_i(flags, weights, layer, y, peer, half, block=8):
     nj, nk = y.shape[0], y.shape[1]
     return pl.pallas_call(
         pass_i_kernel,
-        out_shape=(jax.ShapeDtypeStruct(y.shape, y.dtype), jax.ShapeDtypeStruct((nj, half, SUB, LANES), y.dtype)),
+        out_shape=tuple(jax.ShapeDtypeStruct(lead + (SUB, LANES), y.dtype) for lead in ((nj, nk), (nj, half), (half, nk), (half, half))),
         grid=(nj // block,),
         in_specs=[
             pl.BlockSpec(memory_space=pltpu.SMEM),
-            pl.BlockSpec(weights.shape, lambda b: (0, 0)),
+            pl.BlockSpec((None,) + weights.shape[1:], lambda b: (layer, 0, 0)),
             pl.BlockSpec((block, nk, SUB, LANES), lambda b: (b, 0, 0, 0)),
             pl.BlockSpec((block, nk // 8, SUB, LANES), lambda b: (b, 0, 0, 0)),
         ],
         out_specs=(
             pl.BlockSpec((block, nk, SUB, LANES), lambda b: (b, 0, 0, 0)),
             pl.BlockSpec((block, half, SUB, LANES), lambda b: (b, 0, 0, 0)),
+            pl.BlockSpec((half, nk, SUB, LANES), lambda b: (0, 0, 0, 0)),
+            pl.BlockSpec((half, half, SUB, LANES), lambda b: (0, 0, 0, 0)),
         ),
         compiler_params=PARAMS,
         cost_estimate=pl.CostEstimate(flops=nj * nk * 2 * SUB * 32 * 8 * LANES, bytes_accessed=nj * nk * 10240, transcendentals=0),
@@ -197,20 +211,24 @@
 
     @pl.when(now >= first)
     def _():
-        base = (now - first) * jb
-        for part in range(nk // SUB):
-            ahead_b[part] = along_k(base + 2, part)
-            finish(0, part, ahead_a)
-        following = jnp.minimum(base + 4, nj - 2)
-        for part in range(nk // SUB):
-            ahead_a[part] = along_k(following, part)
-            finish(2, part, ahead_b)
-
-
-def filter_mix(flags, w_j, w_k, mix, bias, u, j_halo, k_halo, corner, y, kb=16):
+        def four(q, carry):
+            base = (now - first) * jb + 4 * q
+            for part in range(nk // SUB):
+                ahead_b[part] = along_k(base + 2, part)
+                finish(4 * q, part, ahead_a)
+            following = jnp.minimum(base + 4, nj - 2)
+            for part in range(nk // SUB):
+                ahead_a[part] = along_k(following, part)
+                finish(4 * q + 2, part, ahead_b)
+            return carry
+
+        lax.fori_loop(0, jb // 4, four, 0)
+
+
+def filter_mix(flags, w_j, w_k, mix, bias, layer, u, j_halo, k_halo, corner, y, kb=16):
     nj, nk = u.shape[0], u.shape[1]
     half = j_halo.shape[0]
-    jb = 4
+    jb = 8
     first = nk // kb
     wide = lambda b: (0, 0, 0, 0)
     columns = lambda b: (0, jnp.minimum(b, first - 1), 0, 0)
@@ -221,10 +239,10 @@
         grid=(first + nj // jb,),
         in_specs=[
             pl.BlockSpec(memory_space=pltpu.SMEM),
-            pl.BlockSpec(w_j.shape, lambda b: (0, 0, 0)),
-            pl.BlockSpec(w_k.shape, lambda b: (0, 0, 0)),
-            pl.BlockSpec(mix.shape, lambda b: (0, 0)),
-            pl.BlockSpec(bias.shape, lambda b: (0, 0)),
+            pl.BlockSpec((None,) + w_j.shape[1:], lambda b: (layer, 0, 0, 0)),
+            pl.BlockSpec((None,) + w_k.shape[1:], lambda b: (layer, 0, 0, 0)),
+            pl.BlockSpec((None,) + mix.shape[1:], lambda b: (layer, 0, 0)),
+            pl.BlockSpec((None,) + bias.shape[1:], lambda b: (layer, 0, 0)),
             pl.BlockSpec((nj, kb, SUB, LANES), columns),
             pl.BlockSpec((half, kb, SUB, LANES), columns),
             pl.BlockSpec((nj, half, SUB, LANES), wide),
@@ -365,7 +383,7 @@
         bias = jnp.tile(0.5 * mix_bias, (1, 2 * GROUPS)).reshape(layers, 1, 2 * LANES)
         j_at = jnp.where(py == 0, nj - half, 0)
         k_at = jnp.where(pz == 0, nk - half, 0)
-        flags_x = jnp.stack([px == 0, px == 1, k_at]).astype(jnp.int32)
+        flags_x = jnp.stack([px == 0, px == 1, k_at, j_at]).astype(jnp.int32)
 
         last = [mix]
 
@@ -374,10 +392,8 @@
             return value
 
         def first_half(layer, y, peer):
-            u1, k_face = pass_i(flags_x, w_i[layer], after(y), peer, half)
+            u1, k_face, j_face, corner = pass_i(flags_x, w_i, layer, after(y), peer, half)
             last[0] = k_face
-            j_face = lax.dynamic_slice_in_dim(u1, j_at, half, axis=0)
-            corner = lax.dynamic_slice_in_dim(k_face, j_at, half, axis=0)
             j_halo = lax.ppermute(j_face, 'py', SWAP)
             k_halo = lax.ppermute(k_face, 'pz', SWAP)
             corner = lax.ppermute(corner, ('pz', 'py'), DIAG)
@@ -386,7 +402,7 @@
 
         def second_half(layer, y, u1, halos):
             u1 = after(u1)
-            y, face = filter_mix(flags_x, w_j[layer], w_k[layer], mix[layer], bias[layer], u1, *halos, y)
+            y, face = filter_mix(flags_x, w_j, w_k, mix, bias, layer, u1, *halos, y)
             last[0] = face
             return y, lax.ppermute(face, 'px', SWAP) if layer + 1 < layers else None
 

time: 673 us -> 644 us (0.957)
  local copies, waits for them, and re-layouts: 45.2 us -> 6.86 us
  waiting for transfers between devices: 102 us -> 118 us
    dynamic_slice x12 -> x0, local copies, waits for them, and re-layouts: 23 us -> none  [the longest x6 17.2 us: first_half(): j_face = lax.dynamic_slice_in_dim(u1, j_at, half, axis=0)]
    ppermute x6, waiting for transfers between devices: 96.9 us -> 110 us  [first_half(): corner = lax.ppermute(corner, ('pz', 'py'), DIAG)]
    pallas_call x6, Pallas kernels: 250 us -> 240 us  [filter_mix(): pl.pallas_call(filter_mix_kernel, out_shape=(jax.ShapeDtypeStruct(u.shape...]
    unnamed x38 -> x2, local copies, waits for them, and re-layouts: 10.5 us -> 1.25 us
    squeeze x6 -> x0, local copies, waits for them, and re-layouts: 6.74 us -> none  [the longest x3 3.06 us: second_half(): mix[layer]]
  transfers between devices with their start and end apart: 24 -> 24, of which waited for: 9 -> 13; matrix products, arithmetic and copies ran while one was open for 7% -> 2% of each run, Pallas kernels for 25% -> 26%
where the time goes in v3:
time: 644 us; the launch traced here: 642 us
  Pallas kernels  483 us (75%)
  waiting for transfers between devices  118 us (18%)
  starting transfers between devices  22.8 us (4%)
  local copies, waits for them, and re-layouts  6.86 us (1%)
    pallas_call x6, Pallas kernels, filter_mix(): pl.pallas_call(filter_mix_kernel, out_shape=(jax.ShapeDtypeStruct(u.shape...  240 us
    pallas_call x6, Pallas kernels, pass_i(): pl.pallas_call(pass_i_kernel, out_shape=tuple((jax.ShapeDtypeStruct(lead...  117 us
    ppermute x6, waiting for transfers between devices, first_half(): corner = lax.ppermute(corner, ('pz', 'py'), DIAG)  110 us
    pallas_call x2, Pallas kernels, leave(): pl.pallas_call(leave_kernel, out_shape=jax.ShapeDtypeStruct(shape, y.dtyp...  65.1 us
    pallas_call x2, Pallas kernels, enter(): pl.pallas_call(enter_kernel, out_shape=(jax.ShapeDtypeStruct((nj, nk, SUB...  61.3 us
  transfers between devices with their start and end apart: 24, of which 13 were waited for; matrix products, arithmetic and copies ran while one was open for 2% of the time, Pallas kernels for 26%

profile of v3, /device:TPU:0, one launch (start us, length us, event | category | flops | bytes accessed | tf_op | source)
XLA Modules:
  0.0 642.2 jit_solution(919673379360737016)
XLA Ops:
  0.0 0.7 broadcast_multiply_fusion.1
  0.9 0.4 mul.33
  1.2 0.3 mul.37
  1.6 1.1 mul.38
  2.7 0.8 broadcast_multiply_fusion.m_ref
  3.5 0.7 pad_add_fusion.flags
  4.1 30.6 %enter.2 = (bf16[64,64,16,128]{3,2,1,0:T(8,128)(2,1)}, bf16[64,8,16,128]{3,2,1,0:T(8,128)(2,1)}) custom-call(s32[4]{0:T(128)} %pad_add_fusion.flags, bf16[2,32,64,64,64]{4,3,2,1,0:T(8,128)(2,1)} %x_ref.1), custom_call_target="tpu_custom_call" | custom-call | flops 100000000 | bytes 50331648 | tf_op jit(solution)/shard_map/enter/pallas_call | solution.py:307
  34.7 0.8 collective-permute-start
  35.6 0.7 convert_convert_fusion
  36.3 0.6 fusion.204
  36.9 0.6 copy_bitcast_fusion
  37.5 0.4 slice_reduce_fusion.14
  38.1 0.3 broadcast_compare_fusion.15
  38.4 1.3 add_convert_fusion.w_ref
  39.7 19.4 %pass_i.6 = (bf16[64,64,16,128]{3,2,1,0:T(8,128)(2,1)}, bf16[64,7,16,128]{3,2,1,0:T(8,128)(2,1)}, bf16[7,64,16,128]{3,2,1,0:T(8,128)(2,1)}, bf16[7,7,16,128]{3,2,1,0:T(8,128)(2,1)}) custom-call(s32[4]{0:T(128)} %pad_add_fusion.flags, bf16[3,128,256]{2,1,0:T(8,128)(2,1)} %add_convert_fusion.w_ref, bf16[64,64,16,128]{3,2,1,0:T(8,128)(2,1)} %get-tuple-element.60.y_ref, ...), custom_call_target="tpu_custom_call" | custom-call | flops 4294967296 | bytes 41943040 | tf_op jit(solution)/shard_map/pass_i/pallas_call | solution.py:115
  59.1 30.7 %enter.3 = (bf16[64,64,16,128]{3,2,1,0:T(8,128)(2,1)}, bf16[64,8,16,128]{3,2,1,0:T(8,128)(2,1)}) custom-call(s32[4]{0:T(128)} %pad_add_fusion.flags, bf16[2,32,64,64,64]{4,3,2,1,0:T(8,128)(2,1)} %x_ref.1), custom_call_target="tpu_custom_call" | custom-call | flops 100000000 | bytes 50331648 | tf_op jit(solution)/shard_map/enter/pallas_call | solution.py:307
  89.8 0.4 collective-permute-start.1
  90.2 0.7 broadcast_multiply_fusion.2
  90.9 2.6 collective-permute-start.3
  93.5 1.5 collective-permute-start.2
  95.0 0.7 copy.14
  95.6 0.7 tile.9.b_ref
  96.3 0.4 slice_reduce_fusion.44
  96.7 1.7 slice_reduce_fusion.29
  98.8 2.7 select_convert_fusion.wk_ref
  101.5 2.7 select_convert_fusion.1.wj_ref
  104.1 19.5 %pass_i.7 = (bf16[64,64,16,128]{3,2,1,0:T(8,128)(2,1)}, bf16[64,7,16,128]{3,2,1,0:T(8,128)(2,1)}, bf16[7,64,16,128]{3,2,1,0:T(8,128)(2,1)}, bf16[7,7,16,128]{3,2,1,0:T(8,128)(2,1)}) custom-call(s32[4]{0:T(128)} %pad_add_fusion.flags, bf16[3,128,256]{2,1,0:T(8,128)(2,1)} %add_convert_fusion.w_ref, bf16[64,64,16,128]{3,2,1,0:T(8,128)(2,1)} %get-tuple-element.64.y_ref, ...), custom_call_target="tpu_custom_call" | custom-call | flops 4294967296 | bytes 41943040 | tf_op jit(solution)/shard_map/pass_i/pallas_call | solution.py:115
  123.6 16.2 %collective-permute-done.4.ch_ref = bf16[7,7,16,128]{3,2,1,0:T(8,128)(2,1)} collective-permute-done((bf16[7,7,16,128]{3,2,1,0:T(8,128)(2,1)}, bf16[7,7,16,128]{3,2,1,0:T(8,128)(2,1)}, u32[]{:S(2)}, u32[]{:S(2)}) %collective-permute-start.4) | collective-permute-done | bytes 200736 | tf_op jit(solution)/shard_map/ppermute | solution.py:399
  139.8 40.0 %filter_mix.6 = (bf16[64,64,16,128]{3,2,1,0:T(8,128)(2,1)}, bf16[64,8,16,128]{3,2,1,0:T(8,128)(2,1)}) custom-call(s32[4]{0:T(128)} %pad_add_fusion.flags, bf16[3,3,256,512]{3,2,1,0:T(8,128)(2,1)} %select_convert_fusion.1.wj_ref, bf16[3,3,256,512]{3,2,1,0:T(8,128)(2,1)} %select_convert_fusion.wk_ref, bf16[3,256,256]{2,1,0:T(8,128)(2,1)} %broadcast_multiply_fusion.m_ref, ...), custom_call_target="tpu_custom_call" | custom-call | flops 21474836480 | bytes 58720256 | tf_op jit(solution)/shard_map/filter_mix/pallas_call | solution.py:236
  179.8 1.7 collective-permute-start.6
  181.6 1.5 collective-permute-start.7
  183.1 0.3 collective-permute-start.8
  183.4 1.0 collective-permute-done.5.n_ref
  184.3 19.5 %pass_i.8 = (bf16[64,64,16,128]{3,2,1,0:T(8,128)(2,1)}, bf16[64,7,16,128]{3,2,1,0:T(8,128)(2,1)}, bf16[7,64,16,128]{3,2,1,0:T(8,128)(2,1)}, bf16[7,7,16,128]{3,2,1,0:T(8,128)(2,1)}) custom-call(s32[4]{0:T(128)} %pad_add_fusion.flags, bf16[3,128,256]{2,1,0:T(8,128)(2,1)} %add_convert_fusion.w_ref, bf16[64,64,16,128]{3,2,1,0:T(8,128)(2,1)} %get-tuple-element.72.y_ref, ...), custom_call_target="tpu_custom_call" | custom-call | flops 4294967296 | bytes 41943040 | tf_op jit(solution)/shard_map/pass_i/pallas_call | solution.py:115
  203.8 24.3 %collective-permute-done.8.ch_ref = bf16[7,7,16,128]{3,2,1,0:T(8,128)(2,1)} collective-permute-done((bf16[7,7,16,128]{3,2,1,0:T(8,128)(2,1)}, bf16[7,7,16,128]{3,2,1,0:T(8,128)(2,1)}, u32[]{:S(2)}, u32[]{:S(2)}) %collective-permute-start.8) | collective-permute-done | bytes 200736 | tf_op jit(solution)/shard_map/ppermute | solution.py:399
  228.3 40.1 %filter_mix.7 = (bf16[64,64,16,128]{3,2,1,0:T(8,128)(2,1)}, bf16[64,8,16,128]{3,2,1,0:T(8,128)(2,1)}) custom-call(s32[4]{0:T(128)} %pad_add_fusion.flags, bf16[3,3,256,512]{3,2,1,0:T(8,128)(2,1)} %select_convert_fusion.1.wj_ref, bf16[3,3,256,512]{3,2,1,0:T(8,128)(2,1)} %select_convert_fusion.wk_ref, bf16[3,256,256]{2,1,0:T(8,128)(2,1)} %broadcast_multiply_fusion.m_ref, ...), custom_call_target="tpu_custom_call" | custom-call | flops 21474836480 | bytes 58720256 | tf_op jit(solution)/shard_map/filter_mix/pallas_call | solution.py:236
  268.4 1.3 collective-permute-start.10
  269.7 0.8 collective-permute-start.11
  270.5 1.5 collective-permute-start.12
  271.9 1.0 collective-permute-done.9.n_ref
  272.9 19.5 %pass_i.9 = (bf16[64,64,16,128]{3,2,1,0:T(8,128)(2,1)}, bf16[64,7,16,128]{3,2,1,0:T(8,128)(2,1)}, bf16[7,64,16,128]{3,2,1,0:T(8,128)(2,1)}, bf16[7,7,16,128]{3,2,1,0:T(8,128)(2,1)}) custom-call(s32[4]{0:T(128)} %pad_add_fusion.flags, bf16[3,128,256]{2,1,0:T(8,128)(2,1)} %add_convert_fusion.w_ref, bf16[64,64,16,128]{3,2,1,0:T(8,128)(2,1)} %get-tuple-element.78.y_ref, ...), custom_call_target="tpu_custom_call" | custom-call | flops 4294967296 | bytes 41943040 | tf_op jit(solution)/shard_map/pass_i/pallas_call | solution.py:115
  292.4 24.0 %collective-permute-done.12.ch_ref = bf16[7,7,16,128]{3,2,1,0:T(8,128)(2,1)} collective-permute-done((bf16[7,7,16,128]{3,2,1,0:T(8,128)(2,1)}, bf16[7,7,16,128]{3,2,1,0:T(8,128)(2,1)}, u32[]{:S(2)}, u32[]{:S(2)}) %collective-permute-start.12) | collective-permute-done | bytes 200736 | tf_op jit(solution)/shard_map/ppermute | solution.py:399
  316.5 40.0 %filter_mix.8 = (bf16[64,64,16,128]{3,2,1,0:T(8,128)(2,1)}, bf16[64,8,16,128]{3,2,1,0:T(8,128)(2,1)}) custom-call(s32[4]{0:T(128)} %pad_add_fusion.flags, bf16[3,3,256,512]{3,2,1,0:T(8,128)(2,1)} %select_convert_fusion.1.wj_ref, bf16[3,3,256,512]{3,2,1,0:T(8,128)(2,1)} %select_convert_fusion.wk_ref, bf16[3,256,256]{2,1,0:T(8,128)(2,1)} %broadcast_multiply_fusion.m_ref, ...), custom_call_target="tpu_custom_call" | custom-call | flops 21474836480 | bytes 58720256 | tf_op jit(solution)/shard_map/filter_mix/pallas_call | solution.py:236
  356.5 0.8 collective-permute-start.14
  357.3 1.4 collective-permute-start.15
  358.7 1.3 collective-permute-start.16
  360.0 1.0 collective-permute-done.13.n_ref
  361.0 19.4 %pass_i.10 = (bf16[64,64,16,128]{3,2,1,0:T(8,128)(2,1)}, bf16[64,7,16,128]{3,2,1,0:T(8,128)(2,1)}, bf16[7,64,16,128]{3,2,1,0:T(8,128)(2,1)}, bf16[7,7,16,128]{3,2,1,0:T(8,128)(2,1)}) custom-call(s32[4]{0:T(128)} %pad_add_fusion.flags, bf16[3,128,256]{2,1,0:T(8,128)(2,1)} %add_convert_fusion.w_ref, bf16[64,64,16,128]{3,2,1,0:T(8,128)(2,1)} %get-tuple-element.86.y_ref, ...), custom_call_target="tpu_custom_call" | custom-call | flops 4294967296 | bytes 41943040 | tf_op jit(solution)/shard_map/pass_i/pallas_call | solution.py:115
  380.4 23.4 %collective-permute-done.16.ch_ref = bf16[7,7,16,128]{3,2,1,0:T(8,128)(2,1)} collective-permute-done((bf16[7,7,16,128]{3,2,1,0:T(8,128)(2,1)}, bf16[7,7,16,128]{3,2,1,0:T(8,128)(2,1)}, u32[]{:S(2)}, u32[]{:S(2)}) %collective-permute-start.16) | collective-permute-done | bytes 200736 | tf_op jit(solution)/shard_map/ppermute | solution.py:399
  404.0 40.0 %filter_mix.9 = (bf16[64,64,16,128]{3,2,1,0:T(8,128)(2,1)}, bf16[64,8,16,128]{3,2,1,0:T(8,128)(2,1)}) custom-call(s32[4]{0:T(128)} %pad_add_fusion.flags, bf16[3,3,256,512]{3,2,1,0:T(8,128)(2,1)} %select_convert_fusion.1.wj_ref, bf16[3,3,256,512]{3,2,1,0:T(8,128)(2,1)} %select_convert_fusion.wk_ref, bf16[3,256,256]{2,1,0:T(8,128)(2,1)} %broadcast_multiply_fusion.m_ref, ...), custom_call_target="tpu_custom_call" | custom-call | flops 21474836480 | bytes 58720256 | tf_op jit(solution)/shard_map/filter_mix/pallas_call | solution.py:236
  444.0 1.3 collective-permute-start.18
  445.3 0.8 collective-permute-start.19
  446.1 1.5 collective-permute-start.20
  447.5 1.0 collective-permute-done.17.n_ref
  448.5 19.5 %pass_i.11 = (bf16[64,64,16,128]{3,2,1,0:T(8,128)(2,1)}, bf16[64,7,16,128]{3,2,1,0:T(8,128)(2,1)}, bf16[7,64,16,128]{3,2,1,0:T(8,128)(2,1)}, bf16[7,7,16,128]{3,2,1,0:T(8,128)(2,1)}) custom-call(s32[4]{0:T(128)} %pad_add_fusion.flags, bf16[3,128,256]{2,1,0:T(8,128)(2,1)} %add_convert_fusion.w_ref, bf16[64,64,16,128]{3,2,1,0:T(8,128)(2,1)} %get-tuple-element.92.y_ref, ...), custom_call_target="tpu_custom_call" | custom-call | flops 4294967296 | bytes 41943040 | tf_op jit(solution)/shard_map/pass_i/pallas_call | solution.py:115
  468.0 1.4 collective-permute-start.22
  469.4 1.3 collective-permute-start.23
  470.7 21.7 %collective-permute-done.20.ch_ref = bf16[7,7,16,128]{3,2,1,0:T(8,128)(2,1)} collective-permute-done((bf16[7,7,16,128]{3,2,1,0:T(8,128)(2,1)}, bf16[7,7,16,128]{3,2,1,0:T(8,128)(2,1)}, u32[]{:S(2)}, u32[]{:S(2)}) %collective-permute-start.20) | collective-permute-done | bytes 200736 | tf_op jit(solution)/shard_map/ppermute | solution.py:399
  492.4 0.7 collective-permute-start.21
  493.1 4.0 collective-permute-done.19.kh_ref
  497.1 40.0 %filter_mix.10 = (bf16[64,64,16,128]{3,2,1,0:T(8,128)(2,1)}, bf16[64,8,16,128]{3,2,1,0:T(8,128)(2,1)}) custom-call(s32[4]{0:T(128)} %pad_add_fusion.flags, bf16[3,3,256,512]{3,2,1,0:T(8,128)(2,1)} %select_convert_fusion.1.wj_ref, bf16[3,3,256,512]{3,2,1,0:T(8,128)(2,1)} %select_convert_fusion.wk_ref, bf16[3,256,256]{2,1,0:T(8,128)(2,1)} %broadcast_multiply_fusion.m_ref, ...), custom_call_target="tpu_custom_call" | custom-call | flops 21474836480 | bytes 58720256 | tf_op jit(solution)/shard_map/filter_mix/pallas_call | solution.py:236
  537.1 32.6 %leave.2.rest_0_ = bf16[2,32,64,64,64]{4,3,2,1,0:T(8,128)(2,1)} custom-call(bf16[64,64,16,128]{3,2,1,0:T(8,128)(2,1)} %get-tuple-element.100.y_ref), custom_call_target="tpu_custom_call" | custom-call | flops 100000000 | bytes 50331648 | tf_op jit(solution)/shard_map/leave/pallas_call | solution.py:355
  569.6 40.0 %filter_mix.11 = (bf16[64,64,16,128]{3,2,1,0:T(8,128)(2,1)}, bf16[64,8,16,128]{3,2,1,0:T(8,128)(2,1)}) custom-call(s32[4]{0:T(128)} %pad_add_fusion.flags, bf16[3,3,256,512]{3,2,1,0:T(8,128)(2,1)} %select_convert_fusion.1.wj_ref, bf16[3,3,256,512]{3,2,1,0:T(8,128)(2,1)} %select_convert_fusion.wk_ref, bf16[3,256,256]{2,1,0:T(8,128)(2,1)} %broadcast_multiply_fusion.m_ref, ...), custom_call_target="tpu_custom_call" | custom-call | flops 21474836480 | bytes 58720256 | tf_op jit(solution)/shard_map/filter_mix/pallas_call | solution.py:236
  609.7 32.6 %leave.3 = bf16[2,32,64,64,64]{4,3,2,1,0:T(8,128)(2,1)} custom-call(bf16[64,64,16,128]{3,2,1,0:T(8,128)(2,1)} %get-tuple-element.104.y_ref, bf16[2,32,64,64,64]{4,3,2,1,0:T(8,128)(2,1)} %leave.2.rest_0_), custom_call_target="tpu_custom_call", output_to_operand_aliasing={{}: (1, {})} | custom-call | flops 100000000 | bytes 50331648 | tf_op jit(solution)/shard_map/leave/pallas_call | solution.py:355
  (41 shorter events, 1.2 us)
Async XLA Ops:
  34.7 5.0 collective-permute-start
  89.8 14.4 %collective-permute-start.1 = (bf16[64,8,16,128]{3,2,1,0:T(8,128)(2,1)}, bf16[64,8,16,128]{3,2,1,0:T(8,128)(2,1)}, u32[]{:S(2)}, u32[]{:S(2)}) collective-permute-start(bf16[64,8,16,128]{3,2,1,0:T(8,128)(2,1)} %get-tuple-element.65), channel_id=1, source_target_pairs={{0,1},{1,0},{2,3},{3,2},{4,5},{5,4},{6,7},{7,6}} | collective-permute-start | bytes 6291464 | tf_op jit(solution)/shard_map/ppermute | solution.py:413
  90.9 49.0 %collective-permute-start.3 = (bf16[64,7,16,128]{3,2,1,0:T(8,128)(2,1)}, bf16[64,7,16,128]{3,2,1,0:T(8,128)(2,1)}, u32[]{:S(2)}, u32[]{:S(2)}) collective-permute-start(bf16[64,7,16,128]{3,2,1,0:T(8,128)(2,1)} %get-tuple-element.62), channel_id=1, source_target_pairs={{0,4},{4,0},{1,5},{5,1},{2,6},{6,2},{3,7},{7,3}} | collective-permute-start | bytes 5505032 | tf_op jit(solution)/shard_map/ppermute | solution.py:398
  93.5 46.3 %collective-permute-start.2 = (bf16[7,64,16,128]{3,2,1,0:T(8,128)(2,1)}, bf16[7,64,16,128]{3,2,1,0:T(8,128)(2,1)}, u32[]{:S(2)}, u32[]{:S(2)}) collective-permute-start(bf16[7,64,16,128]{3,2,1,0:T(8,128)(2,1)} %get-tuple-element.70), channel_id=1, source_target_pairs={{0,2},{2,0},{1,3},{3,1},{4,6},{6,4},{5,7},{7,5}} | collective-permute-start | bytes 5505032 | tf_op jit(solution)/shard_map/ppermute | solution.py:397
  104.1 35.7 %collective-permute-start.4 = (bf16[7,7,16,128]{3,2,1,0:T(8,128)(2,1)}, bf16[7,7,16,128]{3,2,1,0:T(8,128)(2,1)}, u32[]{:S(2)}, u32[]{:S(2)}) collective-permute-start(bf16[7,7,16,128]{3,2,1,0:T(8,128)(2,1)} %get-tuple-element.71), channel_id=1, source_target_pairs={{0,6},{2,4},{4,2},{6,0},{1,7},{3,5},{5,3},{7,1}} | collective-permute-start | bytes 602120 | tf_op jit(solution)/shard_map/ppermute | solution.py:399
  179.8 4.5 collective-permute-start.5
  179.8 48.3 %collective-permute-start.6 = (bf16[7,64,16,128]{3,2,1,0:T(8,128)(2,1)}, bf16[7,64,16,128]{3,2,1,0:T(8,128)(2,1)}, u32[]{:S(2)}, u32[]{:S(2)}) collective-permute-start(bf16[7,64,16,128]{3,2,1,0:T(8,128)(2,1)} %get-tuple-element.76), channel_id=1, source_target_pairs={{0,2},{2,0},{1,3},{3,1},{4,6},{6,4},{5,7},{7,5}} | collective-permute-start | bytes 5505032 | tf_op jit(solution)/shard_map/ppermute | solution.py:397
  181.6 46.7 %collective-permute-start.7 = (bf16[64,7,16,128]{3,2,1,0:T(8,128)(2,1)}, bf16[64,7,16,128]{3,2,1,0:T(8,128)(2,1)}, u32[]{:S(2)}, u32[]{:S(2)}) collective-permute-start(bf16[64,7,16,128]{3,2,1,0:T(8,128)(2,1)} %get-tuple-element.68), channel_id=1, source_target_pairs={{0,4},{4,0},{1,5},{5,1},{2,6},{6,2},{3,7},{7,3}} | collective-permute-start | bytes 5505032 | tf_op jit(solution)/shard_map/ppermute | solution.py:398
  183.1 45.1 %collective-permute-start.8 = (bf16[7,7,16,128]{3,2,1,0:T(8,128)(2,1)}, bf16[7,7,16,128]{3,2,1,0:T(8,128)(2,1)}, u32[]{:S(2)}, u32[]{:S(2)}) collective-permute-start(bf16[7,7,16,128]{3,2,1,0:T(8,128)(2,1)} %get-tuple-element.77), channel_id=1, source_target_pairs={{0,6},{2,4},{4,2},{6,0},{1,7},{3,5},{5,3},{7,1}} | collective-permute-start | bytes 602120 | tf_op jit(solution)/shard_map/ppermute | solution.py:399
  268.4 4.5 collective-permute-start.9
  268.4 47.9 %collective-permute-start.10 = (bf16[7,64,16,128]{3,2,1,0:T(8,128)(2,1)}, bf16[7,64,16,128]{3,2,1,0:T(8,128)(2,1)}, u32[]{:S(2)}, u32[]{:S(2)}) collective-permute-start(bf16[7,64,16,128]{3,2,1,0:T(8,128)(2,1)} %get-tuple-element.84), channel_id=1, source_target_pairs={{0,2},{2,0},{1,3},{3,1},{4,6},{6,4},{5,7},{7,5}} | collective-permute-start | bytes 5505032 | tf_op jit(solution)/shard_map/ppermute | solution.py:397
  269.7 46.7 %collective-permute-start.11 = (bf16[64,7,16,128]{3,2,1,0:T(8,128)(2,1)}, bf16[64,7,16,128]{3,2,1,0:T(8,128)(2,1)}, u32[]{:S(2)}, u32[]{:S(2)}) collective-permute-start(bf16[64,7,16,128]{3,2,1,0:T(8,128)(2,1)} %get-tuple-element.74), channel_id=1, source_target_pairs={{0,4},{4,0},{1,5},{5,1},{2,6},{6,2},{3,7},{7,3}} | collective-permute-start | bytes 5505032 | tf_op jit(solution)/shard_map/ppermute | solution.py:398
  270.5 45.9 %collective-permute-start.12 = (bf16[7,7,16,128]{3,2,1,0:T(8,128)(2,1)}, bf16[7,7,16,128]{3,2,1,0:T(8,128)(2,1)}, u32[]{:S(2)}, u32[]{:S(2)}) collective-permute-start(bf16[7,7,16,128]{3,2,1,0:T(8,128)(2,1)} %get-tuple-element.85), channel_id=1, source_target_pairs={{0,6},{2,4},{4,2},{6,0},{1,7},{3,5},{5,3},{7,1}} | collective-permute-start | bytes 602120 | tf_op jit(solution)/shard_map/ppermute | solution.py:399
  356.5 4.5 collective-permute-start.13
  356.5 47.4 %collective-permute-start.14 = (bf16[7,64,16,128]{3,2,1,0:T(8,128)(2,1)}, bf16[7,64,16,128]{3,2,1,0:T(8,128)(2,1)}, u32[]{:S(2)}, u32[]{:S(2)}) collective-permute-start(bf16[7,64,16,128]{3,2,1,0:T(8,128)(2,1)} %get-tuple-element.90), channel_id=1, source_target_pairs={{0,2},{2,0},{1,3},{3,1},{4,6},{6,4},{5,7},{7,5}} | collective-permute-start | bytes 5505032 | tf_op jit(solution)/shard_map/ppermute | solution.py:397
  357.3 46.7 %collective-permute-start.15 = (bf16[64,7,16,128]{3,2,1,0:T(8,128)(2,1)}, bf16[64,7,16,128]{3,2,1,0:T(8,128)(2,1)}, u32[]{:S(2)}, u32[]{:S(2)}) collective-permute-start(bf16[64,7,16,128]{3,2,1,0:T(8,128)(2,1)} %get-tuple-element.82), channel_id=1, source_target_pairs={{0,4},{4,0},{1,5},{5,1},{2,6},{6,2},{3,7},{7,3}} | collective-permute-start | bytes 5505032 | tf_op jit(solution)/shard_map/ppermute | solution.py:398
  358.7 45.2 %collective-permute-start.16 = (bf16[7,7,16,128]{3,2,1,0:T(8,128)(2,1)}, bf16[7,7,16,128]{3,2,1,0:T(8,128)(2,1)}, u32[]{:S(2)}, u32[]{:S(2)}) collective-permute-start(bf16[7,7,16,128]{3,2,1,0:T(8,128)(2,1)} %get-tuple-element.91), channel_id=1, source_target_pairs={{0,6},{2,4},{4,2},{6,0},{1,7},{3,5},{5,3},{7,1}} | collective-permute-start | bytes 602120 | tf_op jit(solution)/shard_map/ppermute | solution.py:399
  444.0 4.5 collective-permute-start.17
  444.0 49.1 %collective-permute-start.18 = (bf16[7,64,16,128]{3,2,1,0:T(8,128)(2,1)}, bf16[7,64,16,128]{3,2,1,0:T(8,128)(2,1)}, u32[]{:S(2)}, u32[]{:S(2)}) collective-permute-start(bf16[7,64,16,128]{3,2,1,0:T(8,128)(2,1)} %get-tuple-element.98), channel_id=1, source_target_pairs={{0,2},{2,0},{1,3},{3,1},{4,6},{6,4},{5,7},{7,5}} | collective-permute-start | bytes 5505032 | tf_op jit(solution)/shard_map/ppermute | solution.py:397
  445.3 51.8 %collective-permute-start.19 = (bf16[64,7,16,128]{3,2,1,0:T(8,128)(2,1)}, bf16[64,7,16,128]{3,2,1,0:T(8,128)(2,1)}, u32[]{:S(2)}, u32[]{:S(2)}) collective-permute-start(bf16[64,7,16,128]{3,2,1,0:T(8,128)(2,1)} %get-tuple-element.88), channel_id=1, source_target_pairs={{0,4},{4,0},{1,5},{5,1},{2,6},{6,2},{3,7},{7,3}} | collective-permute-start | bytes 5505032 | tf_op jit(solution)/shard_map/ppermute | solution.py:398
  446.1 46.4 %collective-permute-start.20 = (bf16[7,7,16,128]{3,2,1,0:T(8,128)(2,1)}, bf16[7,7,16,128]{3,2,1,0:T(8,128)(2,1)}, u32[]{:S(2)}, u32[]{:S(2)}) collective-permute-start(bf16[7,7,16,128]{3,2,1,0:T(8,128)(2,1)} %get-tuple-element.99), channel_id=1, source_target_pairs={{0,6},{2,4},{4,2},{6,0},{1,7},{3,5},{5,3},{7,1}} | collective-permute-start | bytes 602120 | tf_op jit(solution)/shard_map/ppermute | solution.py:399
  468.0 101.7 %collective-permute-start.22 = (bf16[64,7,16,128]{3,2,1,0:T(8,128)(2,1)}, bf16[64,7,16,128]{3,2,1,0:T(8,128)(2,1)}, u32[]{:S(2)}, u32[]{:S(2)}) collective-permute-start(bf16[64,7,16,128]{3,2,1,0:T(8,128)(2,1)} %get-tuple-element.96), channel_id=1, source_target_pairs={{0,4},{4,0},{1,5},{5,1},{2,6},{6,2},{3,7},{7,3}} | collective-permute-start | bytes 5505032 | tf_op jit(solution)/shard_map/ppermute | solution.py:398
  469.4 100.2 %collective-permute-start.23 = (bf16[7,7,16,128]{3,2,1,0:T(8,128)(2,1)}, bf16[7,7,16,128]{3,2,1,0:T(8,128)(2,1)}, u32[]{:S(2)}, u32[]{:S(2)}) collective-permute-start(bf16[7,7,16,128]{3,2,1,0:T(8,128)(2,1)} %get-tuple-element.103), channel_id=1, source_target_pairs={{0,6},{2,4},{4,2},{6,0},{1,7},{3,5},{5,3},{7,1}} | collective-permute-start | bytes 602120 | tf_op jit(solution)/shard_map/ppermute | solution.py:399
  492.4 77.2 %collective-permute-start.21 = (bf16[7,64,16,128]{3,2,1,0:T(8,128)(2,1)}, bf16[7,64,16,128]{3,2,1,0:T(8,128)(2,1)}, u32[]{:S(2)}, u32[]{:S(2)}) collective-permute-start(bf16[7,64,16,128]{3,2,1,0:T(8,128)(2,1)} %get-tuple-element.102), channel_id=1, source_target_pairs={{0,2},{2,0},{1,3},{3,1},{4,6},{6,4},{5,7},{7,5}} | collective-permute-start | bytes 5505032 | tf_op jit(solution)/shard_map/ppermute | solution.py:397

commit v4 on v3

--- a/solution.py
+++ b/solution.py
@@ -287,19 +287,21 @@
 
     lax.fori_loop(0, SUB // 2, pair, 0)
 
-    def emit(j, carry):
-        base = pl.multiple_of(j * (nk * PITCH), 8)
-        for k in range(0, nk, 8):
-            faces = []
-            for side in range(8):
-                tile = s2[pl.ds(base + (k + side) * PITCH, SUB), :]
-                o_ref[j, k + side] = tile.astype(jnp.bfloat16)
-                faces.append(jnp.where(send_high, tile[8:], tile[:8]))
-            pairs = [jnp.concatenate(faces[2 * q:2 * q + 2], axis=0).astype(jnp.bfloat16) for q in range(GROUPS)]
-            f_ref[j, k // 8] = gather_faces(pairs, flags[0])
+    def emit(q, carry):
+        for r in range(2):
+            j = 2 * q + r
+            base = pl.multiple_of(j * (nk * PITCH), 8)
+            for k in range(0, nk, 8):
+                faces = []
+                for side in range(8):
+                    tile = s2[pl.ds(base + (k + side) * PITCH, SUB), :]
+                    o_ref[j, k + side] = tile.astype(jnp.bfloat16)
+                    faces.append(jnp.where(send_high, tile[8:], tile[:8]))
+                pairs = [jnp.concatenate(faces[2 * t:2 * t + 2], axis=0).astype(jnp.bfloat16) for t in range(GROUPS)]
+                f_ref[j, k // 8] = gather_faces(pairs, flags[0])
         return carry
 
-    lax.fori_loop(0, SUB, emit, 0)
+    lax.fori_loop(0, SUB // 2, emit, 0)
 
 
 def enter(flags, vol, v):

time: 644 us -> 639 us (level)
  transfers between devices with their start and end apart: 24 -> 24, of which waited for: 13 -> 13; matrix products, arithmetic and copies ran while one was open for 2% -> 2% of each run, Pallas kernels for 26% -> 27%
where the time goes in v4:
time: 639 us; the launch traced here: 638 us
  Pallas kernels  479 us (75%)
  waiting for transfers between devices  118 us (18%)
  starting transfers between devices  22.8 us (4%)
  local copies, waits for them, and re-layouts  6.86 us (1%)
    pallas_call x6, Pallas kernels, filter_mix(): pl.pallas_call(filter_mix_kernel, out_shape=(jax.ShapeDtypeStruct(u.shape...  240 us
    pallas_call x6, Pallas kernels, pass_i(): pl.pallas_call(pass_i_kernel, out_shape=tuple((jax.ShapeDtypeStruct(lead...  117 us
    ppermute x6, waiting for transfers between devices, first_half(): corner = lax.ppermute(corner, ('pz', 'py'), DIAG)  110 us
    pallas_call x2, Pallas kernels, leave(): pl.pallas_call(leave_kernel, out_shape=jax.ShapeDtypeStruct(shape, y.dtyp...  65.1 us
    pallas_call x2, Pallas kernels, enter(): pl.pallas_call(enter_kernel, out_shape=(jax.ShapeDtypeStruct((nj, nk, SUB...  57 us
  transfers between devices with their start and end apart: 24, of which 13 were waited for; matrix products, arithmetic and copies ran while one was open for 2% of the time, Pallas kernels for 27%

profile of v4, /device:TPU:0, one launch (start us, length us, event | category | flops | bytes accessed | tf_op | source)
XLA Modules:
  0.0 637.9 jit_solution(9565280711197804815)
XLA Ops:
  0.0 0.7 broadcast_multiply_fusion.1
  0.9 0.4 mul.33
  1.2 0.3 mul.37
  1.6 1.1 mul.38
  2.7 0.8 broadcast_multiply_fusion.m_ref
  3.5 0.7 pad_add_fusion.flags
  4.1 28.5 %enter.2 = (bf16[64,64,16,128]{3,2,1,0:T(8,128)(2,1)}, bf16[64,8,16,128]{3,2,1,0:T(8,128)(2,1)}) custom-call(s32[4]{0:T(128)} %pad_add_fusion.flags, bf16[2,32,64,64,64]{4,3,2,1,0:T(8,128)(2,1)} %x_ref.1), custom_call_target="tpu_custom_call" | custom-call | flops 100000000 | bytes 50331648 | tf_op jit(solution)/shard_map/enter/pallas_call | solution.py:309
  32.6 0.8 collective-permute-start
  33.5 0.7 convert_convert_fusion
  34.2 0.6 fusion.204
  34.8 0.6 copy_bitcast_fusion
  35.4 0.4 slice_reduce_fusion.14
  36.0 0.3 broadcast_compare_fusion.15
  36.2 1.3 add_convert_fusion.w_ref
  37.5 19.4 %pass_i.6 = (bf16[64,64,16,128]{3,2,1,0:T(8,128)(2,1)}, bf16[64,7,16,128]{3,2,1,0:T(8,128)(2,1)}, bf16[7,64,16,128]{3,2,1,0:T(8,128)(2,1)}, bf16[7,7,16,128]{3,2,1,0:T(8,128)(2,1)}) custom-call(s32[4]{0:T(128)} %pad_add_fusion.flags, bf16[3,128,256]{2,1,0:T(8,128)(2,1)} %add_convert_fusion.w_ref, bf16[64,64,16,128]{3,2,1,0:T(8,128)(2,1)} %get-tuple-element.60.y_ref, ...), custom_call_target="tpu_custom_call" | custom-call | flops 4294967296 | bytes 41943040 | tf_op jit(solution)/shard_map/pass_i/pallas_call | solution.py:115
  57.0 28.5 %enter.3 = (bf16[64,64,16,128]{3,2,1,0:T(8,128)(2,1)}, bf16[64,8,16,128]{3,2,1,0:T(8,128)(2,1)}) custom-call(s32[4]{0:T(128)} %pad_add_fusion.flags, bf16[2,32,64,64,64]{4,3,2,1,0:T(8,128)(2,1)} %x_ref.1), custom_call_target="tpu_custom_call" | custom-call | flops 100000000 | bytes 50331648 | tf_op jit(solution)/shard_map/enter/pallas_call | solution.py:309
  85.5 0.4 collective-permute-start.1
  85.9 0.7 broadcast_multiply_fusion.2
  86.6 2.6 collective-permute-start.3
  89.2 1.5 collective-permute-start.2
  90.7 0.7 copy.14
  91.4 0.7 tile.9.b_ref
  92.1 0.4 slice_reduce_fusion.44
  92.4 1.7 slice_reduce_fusion.29
  94.5 2.7 select_convert_fusion.wk_ref
  97.2 2.7 select_convert_fusion.1.wj_ref
  99.9 19.5 %pass_i.7 = (bf16[64,64,16,128]{3,2,1,0:T(8,128)(2,1)}, bf16[64,7,16,128]{3,2,1,0:T(8,128)(2,1)}, bf16[7,64,16,128]{3,2,1,0:T(8,128)(2,1)}, bf16[7,7,16,128]{3,2,1,0:T(8,128)(2,1)}) custom-call(s32[4]{0:T(128)} %pad_add_fusion.flags, bf16[3,128,256]{2,1,0:T(8,128)(2,1)} %add_convert_fusion.w_ref, bf16[64,64,16,128]{3,2,1,0:T(8,128)(2,1)} %get-tuple-element.64.y_ref, ...), custom_call_target="tpu_custom_call" | custom-call | flops 4294967296 | bytes 41943040 | tf_op jit(solution)/shard_map/pass_i/pallas_call | solution.py:115
  119.3 16.2 %collective-permute-done.4.ch_ref = bf16[7,7,16,128]{3,2,1,0:T(8,128)(2,1)} collective-permute-done((bf16[7,7,16,128]{3,2,1,0:T(8,128)(2,1)}, bf16[7,7,16,128]{3,2,1,0:T(8,128)(2,1)}, u32[]{:S(2)}, u32[]{:S(2)}) %collective-permute-start.4) | collective-permute-done | bytes 200736 | tf_op jit(solution)/shard_map/ppermute | solution.py:401
  135.6 40.0 %filter_mix.6 = (bf16[64,64,16,128]{3,2,1,0:T(8,128)(2,1)}, bf16[64,8,16,128]{3,2,1,0:T(8,128)(2,1)}) custom-call(s32[4]{0:T(128)} %pad_add_fusion.flags, bf16[3,3,256,512]{3,2,1,0:T(8,128)(2,1)} %select_convert_fusion.1.wj_ref, bf16[3,3,256,512]{3,2,1,0:T(8,128)(2,1)} %select_convert_fusion.wk_ref, bf16[3,256,256]{2,1,0:T(8,128)(2,1)} %broadcast_multiply_fusion.m_ref, ...), custom_call_target="tpu_custom_call" | custom-call | flops 21474836480 | bytes 58720256 | tf_op jit(solution)/shard_map/filter_mix/pallas_call | solution.py:236
  175.6 1.7 collective-permute-start.6
  177.3 1.5 collective-permute-start.7
  178.8 0.3 collective-permute-start.8
  179.1 1.0 collective-permute-done.5.n_ref
  180.1 19.5 %pass_i.8 = (bf16[64,64,16,128]{3,2,1,0:T(8,128)(2,1)}, bf16[64,7,16,128]{3,2,1,0:T(8,128)(2,1)}, bf16[7,64,16,128]{3,2,1,0:T(8,128)(2,1)}, bf16[7,7,16,128]{3,2,1,0:T(8,128)(2,1)}) custom-call(s32[4]{0:T(128)} %pad_add_fusion.flags, bf16[3,128,256]{2,1,0:T(8,128)(2,1)} %add_convert_fusion.w_ref, bf16[64,64,16,128]{3,2,1,0:T(8,128)(2,1)} %get-tuple-element.72.y_ref, ...), custom_call_target="tpu_custom_call" | custom-call | flops 4294967296 | bytes 41943040 | tf_op jit(solution)/shard_map/pass_i/pallas_call | solution.py:115
  199.6 24.3 %collective-permute-done.8.ch_ref = bf16[7,7,16,128]{3,2,1,0:T(8,128)(2,1)} collective-permute-done((bf16[7,7,16,128]{3,2,1,0:T(8,128)(2,1)}, bf16[7,7,16,128]{3,2,1,0:T(8,128)(2,1)}, u32[]{:S(2)}, u32[]{:S(2)}) %collective-permute-start.8) | collective-permute-done | bytes 200736 | tf_op jit(solution)/shard_map/ppermute | solution.py:401
  224.0 40.1 %filter_mix.7 = (bf16[64,64,16,128]{3,2,1,0:T(8,128)(2,1)}, bf16[64,8,16,128]{3,2,1,0:T(8,128)(2,1)}) custom-call(s32[4]{0:T(128)} %pad_add_fusion.flags, bf16[3,3,256,512]{3,2,1,0:T(8,128)(2,1)} %select_convert_fusion.1.wj_ref, bf16[3,3,256,512]{3,2,1,0:T(8,128)(2,1)} %select_convert_fusion.wk_ref, bf16[3,256,256]{2,1,0:T(8,128)(2,1)} %broadcast_multiply_fusion.m_ref, ...), custom_call_target="tpu_custom_call" | custom-call | flops 21474836480 | bytes 58720256 | tf_op jit(solution)/shard_map/filter_mix/pallas_call | solution.py:236
  264.2 1.3 collective-permute-start.10
  265.5 0.8 collective-permute-start.11
  266.2 1.5 collective-permute-start.12
  267.7 1.0 collective-permute-done.9.n_ref
  268.7 19.5 %pass_i.9 = (bf16[64,64,16,128]{3,2,1,0:T(8,128)(2,1)}, bf16[64,7,16,128]{3,2,1,0:T(8,128)(2,1)}, bf16[7,64,16,128]{3,2,1,0:T(8,128)(2,1)}, bf16[7,7,16,128]{3,2,1,0:T(8,128)(2,1)}) custom-call(s32[4]{0:T(128)} %pad_add_fusion.flags, bf16[3,128,256]{2,1,0:T(8,128)(2,1)} %add_convert_fusion.w_ref, bf16[64,64,16,128]{3,2,1,0:T(8,128)(2,1)} %get-tuple-element.78.y_ref, ...), custom_call_target="tpu_custom_call" | custom-call | flops 4294967296 | bytes 41943040 | tf_op jit(solution)/shard_map/pass_i/pallas_call | solution.py:115
  288.1 24.0 %collective-permute-done.12.ch_ref = bf16[7,7,16,128]{3,2,1,0:T(8,128)(2,1)} collective-permute-done((bf16[7,7,16,128]{3,2,1,0:T(8,128)(2,1)}, bf16[7,7,16,128]{3,2,1,0:T(8,128)(2,1)}, u32[]{:S(2)}, u32[]{:S(2)}) %collective-permute-start.12) | collective-permute-done | bytes 200736 | tf_op jit(solution)/shard_map/ppermute | solution.py:401
  312.2 40.0 %filter_mix.8 = (bf16[64,64,16,128]{3,2,1,0:T(8,128)(2,1)}, bf16[64,8,16,128]{3,2,1,0:T(8,128)(2,1)}) custom-call(s32[4]{0:T(128)} %pad_add_fusion.flags, bf16[3,3,256,512]{3,2,1,0:T(8,128)(2,1)} %select_convert_fusion.1.wj_ref, bf16[3,3,256,512]{3,2,1,0:T(8,128)(2,1)} %select_convert_fusion.wk_ref, bf16[3,256,256]{2,1,0:T(8,128)(2,1)} %broadcast_multiply_fusion.m_ref, ...), custom_call_target="tpu_custom_call" | custom-call | flops 21474836480 | bytes 58720256 | tf_op jit(solution)/shard_map/filter_mix/pallas_call | solution.py:236
  352.2 0.8 collective-permute-start.14
  353.0 1.4 collective-permute-start.15
  354.4 1.3 collective-permute-start.16
  355.7 1.0 collective-permute-done.13.n_ref
  356.7 19.4 %pass_i.10 = (bf16[64,64,16,128]{3,2,1,0:T(8,128)(2,1)}, bf16[64,7,16,128]{3,2,1,0:T(8,128)(2,1)}, bf16[7,64,16,128]{3,2,1,0:T(8,128)(2,1)}, bf16[7,7,16,128]{3,2,1,0:T(8,128)(2,1)}) custom-call(s32[4]{0:T(128)} %pad_add_fusion.flags, bf16[3,128,256]{2,1,0:T(8,128)(2,1)} %add_convert_fusion.w_ref, bf16[64,64,16,128]{3,2,1,0:T(8,128)(2,1)} %get-tuple-element.86.y_ref, ...), custom_call_target="tpu_custom_call" | custom-call | flops 4294967296 | bytes 41943040 | tf_op jit(solution)/shard_map/pass_i/pallas_call | solution.py:115
  376.1 23.4 %collective-permute-done.16.ch_ref = bf16[7,7,16,128]{3,2,1,0:T(8,128)(2,1)} collective-permute-done((bf16[7,7,16,128]{3,2,1,0:T(8,128)(2,1)}, bf16[7,7,16,128]{3,2,1,0:T(8,128)(2,1)}, u32[]{:S(2)}, u32[]{:S(2)}) %collective-permute-start.16) | collective-permute-done | bytes 200736 | tf_op jit(solution)/shard_map/ppermute | solution.py:401
  399.8 40.0 %filter_mix.9 = (bf16[64,64,16,128]{3,2,1,0:T(8,128)(2,1)}, bf16[64,8,16,128]{3,2,1,0:T(8,128)(2,1)}) custom-call(s32[4]{0:T(128)} %pad_add_fusion.flags, bf16[3,3,256,512]{3,2,1,0:T(8,128)(2,1)} %select_convert_fusion.1.wj_ref, bf16[3,3,256,512]{3,2,1,0:T(8,128)(2,1)} %select_convert_fusion.wk_ref, bf16[3,256,256]{2,1,0:T(8,128)(2,1)} %broadcast_multiply_fusion.m_ref, ...), custom_call_target="tpu_custom_call" | custom-call | flops 21474836480 | bytes 58720256 | tf_op jit(solution)/shard_map/filter_mix/pallas_call | solution.py:236
  439.7 1.3 collective-permute-start.18
  441.0 0.8 collective-permute-start.19
  441.8 1.5 collective-permute-start.20
  443.2 1.0 collective-permute-done.17.n_ref
  444.2 19.5 %pass_i.11 = (bf16[64,64,16,128]{3,2,1,0:T(8,128)(2,1)}, bf16[64,7,16,128]{3,2,1,0:T(8,128)(2,1)}, bf16[7,64,16,128]{3,2,1,0:T(8,128)(2,1)}, bf16[7,7,16,128]{3,2,1,0:T(8,128)(2,1)}) custom-call(s32[4]{0:T(128)} %pad_add_fusion.flags, bf16[3,128,256]{2,1,0:T(8,128)(2,1)} %add_convert_fusion.w_ref, bf16[64,64,16,128]{3,2,1,0:T(8,128)(2,1)} %get-tuple-element.92.y_ref, ...), custom_call_target="tpu_custom_call" | custom-call | flops 4294967296 | bytes 41943040 | tf_op jit(solution)/shard_map/pass_i/pallas_call | solution.py:115
  463.7 1.4 collective-permute-start.22
  465.1 1.3 collective-permute-start.23
  466.4 21.7 %collective-permute-done.20.ch_ref = bf16[7,7,16,128]{3,2,1,0:T(8,128)(2,1)} collective-permute-done((bf16[7,7,16,128]{3,2,1,0:T(8,128)(2,1)}, bf16[7,7,16,128]{3,2,1,0:T(8,128)(2,1)}, u32[]{:S(2)}, u32[]{:S(2)}) %collective-permute-start.20) | collective-permute-done | bytes 200736 | tf_op jit(solution)/shard_map/ppermute | solution.py:401
  488.2 0.7 collective-permute-start.21
  488.8 4.0 collective-permute-done.19.kh_ref
  492.8 40.0 %filter_mix.10 = (bf16[64,64,16,128]{3,2,1,0:T(8,128)(2,1)}, bf16[64,8,16,128]{3,2,1,0:T(8,128)(2,1)}) custom-call(s32[4]{0:T(128)} %pad_add_fusion.flags, bf16[3,3,256,512]{3,2,1,0:T(8,128)(2,1)} %select_convert_fusion.1.wj_ref, bf16[3,3,256,512]{3,2,1,0:T(8,128)(2,1)} %select_convert_fusion.wk_ref, bf16[3,256,256]{2,1,0:T(8,128)(2,1)} %broadcast_multiply_fusion.m_ref, ...), custom_call_target="tpu_custom_call" | custom-call | flops 21474836480 | bytes 58720256 | tf_op jit(solution)/shard_map/filter_mix/pallas_call | solution.py:236
  532.8 32.6 %leave.2.rest_0_ = bf16[2,32,64,64,64]{4,3,2,1,0:T(8,128)(2,1)} custom-call(bf16[64,64,16,128]{3,2,1,0:T(8,128)(2,1)} %get-tuple-element.100.y_ref), custom_call_target="tpu_custom_call" | custom-call | flops 100000000 | bytes 50331648 | tf_op jit(solution)/shard_map/leave/pallas_call | solution.py:357
  565.3 40.0 %filter_mix.11 = (bf16[64,64,16,128]{3,2,1,0:T(8,128)(2,1)}, bf16[64,8,16,128]{3,2,1,0:T(8,128)(2,1)}) custom-call(s32[4]{0:T(128)} %pad_add_fusion.flags, bf16[3,3,256,512]{3,2,1,0:T(8,128)(2,1)} %select_convert_fusion.1.wj_ref, bf16[3,3,256,512]{3,2,1,0:T(8,128)(2,1)} %select_convert_fusion.wk_ref, bf16[3,256,256]{2,1,0:T(8,128)(2,1)} %broadcast_multiply_fusion.m_ref, ...), custom_call_target="tpu_custom_call" | custom-call | flops 21474836480 | bytes 58720256 | tf_op jit(solution)/shard_map/filter_mix/pallas_call | solution.py:236
  605.4 32.6 %leave.3 = bf16[2,32,64,64,64]{4,3,2,1,0:T(8,128)(2,1)} custom-call(bf16[64,64,16,128]{3,2,1,0:T(8,128)(2,1)} %get-tuple-element.104.y_ref, bf16[2,32,64,64,64]{4,3,2,1,0:T(8,128)(2,1)} %leave.2.rest_0_), custom_call_target="tpu_custom_call", output_to_operand_aliasing={{}: (1, {})} | custom-call | flops 100000000 | bytes 50331648 | tf_op jit(solution)/shard_map/leave/pallas_call | solution.py:357
  (41 shorter events, 1.2 us)
Async XLA Ops:
  32.6 5.0 collective-permute-start
  85.5 14.4 %collective-permute-start.1 = (bf16[64,8,16,128]{3,2,1,0:T(8,128)(2,1)}, bf16[64,8,16,128]{3,2,1,0:T(8,128)(2,1)}, u32[]{:S(2)}, u32[]{:S(2)}) collective-permute-start(bf16[64,8,16,128]{3,2,1,0:T(8,128)(2,1)} %get-tuple-element.65), channel_id=1, source_target_pairs={{0,1},{1,0},{2,3},{3,2},{4,5},{5,4},{6,7},{7,6}} | collective-permute-start | bytes 6291464 | tf_op jit(solution)/shard_map/ppermute | solution.py:415
  86.6 49.0 %collective-permute-start.3 = (bf16[64,7,16,128]{3,2,1,0:T(8,128)(2,1)}, bf16[64,7,16,128]{3,2,1,0:T(8,128)(2,1)}, u32[]{:S(2)}, u32[]{:S(2)}) collective-permute-start(bf16[64,7,16,128]{3,2,1,0:T(8,128)(2,1)} %get-tuple-element.62), channel_id=1, source_target_pairs={{0,4},{4,0},{1,5},{5,1},{2,6},{6,2},{3,7},{7,3}} | collective-permute-start | bytes 5505032 | tf_op jit(solution)/shard_map/ppermute | solution.py:400
  89.2 46.3 %collective-permute-start.2 = (bf16[7,64,16,128]{3,2,1,0:T(8,128)(2,1)}, bf16[7,64,16,128]{3,2,1,0:T(8,128)(2,1)}, u32[]{:S(2)}, u32[]{:S(2)}) collective-permute-start(bf16[7,64,16,128]{3,2,1,0:T(8,128)(2,1)} %get-tuple-element.70), channel_id=1, source_target_pairs={{0,2},{2,0},{1,3},{3,1},{4,6},{6,4},{5,7},{7,5}} | collective-permute-start | bytes 5505032 | tf_op jit(solution)/shard_map/ppermute | solution.py:399
  99.8 35.7 %collective-permute-start.4 = (bf16[7,7,16,128]{3,2,1,0:T(8,128)(2,1)}, bf16[7,7,16,128]{3,2,1,0:T(8,128)(2,1)}, u32[]{:S(2)}, u32[]{:S(2)}) collective-permute-start(bf16[7,7,16,128]{3,2,1,0:T(8,128)(2,1)} %get-tuple-element.71), channel_id=1, source_target_pairs={{0,6},{2,4},{4,2},{6,0},{1,7},{3,5},{5,3},{7,1}} | collective-permute-start | bytes 602120 | tf_op jit(solution)/shard_map/ppermute | solution.py:401
  175.6 4.5 collective-permute-start.5
  175.6 48.3 %collective-permute-start.6 = (bf16[7,64,16,128]{3,2,1,0:T(8,128)(2,1)}, bf16[7,64,16,128]{3,2,1,0:T(8,128)(2,1)}, u32[]{:S(2)}, u32[]{:S(2)}) collective-permute-start(bf16[7,64,16,128]{3,2,1,0:T(8,128)(2,1)} %get-tuple-element.76), channel_id=1, source_target_pairs={{0,2},{2,0},{1,3},{3,1},{4,6},{6,4},{5,7},{7,5}} | collective-permute-start | bytes 5505032 | tf_op jit(solution)/shard_map/ppermute | solution.py:399
  177.3 46.7 %collective-permute-start.7 = (bf16[64,7,16,128]{3,2,1,0:T(8,128)(2,1)}, bf16[64,7,16,128]{3,2,1,0:T(8,128)(2,1)}, u32[]{:S(2)}, u32[]{:S(2)}) collective-permute-start(bf16[64,7,16,128]{3,2,1,0:T(8,128)(2,1)} %get-tuple-element.68), channel_id=1, source_target_pairs={{0,4},{4,0},{1,5},{5,1},{2,6},{6,2},{3,7},{7,3}} | collective-permute-start | bytes 5505032 | tf_op jit(solution)/shard_map/ppermute | solution.py:400
  178.8 45.1 %collective-permute-start.8 = (bf16[7,7,16,128]{3,2,1,0:T(8,128)(2,1)}, bf16[7,7,16,128]{3,2,1,0:T(8,128)(2,1)}, u32[]{:S(2)}, u32[]{:S(2)}) collective-permute-start(bf16[7,7,16,128]{3,2,1,0:T(8,128)(2,1)} %get-tuple-element.77), channel_id=1, source_target_pairs={{0,6},{2,4},{4,2},{6,0},{1,7},{3,5},{5,3},{7,1}} | collective-permute-start | bytes 602120 | tf_op jit(solution)/shard_map/ppermute | solution.py:401
  264.1 4.5 collective-permute-start.9
  264.2 47.9 %collective-permute-start.10 = (bf16[7,64,16,128]{3,2,1,0:T(8,128)(2,1)}, bf16[7,64,16,128]{3,2,1,0:T(8,128)(2,1)}, u32[]{:S(2)}, u32[]{:S(2)}) collective-permute-start(bf16[7,64,16,128]{3,2,1,0:T(8,128)(2,1)} %get-tuple-element.84), channel_id=1, source_target_pairs={{0,2},{2,0},{1,3},{3,1},{4,6},{6,4},{5,7},{7,5}} | collective-permute-start | bytes 5505032 | tf_op jit(solution)/shard_map/ppermute | solution.py:399
  265.5 46.7 %collective-permute-start.11 = (bf16[64,7,16,128]{3,2,1,0:T(8,128)(2,1)}, bf16[64,7,16,128]{3,2,1,0:T(8,128)(2,1)}, u32[]{:S(2)}, u32[]{:S(2)}) collective-permute-start(bf16[64,7,16,128]{3,2,1,0:T(8,128)(2,1)} %get-tuple-element.74), channel_id=1, source_target_pairs={{0,4},{4,0},{1,5},{5,1},{2,6},{6,2},{3,7},{7,3}} | collective-permute-start | bytes 5505032 | tf_op jit(solution)/shard_map/ppermute | solution.py:400
  266.2 45.9 %collective-permute-start.12 = (bf16[7,7,16,128]{3,2,1,0:T(8,128)(2,1)}, bf16[7,7,16,128]{3,2,1,0:T(8,128)(2,1)}, u32[]{:S(2)}, u32[]{:S(2)}) collective-permute-start(bf16[7,7,16,128]{3,2,1,0:T(8,128)(2,1)} %get-tuple-element.85), channel_id=1, source_target_pairs={{0,6},{2,4},{4,2},{6,0},{1,7},{3,5},{5,3},{7,1}} | collective-permute-start | bytes 602120 | tf_op jit(solution)/shard_map/ppermute | solution.py:401
  352.2 4.5 collective-permute-start.13
  352.2 47.4 %collective-permute-start.14 = (bf16[7,64,16,128]{3,2,1,0:T(8,128)(2,1)}, bf16[7,64,16,128]{3,2,1,0:T(8,128)(2,1)}, u32[]{:S(2)}, u32[]{:S(2)}) collective-permute-start(bf16[7,64,16,128]{3,2,1,0:T(8,128)(2,1)} %get-tuple-element.90), channel_id=1, source_target_pairs={{0,2},{2,0},{1,3},{3,1},{4,6},{6,4},{5,7},{7,5}} | collective-permute-start | bytes 5505032 | tf_op jit(solution)/shard_map/ppermute | solution.py:399
  353.0 46.7 %collective-permute-start.15 = (bf16[64,7,16,128]{3,2,1,0:T(8,128)(2,1)}, bf16[64,7,16,128]{3,2,1,0:T(8,128)(2,1)}, u32[]{:S(2)}, u32[]{:S(2)}) collective-permute-start(bf16[64,7,16,128]{3,2,1,0:T(8,128)(2,1)} %get-tuple-element.82), channel_id=1, source_target_pairs={{0,4},{4,0},{1,5},{5,1},{2,6},{6,2},{3,7},{7,3}} | collective-permute-start | bytes 5505032 | tf_op jit(solution)/shard_map/ppermute | solution.py:400
  354.4 45.2 %collective-permute-start.16 = (bf16[7,7,16,128]{3,2,1,0:T(8,128)(2,1)}, bf16[7,7,16,128]{3,2,1,0:T(8,128)(2,1)}, u32[]{:S(2)}, u32[]{:S(2)}) collective-permute-start(bf16[7,7,16,128]{3,2,1,0:T(8,128)(2,1)} %get-tuple-element.91), channel_id=1, source_target_pairs={{0,6},{2,4},{4,2},{6,0},{1,7},{3,5},{5,3},{7,1}} | collective-permute-start | bytes 602120 | tf_op jit(solution)/shard_map/ppermute | solution.py:401
  439.7 4.5 collective-permute-start.17
  439.7 49.1 %collective-permute-start.18 = (bf16[7,64,16,128]{3,2,1,0:T(8,128)(2,1)}, bf16[7,64,16,128]{3,2,1,0:T(8,128)(2,1)}, u32[]{:S(2)}, u32[]{:S(2)}) collective-permute-start(bf16[7,64,16,128]{3,2,1,0:T(8,128)(2,1)} %get-tuple-element.98), channel_id=1, source_target_pairs={{0,2},{2,0},{1,3},{3,1},{4,6},{6,4},{5,7},{7,5}} | collective-permute-start | bytes 5505032 | tf_op jit(solution)/shard_map/ppermute | solution.py:399
  441.0 51.8 %collective-permute-start.19 = (bf16[64,7,16,128]{3,2,1,0:T(8,128)(2,1)}, bf16[64,7,16,128]{3,2,1,0:T(8,128)(2,1)}, u32[]{:S(2)}, u32[]{:S(2)}) collective-permute-start(bf16[64,7,16,128]{3,2,1,0:T(8,128)(2,1)} %get-tuple-element.88), channel_id=1, source_target_pairs={{0,4},{4,0},{1,5},{5,1},{2,6},{6,2},{3,7},{7,3}} | collective-permute-start | bytes 5505032 | tf_op jit(solution)/shard_map/ppermute | solution.py:400
  441.8 46.4 %collective-permute-start.20 = (bf16[7,7,16,128]{3,2,1,0:T(8,128)(2,1)}, bf16[7,7,16,128]{3,2,1,0:T(8,128)(2,1)}, u32[]{:S(2)}, u32[]{:S(2)}) collective-permute-start(bf16[7,7,16,128]{3,2,1,0:T(8,128)(2,1)} %get-tuple-element.99), channel_id=1, source_target_pairs={{0,6},{2,4},{4,2},{6,0},{1,7},{3,5},{5,3},{7,1}} | collective-permute-start | bytes 602120 | tf_op jit(solution)/shard_map/ppermute | solution.py:401
  463.7 101.7 %collective-permute-start.22 = (bf16[64,7,16,128]{3,2,1,0:T(8,128)(2,1)}, bf16[64,7,16,128]{3,2,1,0:T(8,128)(2,1)}, u32[]{:S(2)}, u32[]{:S(2)}) collective-permute-start(bf16[64,7,16,128]{3,2,1,0:T(8,128)(2,1)} %get-tuple-element.96), channel_id=1, source_target_pairs={{0,4},{4,0},{1,5},{5,1},{2,6},{6,2},{3,7},{7,3}} | collective-permute-start | bytes 5505032 | tf_op jit(solution)/shard_map/ppermute | solution.py:400
  465.1 100.2 %collective-permute-start.23 = (bf16[7,7,16,128]{3,2,1,0:T(8,128)(2,1)}, bf16[7,7,16,128]{3,2,1,0:T(8,128)(2,1)}, u32[]{:S(2)}, u32[]{:S(2)}) collective-permute-start(bf16[7,7,16,128]{3,2,1,0:T(8,128)(2,1)} %get-tuple-element.103), channel_id=1, source_target_pairs={{0,6},{2,4},{4,2},{6,0},{1,7},{3,5},{5,3},{7,1}} | collective-permute-start | bytes 602120 | tf_op jit(solution)/shard_map/ppermute | solution.py:401
  488.2 77.2 %collective-permute-start.21 = (bf16[7,64,16,128]{3,2,1,0:T(8,128)(2,1)}, bf16[7,64,16,128]{3,2,1,0:T(8,128)(2,1)}, u32[]{:S(2)}, u32[]{:S(2)}) collective-permute-start(bf16[7,64,16,128]{3,2,1,0:T(8,128)(2,1)} %get-tuple-element.102), channel_id=1, source_target_pairs={{0,2},{2,0},{1,3},{3,1},{4,6},{6,4},{5,7},{7,5}} | collective-permute-start | bytes 5505032 | tf_op jit(solution)/shard_map/ppermute | solution.py:399
